TPU v7x, 32 devices: a whole 2x2x4 slice. The times are simulated.
32 devices in a mesh: dp: 8 (over z, y), tensor: 4 (over x, core).
Axes of the slice: x: 2, y: 2, z: 4, core: 2. Of those that a mesh axis runs over, the one named last changes fastest.
Arguments:
- tokens: bfloat16 [8192, 2048], P(('dp', 'tensor')), may hold values from -6 to 6
- lengths: int32 [8], P('dp'), may hold values from 256 to 1024, as said below
- attn_gain: bfloat16 [2048], replicated, may hold values from 0.25 to 1.75
- w_query: bfloat16 [2048, 2048], P('dp', 'tensor'), may hold values from -0.125 to 0.125
- w_key: bfloat16 [2048, 512], P('dp', 'tensor'), may hold values from -0.125 to 0.125
- w_value: bfloat16 [2048, 512], P('dp', 'tensor'), may hold values from -0.125 to 0.125
- w_output: bfloat16 [2048, 2048], P('tensor', 'dp'), may hold values from -1 to 1
- mlp_gain: bfloat16 [2048], replicated, may hold values from 0.25 to 1.75
- w_gate: bfloat16 [2048, 8192], P('dp', 'tensor'), may hold values from -0.125 to 0.125
- w_up: bfloat16 [2048, 8192], P('dp', 'tensor'), may hold values from -0.125 to 0.125
- w_down: bfloat16 [8192, 2048], P('tensor', 'dp'), may hold values from -0.125 to 0.125
- cotangent: bfloat16 [8192, 2048], P(('dp', 'tensor')), may hold values from -6 to 6
Outputs:
- layer_out: bfloat16 [8192, 2048], P(('dp', 'tensor'))
- grad_tokens: float32 [8192, 2048], P(('dp', 'tensor'))
- grad_query: float32 [2048, 2048], P('dp', 'tensor')
- grad_key: float32 [2048, 512], P('dp', 'tensor')
- grad_value: float32 [2048, 512], P('dp', 'tensor')
- grad_output: float32 [2048, 2048], P('tensor', 'dp')
- grad_gate: float32 [2048, 8192], P('dp', 'tensor')
- grad_up: float32 [2048, 8192], P('dp', 'tensor')
- grad_down: float32 [8192, 2048], P('tensor', 'dp')
- grad_attn_gain: float32 [2048], P(('dp', 'tensor'))
- grad_mlp_gain: float32 [2048], P(('dp', 'tensor'))
Inputs may be any that keep to these rules, and one draw needn't show every extreme that they name: `lengths`: each of the 8 sequences has a valid length from 256 to 1024; at least one has length exactly 1024.
All inputs are finite; a program needn't handle non-finite values.
Results may differ from a plain program's by a relative error of at most 0.015.
Values may be sent and summed in bfloat16 or wider, within the bound.
A program may use at most 192 MiB of HBM per device.

v0:
```python
import jax
import jax.numpy as jnp
from jax import lax
from jax.sharding import PartitionSpec as P

HD = 64
LEN = 1024


epsilon = 1e-05
theta = 500000.0


def rope_frequencies():
    half_size = HD // 2
    base_freq = theta ** (-(jnp.arange(half_size, dtype=jnp.float32) * 2.0) / HD)
    wavelength = 2.0 * jnp.pi / base_freq
    smooth = (8192.0 / wavelength - 1.0) / 3.0
    middle = (1.0 - smooth) * base_freq / 32.0 + smooth * base_freq
    return jnp.where(
        wavelength < 2048.0, base_freq, jnp.where(wavelength > 8192.0, base_freq / 32.0, middle)
    )


def rope_tables(positions):
    frequency = rope_frequencies()
    angles = positions.astype(jnp.float32)[:, None] * frequency[None, :]
    angles = jnp.concatenate([angles, angles], axis=1)
    return (jnp.cos(angles), jnp.sin(angles))


def rotate_half(vector):
    half_size = vector.shape[-1] // 2
    return jnp.concatenate([-vector[..., half_size:], vector[..., :half_size]], axis=-1)


def rope_apply(vector, cosine_table, sine_table):
    return vector * cosine_table[:, None, :] + rotate_half(vector) * sine_table[:, None, :]


def rope_back(grads, cosine_table, sine_table):
    return grads * cosine_table[:, None, :] - rotate_half(grads * sine_table[:, None, :])


def gather_attention(w_query, w_key, w_value, w_output):
    return (
        lax.all_gather(w_query, "dp", axis=0, tiled=True),
        lax.all_gather(w_key, "dp", axis=0, tiled=True),
        lax.all_gather(w_value, "dp", axis=0, tiled=True),
        lax.all_gather(w_output, "dp", axis=1, tiled=True),
    )


def gather_mlp(w_gate, w_up, w_down):
    return (
        lax.all_gather(w_gate, "dp", axis=0, tiled=True),
        lax.all_gather(w_up, "dp", axis=0, tiled=True),
        lax.all_gather(w_down, "dp", axis=1, tiled=True),
    )


def add_rows(accum, piece):
    return accum + piece


def block_scores(queries, key_vecs, lengths, block_index, block_rows):
    per_seq = LEN // block_rows
    sequence = block_index // per_seq
    row_start = block_index * block_rows
    query_blk = lax.dynamic_slice_in_dim(queries, row_start, block_rows, 0)
    length = lax.dynamic_index_in_dim(lengths, sequence, 0, keepdims=False)
    scores = jnp.einsum(
        "qkrd,jkd->krqj", query_blk, key_vecs, preferred_element_type=jnp.float32
    ) * HD ** (-0.5)
    query_pos = row_start % LEN + jnp.arange(block_rows)
    key_pos = jnp.arange(LEN)
    allowed = (key_pos[None, :] <= query_pos[:, None]) & (key_pos[None, :] < length)
    return (jnp.where(allowed, scores, -1e30), sequence, row_start, query_blk, key_vecs)


def attend(queries, key_vecs, values, lengths):
    total_rows = queries.shape[0]
    block_rows = min(512, LEN)
    blocks = total_rows // block_rows

    def one_block(block_index):
        scores, sequence, row_start, query_blk, key_seq = block_scores(
            queries, key_vecs, lengths, block_index, block_rows
        )
        row_max = jnp.max(scores, axis=-1, keepdims=True)
        exp_scores = jnp.exp(scores - row_max)
        denom = jnp.sum(exp_scores, axis=-1, keepdims=True)
        soft_low = (exp_scores / denom).astype(jnp.bfloat16)
        result = jnp.einsum("krqj,jkd->qkrd", soft_low, values, preferred_element_type=jnp.float32)
        return (result, row_max[..., 0] + jnp.log(denom[..., 0]))

    results, logsum = lax.map(one_block, jnp.arange(blocks, dtype=jnp.int32))
    return (results.reshape((total_rows,) + queries.shape[1:]), logsum)


def attend_back(queries, key_vecs, values, grad_heads, logsum, lengths):
    total_rows = queries.shape[0]
    block_rows = min(512, LEN)
    blocks = total_rows // block_rows

    def one_block(carry, item):
        key_acc, value_acc = carry
        block_index, logsum_blk = item
        scores, sequence, row_start, query_blk, key_seq = block_scores(
            queries, key_vecs, lengths, block_index, block_rows
        )
        grad_blk = lax.dynamic_slice_in_dim(grad_heads, row_start, block_rows, 0)
        soft_weights = jnp.exp(scores - logsum_blk[..., None])
        grad_soft = jnp.einsum(
            "qkrd,jkd->krqj", grad_blk, values, preferred_element_type=jnp.float32
        )
        inner_sum = jnp.sum(soft_weights * grad_soft, axis=-1, keepdims=True)
        grad_scores = (soft_weights * (grad_soft - inner_sum)).astype(jnp.bfloat16)
        grad_query = jnp.einsum(
            "krqj,jkd->qkrd", grad_scores, key_seq, preferred_element_type=jnp.float32
        ) * HD ** (-0.5)
        grad_keyblk = jnp.einsum(
            "krqj,qkrd->jkd", grad_scores, query_blk, preferred_element_type=jnp.float32
        ) * HD ** (-0.5)
        grad_valblk = jnp.einsum(
            "krqj,qkrd->jkd",
            soft_weights.astype(jnp.bfloat16),
            grad_blk,
            preferred_element_type=jnp.float32,
        )
        key_acc = add_rows(key_acc, grad_keyblk)
        value_acc = add_rows(value_acc, grad_valblk)
        return ((key_acc, value_acc), grad_query)

    zero_keys = jnp.zeros(key_vecs.shape, jnp.float32)
    (grad_keys, grad_values), grad_queries = lax.scan(
        one_block, (zero_keys, zero_keys), (jnp.arange(blocks, dtype=jnp.int32), logsum)
    )
    return (grad_queries.reshape((total_rows,) + queries.shape[1:]), grad_keys, grad_values)


def body(
    tokens,
    lengths,
    attn_gain,
    w_query,
    w_key,
    w_value,
    w_output,
    mlp_gain,
    w_gate,
    w_up,
    w_down,
    cotangent,
):
    local_rows = tokens.shape[0]
    token_full = tokens.astype(jnp.float32)
    gain_attn = attn_gain.astype(jnp.float32)
    gain_mlp = mlp_gain.astype(jnp.float32)
    inv_first = lax.rsqrt(jnp.mean(token_full * token_full, axis=1, keepdims=True) + epsilon)
    normed_attn = (token_full * inv_first * gain_attn).astype(jnp.bfloat16)
    rows_attn = lax.all_gather(normed_attn, "tensor", axis=0, tiled=True)
    group_rows = rows_attn.shape[0]
    cosine_table, sine_table = rope_tables(jnp.arange(group_rows) % LEN)
    query_all, key_all, value_all, output_all = gather_attention(w_query, w_key, w_value, w_output)
    heads_local = query_all.shape[1] // HD
    kv_local = key_all.shape[1] // HD
    query_pre = jnp.dot(rows_attn, query_all, preferred_element_type=jnp.float32)
    key_pre = jnp.dot(rows_attn, key_all, preferred_element_type=jnp.float32)
    values = (
        jnp.dot(rows_attn, value_all, preferred_element_type=jnp.float32)
        .astype(jnp.bfloat16)
        .reshape(group_rows, kv_local, HD)
    )
    queries = rope_apply(
        query_pre.reshape(group_rows, heads_local, HD), cosine_table, sine_table
    ).astype(jnp.bfloat16)
    queries = queries.reshape(group_rows, kv_local, heads_local // kv_local, HD)
    key_vecs = rope_apply(
        key_pre.reshape(group_rows, kv_local, HD), cosine_table, sine_table
    ).astype(jnp.bfloat16)
    head_full, logsum = attend(queries, key_vecs, values, lengths)
    head_out = head_full.reshape(group_rows, heads_local * HD).astype(jnp.bfloat16)
    picked = head_out
    attn_branch = lax.psum_scatter(
        jnp.dot(picked, output_all, preferred_element_type=jnp.float32),
        "tensor",
        scatter_dimension=0,
        tiled=True,
    )
    hidden = token_full + attn_branch
    inv_second = lax.rsqrt(jnp.mean(hidden * hidden, axis=1, keepdims=True) + epsilon)
    normed_mlp = (hidden * inv_second * gain_mlp).astype(jnp.bfloat16)
    rows_mlp = lax.all_gather(normed_mlp, "tensor", axis=0, tiled=True)
    gate_all, up_all, down_all = gather_mlp(w_gate, w_up, w_down)
    gate_proj = jnp.dot(rows_mlp, gate_all, preferred_element_type=jnp.float32)
    up_proj = jnp.dot(rows_mlp, up_all, preferred_element_type=jnp.float32)
    gate_sig = jax.nn.sigmoid(gate_proj)
    activated = (gate_proj * gate_sig * up_proj).astype(jnp.bfloat16)
    picked = activated
    mlp_branch = lax.psum_scatter(
        jnp.dot(picked, down_all, preferred_element_type=jnp.float32).astype(jnp.bfloat16),
        "tensor",
        scatter_dimension=0,
        tiled=True,
    ).astype(jnp.float32)
    layer_out = (hidden + mlp_branch).astype(jnp.bfloat16)
    group_row = lax.axis_index("tensor") * local_rows + jnp.arange(local_rows)
    row_seq = group_row // LEN
    row_pos = group_row % LEN
    seq_ids = jnp.arange(lengths.shape[0])
    row_len = jnp.sum(jnp.where(row_seq[:, None] == seq_ids[None, :], lengths[None, :], 0), axis=1)
    valid_rows = (row_pos < row_len).astype(jnp.float32)
    cot_masked = cotangent.astype(jnp.float32) * valid_rows[:, None]
    gate_all, up_all, down_all = gather_mlp(w_gate, w_up, w_down)
    grad_branch = lax.all_gather(cot_masked.astype(jnp.bfloat16), "tensor", axis=0, tiled=True)
    grad_down = jnp.einsum("gf,gd->fd", activated, grad_branch, preferred_element_type=jnp.float32)
    grad_act = jnp.einsum("gd,fd->gf", grad_branch, down_all, preferred_element_type=jnp.float32)
    grad_gate_pre = (grad_act * up_proj * gate_sig * (1.0 + gate_proj * (1.0 - gate_sig))).astype(
        jnp.bfloat16
    )
    grad_up_pre = (grad_act * gate_proj * gate_sig).astype(jnp.bfloat16)
    grad_gate = jnp.einsum("gd,gf->df", rows_mlp, grad_gate_pre, preferred_element_type=jnp.float32)
    grad_up = jnp.einsum("gd,gf->df", rows_mlp, grad_up_pre, preferred_element_type=jnp.float32)
    grad_gate, grad_up, grad_down = (
        lax.psum_scatter(grad_gate, "dp", scatter_dimension=0, tiled=True),
        lax.psum_scatter(grad_up, "dp", scatter_dimension=0, tiled=True),
        lax.psum_scatter(grad_down, "dp", scatter_dimension=1, tiled=True),
    )
    grad_norm_two = lax.psum_scatter(
        jnp.einsum("gf,df->gd", grad_gate_pre, gate_all, preferred_element_type=jnp.float32)
        + jnp.einsum("gf,df->gd", grad_up_pre, up_all, preferred_element_type=jnp.float32),
        "tensor",
        scatter_dimension=0,
        tiled=True,
    )
    scaled_two = grad_norm_two * gain_mlp
    gain_two_part = jnp.sum(grad_norm_two * hidden * inv_second, axis=0)
    grad_hidden = (
        cot_masked
        + inv_second * scaled_two
        - hidden * inv_second**3 * jnp.mean(scaled_two * hidden, axis=1, keepdims=True)
    )
    query_all, key_all, value_all, output_all = gather_attention(w_query, w_key, w_value, w_output)
    grad_attn = lax.all_gather(grad_hidden.astype(jnp.bfloat16), "tensor", axis=0, tiled=True)
    grad_output = jnp.einsum("gh,gd->hd", head_out, grad_attn, preferred_element_type=jnp.float32)
    grad_heads = jnp.einsum(
        "gd,hd->gh", grad_attn, output_all, preferred_element_type=jnp.float32
    ).astype(jnp.bfloat16)
    grad_heads = grad_heads.reshape(group_rows, kv_local, heads_local // kv_local, HD)
    grad_queries, grad_keys, grad_values = attend_back(
        queries, key_vecs, values, grad_heads, logsum, lengths
    )
    grad_qpre = rope_back(
        grad_queries.reshape(group_rows, heads_local, HD), cosine_table, sine_table
    )
    grad_qpre = grad_qpre.astype(jnp.bfloat16).reshape(group_rows, heads_local * HD)
    grad_kpre = (
        rope_back(grad_keys, cosine_table, sine_table)
        .astype(jnp.bfloat16)
        .reshape(group_rows, kv_local * HD)
    )
    grad_vpre = grad_values.astype(jnp.bfloat16).reshape(group_rows, kv_local * HD)
    grad_query = jnp.einsum("gd,gh->dh", rows_attn, grad_qpre, preferred_element_type=jnp.float32)
    grad_key = jnp.einsum("gd,gh->dh", rows_attn, grad_kpre, preferred_element_type=jnp.float32)
    grad_value = jnp.einsum("gd,gh->dh", rows_attn, grad_vpre, preferred_element_type=jnp.float32)
    grad_query, grad_key, grad_value, grad_output = (
        lax.psum_scatter(grad_query, "dp", scatter_dimension=0, tiled=True),
        lax.psum_scatter(grad_key, "dp", scatter_dimension=0, tiled=True),
        lax.psum_scatter(grad_value, "dp", scatter_dimension=0, tiled=True),
        lax.psum_scatter(grad_output, "dp", scatter_dimension=1, tiled=True),
    )
    grad_norm_one = lax.psum_scatter(
        jnp.einsum("gh,dh->gd", grad_qpre, query_all, preferred_element_type=jnp.float32)
        + jnp.einsum("gh,dh->gd", grad_kpre, key_all, preferred_element_type=jnp.float32)
        + jnp.einsum("gh,dh->gd", grad_vpre, value_all, preferred_element_type=jnp.float32),
        "tensor",
        scatter_dimension=0,
        tiled=True,
    )
    scaled_one = grad_norm_one * gain_attn
    gain_one_part = jnp.sum(grad_norm_one * token_full * inv_first, axis=0)
    grad_tokens = (
        grad_hidden
        + inv_first * scaled_one
        - token_full * inv_first**3 * jnp.mean(scaled_one * token_full, axis=1, keepdims=True)
    )
    grad_attn_gain, grad_mlp_gain = (
        lax.psum_scatter(gain_one_part, ("dp", "tensor"), scatter_dimension=0, tiled=True),
        lax.psum_scatter(gain_two_part, ("dp", "tensor"), scatter_dimension=0, tiled=True),
    )
    return (
        layer_out,
        grad_tokens,
        grad_query,
        grad_key,
        grad_value,
        grad_output,
        grad_gate,
        grad_up,
        grad_down,
        grad_attn_gain,
        grad_mlp_gain,
    )


def solution(mesh):
    in_specs = (
        P(("dp", "tensor"), None),
        P("dp"),
        P(),
        P("dp", "tensor"),
        P("dp", "tensor"),
        P("dp", "tensor"),
        P("tensor", "dp"),
        P(),
        P("dp", "tensor"),
        P("dp", "tensor"),
        P("tensor", "dp"),
        P(("dp", "tensor"), None),
    )
    out_specs = (
        P(("dp", "tensor"), None),
        P(("dp", "tensor"), None),
        P("dp", "tensor"),
        P("dp", "tensor"),
        P("dp", "tensor"),
        P("tensor", "dp"),
        P("dp", "tensor"),
        P("dp", "tensor"),
        P("tensor", "dp"),
        P(("dp", "tensor")),
        P(("dp", "tensor")),
    )
    return jax.shard_map(body, mesh=mesh, in_specs=in_specs, out_specs=out_specs, check_vma=False)
```

profile of v0, /device:TPU:0, one launch (start us, length us, event | category | flops | bytes accessed | tf_op | source)
XLA Modules:
  0.0 2289.9 jit_solution(13640120241173803262)
XLA Ops:
  15.9 33.1 %all_gather.42 = bf16[2048,128]{1,0:T(8,128)(2,1)S(1)} all-gather(bf16[256,128]{1,0:T(8,128)(2,1)S(1)} %copy-done.27), channel_id=1, replica_groups=mesh['dp'=8,'tensor'=4] {'dp'}, dimensions={0}, use_global_device_ids=true | all-gather | bytes 589824 | tf_op jit(solution)/shard_map/all_gather | solution.py:48
  49.0 31.9 %all_gather.43 = bf16[2048,128]{1,0:T(8,128)(2,1)S(1)} all-gather(bf16[256,128]{1,0:T(8,128)(2,1)S(1)} %copy-done.28), channel_id=1, replica_groups=mesh['dp'=8,'tensor'=4] {'dp'}, dimensions={0}, use_global_device_ids=true | all-gather | bytes 589824 | tf_op jit(solution)/shard_map/all_gather | solution.py:49
  80.9 3.9 fusion.70
  85.5 17.7 all-gather.12.cloned.1.call-done
  103.3 5.2 fusion.69
  113.4 33.0 %while.31 = (s32[]{:T(128)}, bf16[2,512,2,4,64]{1,4,3,2,0:T(8,128)(2,1)S(1)}, f32[2,2,4,512]{3,2,1,0:T(4,128)}, s32[2]{0:T(128)S(1)}, s32[1]{0:T(128)}, /*index=...) while((s32[]{:T(128)}, ...), condition=%wide.region_4.5_spmd, body=%wide.region_1.4_spmd.sunk | while | flops 1125119488 | bytes 54663480 | solution.py:97
  116.0 3.9 bitcast_reduce_fusion.2
  119.9 4.4 fusion.149
  124.2 5.1 fusion.150
  132.3 3.9 bitcast_reduce_fusion.2
  136.3 4.4 fusion.149
  140.6 5.1 fusion.150
  147.7 6.5 all-gather.14.cloned.1.call-done
  154.2 7.2 fusion.71
  162.1 69.1 %reduce-scatter.12.cloned.1.call-done = f32[256,2048]{1,0:T(8,128)} async-done(((f32[1024,2048]{1,0:T(8,128)}), f32[256,2048]{1,0:T(8,128)}) %reduce-scatter.12.cloned.1.call-update) | async-done | bytes 2097168 | tf_op jit(solution)/shard_map/reduce_scatter | solution.py:185
  239.1 118.6 %all-gather.20.cloned.1.call-done = bf16[2048,2048]{1,0:T(8,128)(2,1)} async-done(((bf16[256,2048]{1,0:T(8,128)(2,1)}), bf16[2048,2048]{1,0:T(8,128)(2,1)}) %all-gather.20.cloned.1.call-update) | async-done | bytes 8388624 | tf_op jit(solution)/shard_map/all_gather | solution.py:57
  357.7 34.7 %all-gather.16.cloned.1.call-done = bf16[1024,2048]{1,0:T(8,128)(2,1)} async-done(((bf16[256,2048]{1,0:T(8,128)(2,1)}), bf16[1024,2048]{1,0:T(8,128)(2,1)}) %all-gather.16.cloned.1.call-update) | async-done | bytes 4194320 | tf_op jit(solution)/shard_map/all_gather | solution.py:194
  392.3 15.0 fusion.73
  407.3 111.7 %all-gather.18.cloned.1.call-done = bf16[2048,2048]{1,0:T(8,128)(2,1)} async-done(((bf16[256,2048]{1,0:T(8,128)(2,1)}), bf16[2048,2048]{1,0:T(8,128)(2,1)}) %all-gather.18.cloned.1.call-update) | async-done | bytes 8388624 | tf_op jit(solution)/shard_map/all_gather | solution.py:56
  519.0 14.5 fusion.72
  533.5 20.3 all-gather.24.cloned.1.call-done
  553.8 127.0 %all-gather.22.cloned.1.call-done = bf16[2048,2048]{1,0:T(8,128)(2,1)} async-done(((bf16[2048,256]{1,0:T(8,128)(2,1)}), bf16[2048,2048]{1,0:T(8,128)(2,1)}) %all-gather.22.cloned.1.call-update) | async-done | bytes 8388624 | tf_op jit(solution)/shard_map/all_gather | solution.py:58
  680.8 22.1 multiply_convert_fusion
  702.9 12.9 fusion.74
  715.8 13.6 convolution_add_fusion
  729.5 13.9 convolution_convert_fusion
  743.5 55.7 %reduce-scatter.16.cloned.1.call-done = f32[256,2048]{1,0:T(8,128)} async-done(((f32[1024,2048]{1,0:T(8,128)}), f32[256,2048]{1,0:T(8,128)}) %reduce-scatter.16.cloned.1.call-update) | async-done | bytes 2097168 | tf_op jit(solution)/shard_map/reduce_scatter | solution.py:230
  801.9 44.4 %reduce-scatter.14.cloned.1.call-done = bf16[256,2048]{1,0:T(8,128)(2,1)} async-done(((bf16[1024,2048]{1,0:T(8,128)(2,1)}), bf16[256,2048]{1,0:T(8,128)(2,1)}) %reduce-scatter.14.cloned.1.call-update) | async-done | bytes 1048592 | tf_op jit(solution)/shard_map/reduce_scatter | solution.py:201
  846.3 4.7 fusion.68
  851.1 34.5 %all-gather.26.cloned.1.call-done = bf16[1024,2048]{1,0:T(8,128)(2,1)} async-done(((bf16[256,2048]{1,0:T(8,128)(2,1)}), bf16[1024,2048]{1,0:T(8,128)(2,1)}) %all-gather.26.cloned.1.call-update) | async-done | bytes 4194320 | tf_op jit(solution)/shard_map/all_gather | solution.py:245
  885.6 6.2 convolution_convert_fusion.1
  891.8 129.4 %while.32 = (s32[]{:T(128)}, f32[1024,2,64]{0,2,1:T(8,128)S(1)}, f32[1024,2,64]{0,2,1:T(8,128)}, f32[2,512,2,4,64]{1,0,4,3,2:T(2,128)}, s32[2]{0:T(128)S(1)}, /*...) while((s32[]{:T(128)}, f32[1024,2,64]{0,2,1:T(8,128)S(1)}, ...), condition=%wide.region_12.13_spmd.clone, body=%wide.region_10.12_spmd.clone.sunk | while | flops 2749232640 | bytes 176085424 | solution.py:136
  895.3 3.6 fusion.159
  898.9 5.3 fusion.164
  904.2 11.0 fusion.161
  915.2 8.2 fusion.162
  923.4 3.3 copy-done
  929.4 6.0 fusion.165
  936.5 19.6 dynamic_update_slice.28
  959.2 3.6 fusion.159
  962.8 6.3 fusion.164
  969.2 11.0 fusion.161
  980.1 8.2 fusion.162
  988.3 3.3 copy-done
  994.4 6.0 fusion.165
  1001.5 19.6 dynamic_update_slice.28
  1025.0 2.8 reshape_reshape.7
  1036.0 4.6 add_add_fusion
  1040.7 4.5 fusion.78
  1045.2 5.2 fusion.79
  1050.7 7.7 fusion.80
  1058.5 6.5 fusion.77
  1065.1 15.3 fusion.82
  1080.8 15.3 fusion.81
  1096.2 15.4 fusion.83
  1115.1 39.9 %all-reduce.2 = (f32[2048]{0:T(1024)S(1)}, f32[2048]{0:T(1024)S(1)}) all-reduce(f32[2048]{0:T(1024)S(1)} %get-tuple-element.297, f32[2048]{0:T(1024)S(1)} %copy-done.29), channel_id=13, replica_groups=mesh['dp'=8,'tensor'=4] {'dp','tensor'}, use_global_device_ids=true, to_apply=%region_23.24.clone | all-reduce | flops 4096 | bytes 32768
  1156.2 3.5 fusion.51
  1159.7 20.7 reduce-scatter.22.cloned.1.call-done
  1180.4 67.1 %reduce-scatter.24.cloned.1.call-done = f32[256,128]{1,0:T(8,128)} async-done(((f32[2048,128]{1,0:T(8,128)}), f32[256,128]{1,0:T(8,128)}) %reduce-scatter.24.cloned.1.call-update) | async-done | bytes 131088 | tf_op jit(solution)/shard_map/reduce_scatter | solution.py:270
  1247.5 91.8 %reduce-scatter.26.cloned.1.call-done = f32[512,256]{1,0:T(8,128)} async-done(((f32[512,2048]{1,0:T(8,128)}), f32[512,256]{1,0:T(8,128)}) %reduce-scatter.26.cloned.1.call-update) | async-done | bytes 524304 | tf_op jit(solution)/shard_map/reduce_scatter | solution.py:271
  1339.2 92.0 %reduce-scatter.20.cloned.1.call-done = f32[256,512]{1,0:T(8,128)} async-done(((f32[2048,512]{1,0:T(8,128)}), f32[256,512]{1,0:T(8,128)}) %reduce-scatter.20.cloned.1.call-update) | async-done | bytes 524304 | tf_op jit(solution)/shard_map/reduce_scatter | solution.py:268
  1431.3 284.1 %reduce-scatter.30.cloned.1.call-done = f32[256,2048]{1,0:T(8,128)} async-done(((f32[2048,2048]{1,0:T(8,128)}), f32[256,2048]{1,0:T(8,128)}) %reduce-scatter.30.cloned.1.call-update) | async-done | bytes 2097168 | tf_op jit(solution)/shard_map/reduce_scatter | solution.py:227
  1715.4 283.7 %reduce-scatter.28.cloned.1.call-done = f32[256,2048]{1,0:T(8,128)} async-done(((f32[2048,2048]{1,0:T(8,128)}), f32[256,2048]{1,0:T(8,128)}) %reduce-scatter.28.cloned.1.call-update) | async-done | bytes 2097168 | tf_op jit(solution)/shard_map/reduce_scatter | solution.py:226
  1999.1 283.5 %reduce-scatter.32.cloned.1.call-done = f32[2048,256]{1,0:T(8,128)} async-done(((f32[2048,2048]{1,0:T(8,128)}), f32[2048,256]{1,0:T(8,128)}) %reduce-scatter.32.cloned.1.call-update) | async-done | bytes 2097168 | tf_op jit(solution)/shard_map/reduce_scatter | solution.py:228
  (187 shorter events, 60.6 us)
Async XLA Ops:
  7.2 8.7 copy-start.27
  7.2 41.8 %copy-start.28 = (bf16[256,128]{1,0:T(8,128)(2,1)S(1)}, bf16[256,128]{1,0:T(8,128)(2,1)}, u32[]{:S(2)}) copy-start(bf16[256,128]{1,0:T(8,128)(2,1)} %param.21) | copy-start | bytes 196612
  7.2 73.7 %all-gather.10.cloned.1.call-start = ((), (), s32[]{:S(2)}) async-start(), calls=%async_computation.11 | async-start | bytes 5242880 | tf_op jit(solution)/shard_map/all_gather | solution.py:162
  9.4 6.5 copy-start.30
  10.1 0.6 copy-start.25
  13.2 90.1 %all-gather.12.cloned.1.call-start = ((), (), s32[]{:S(2)}) async-start(), calls=%async_computation.12 | async-start | bytes 2359296 | tf_op jit(solution)/shard_map/all_gather | solution.py:47
  13.9 140.3 %all-gather.14.cloned.1.call-start = ((), (), s32[]{:S(2)}) async-start(), calls=%async_computation.13 | async-start | bytes 2359296 | tf_op jit(solution)/shard_map/all_gather | solution.py:50
  14.7 216.5 %reduce-scatter.12.cloned.1.call-start = ((), (), s32[]{:S(2)}) async-start(), calls=%async_computation.14 | async-start | bytes 10485760 | tf_op jit(solution)/shard_map/reduce_scatter | solution.py:185
  15.8 94.5 %copy-start.9 = (f32[1024,64]{0,1:T(8,128)}, f32[1024,64]{0,1:T(8,128)S(1)}, u32[]{:S(2)}) copy-start(f32[1024,64]{0,1:T(8,128)S(1)} %get-tuple-element.360) | copy-start | bytes 786436
  15.8 94.5 %copy-start.11 = (f32[1024,64]{0,1:T(8,128)}, f32[1024,64]{0,1:T(8,128)S(1)}, u32[]{:S(2)}) copy-start(f32[1024,64]{0,1:T(8,128)S(1)} %get-tuple-element.359) | copy-start | bytes 786436
  49.0 59.5 %copy-start.15 = (bf16[2048,128]{1,0:T(8,128)(2,1)}, bf16[2048,128]{1,0:T(8,128)(2,1)S(1)}, u32[]{:S(2)}) copy-start(bf16[2048,128]{1,0:T(8,128)(2,1)S(1)} %all_gather.42) | copy-start | bytes 1572868
  80.9 31.0 %copy-start.13 = (bf16[2048,128]{1,0:T(8,128)(2,1)}, bf16[2048,128]{1,0:T(8,128)(2,1)S(1)}, u32[]{:S(2)}) copy-start(bf16[2048,128]{1,0:T(8,128)(2,1)S(1)} %all_gather.43) | copy-start | bytes 1572868
  108.5 1.0 copy-start.22
  108.8 3.1 copy-start.1
  146.3 15.1 copy-start.4
  147.7 13.8 copy-start.20
  161.4 0.7 copy-start.33
  161.4 69.8 %copy-start.2 = (bf16[256,2048]{1,0:T(8,128)(2,1)S(1)}, bf16[256,2048]{1,0:T(8,128)(2,1)}, u32[]{:S(2)}) copy-start(bf16[256,2048]{1,0:T(8,128)(2,1)} %param.16) | copy-start | bytes 3145732
  161.5 196.2 %all-gather.20.cloned.1.call-start = ((), (), s32[]{:S(2)}) async-start(), calls=%async_computation.17 | async-start | bytes 9437184 | tf_op jit(solution)/shard_map/all_gather | solution.py:57
  162.1 230.3 %all-gather.16.cloned.1.call-start = ((), (), s32[]{:S(2)}) async-start(), calls=%async_computation.15 | async-start | bytes 5242880 | tf_op jit(solution)/shard_map/all_gather | solution.py:194
  234.4 284.6 %all-gather.18.cloned.1.call-start = ((), (), s32[]{:S(2)}) async-start(), calls=%async_computation.16 | async-start | bytes 9437184 | tf_op jit(solution)/shard_map/all_gather | solution.py:56
  235.2 318.6 %all-gather.24.cloned.1.call-start = ((), (), s32[]{:S(2)}) async-start(), calls=%async_computation.20 | async-start | bytes 5242880 | tf_op jit(solution)/shard_map/all_gather | solution.py:216
  238.3 442.5 %all-gather.22.cloned.1.call-start = ((), (), s32[]{:S(2)}) async-start(), calls=%async_computation.18 | async-start | bytes 9437184 | tf_op jit(solution)/shard_map/all_gather | solution.py:58
  239.1 560.1 %reduce-scatter.16.cloned.1.call-start = ((), (), s32[]{:S(2)}) async-start(), calls=%async_computation.21 | async-start | bytes 10485760 | tf_op jit(solution)/shard_map/reduce_scatter | solution.py:230
  702.9 12.9 copy-start.35
  729.4 116.9 %reduce-scatter.14.cloned.1.call-start = ((), (), s32[]{:S(2)}) async-start(), calls=%async_computation.19 | async-start | bytes 5242880 | tf_op jit(solution)/shard_map/reduce_scatter | solution.py:201
  743.4 102.9 %copy-start.17 = (bf16[256,2048]{1,0:T(8,128)(2,1)S(1)}, bf16[256,2048]{1,0:T(8,128)(2,1)}, u32[]{:S(2)}) copy-start(bf16[256,2048]{1,0:T(8,128)(2,1)} %param.27) | copy-start | bytes 3145732
  743.4 142.2 %all-gather.26.cloned.1.call-start = ((), (), s32[]{:S(2)}) async-start(), calls=%async_computation.22 | async-start | bytes 5242880 | tf_op jit(solution)/shard_map/all_gather | solution.py:245
  851.0 261.2 %reduce-scatter.18.cloned.1.call-start = ((), (), s32[]{:S(2)}) async-start(), calls=%async_computation.23 | async-start | bytes 10485760 | tf_op jit(solution)/shard_map/reduce_scatter | solution.py:273
  894.9 4.0 copy-start.18
  895.3 3.6 copy-start.8
  923.4 3.3 copy-start
  958.8 4.0 copy-start.18
  959.2 3.6 copy-start.8
  988.3 3.3 copy-start
  1021.3 3.8 copy-start.6
  1025.0 3.3 copy-start.10
  1027.8 1.6 copy-start.7
  1029.4 0.9 copy-start.12
  1029.4 1.0 copy-start.23
  1029.4 1.1 copy-start.24
  1029.4 1.3 copy-start.16
  1032.0 1.6 copy-start.34
  1033.6 2.4 copy-start.14
  1033.6 2.4 copy-start.19
  1040.6 139.8 %reduce-scatter.22.cloned.1.call-start = ((), (), s32[]{:S(2)}) async-start(), calls=%async_computation.25 | async-start | bytes 1179648 | tf_op jit(solution)/shard_map/reduce_scatter | solution.py:269
  1045.1 5.6 copy-start.21
  1045.2 202.3 %reduce-scatter.24.cloned.1.call-start = ((), (), s32[]{:S(2)}) async-start(), calls=%async_computation.26 | async-start | bytes 1179648 | tf_op jit(solution)/shard_map/reduce_scatter | solution.py:270
  1050.4 288.8 %reduce-scatter.26.cloned.1.call-start = ((), (), s32[]{:S(2)}) async-start(), calls=%async_computation.27 | async-start | bytes 4718592 | tf_op jit(solution)/shard_map/reduce_scatter | solution.py:271
  1058.5 372.8 %reduce-scatter.20.cloned.1.call-start = ((), (), s32[]{:S(2)}) async-start(), calls=%async_computation.24 | async-start | bytes 4718592 | tf_op jit(solution)/shard_map/reduce_scatter | solution.py:268
  1065.1 650.3 %reduce-scatter.30.cloned.1.call-start = ((), (), s32[]{:S(2)}) async-start(), calls=%async_computation.29 | async-start | bytes 18874368 | tf_op jit(solution)/shard_map/reduce_scatter | solution.py:227
  1080.5 918.6 %reduce-scatter.28.cloned.1.call-start = ((), (), s32[]{:S(2)}) async-start(), calls=%async_computation.28 | async-start | bytes 18874368 | tf_op jit(solution)/shard_map/reduce_scatter | solution.py:226
  1096.1 1186.5 %reduce-scatter.32.cloned.1.call-start = ((), (), s32[]{:S(2)}) async-start(), calls=%async_computation.30 | async-start | bytes 18874368 | tf_op jit(solution)/shard_map/reduce_scatter | solution.py:228
  1111.5 1.3 copy-start.3
  1111.5 1.3 copy-start.26
  1111.5 1.3 copy-start.31
  1111.5 3.5 copy-start.29
  1111.6 44.6 %copy-start.32 = (f32[256]{0:T(256)S(1)}, f32[256]{0:T(256)}, u32[]{:S(2)}) copy-start(f32[256]{0:T(256)} %get-tuple-element.361) | copy-start | bytes 3076
  1112.8 43.4 %copy-start.5 = (f32[256,2048]{1,0:T(8,128)S(1)}, f32[256,2048]{1,0:T(8,128)}, u32[]{:S(2)}) copy-start(f32[256,2048]{1,0:T(8,128)} %reduce-scatter.18.cloned.1.call-done) | copy-start | bytes 6291460
Sparse Core Ops, SparseCore 0:
  13.3 37.1 all-gather.9
  52.6 50.5 all-gather.11
  105.3 48.8 all-gather.13
  161.6 69.5 reduce-scatter.11
  233.2 124.4 all-gather.19
  359.7 32.6 all-gather.15
  394.5 124.4 all-gather.17
  521.1 32.6 all-gather.23
  555.8 124.9 all-gather.21
  729.6 69.5 reduce-scatter.15
  801.7 44.5 reduce-scatter.13
  851.1 34.4 all-gather.25
  1040.7 71.4 reduce-scatter.17
  1116.0 64.2 reduce-scatter.21
  1184.2 63.2 reduce-scatter.23
  1251.5 87.6 reduce-scatter.25
  1343.3 87.9 reduce-scatter.19
  1435.5 279.8 reduce-scatter.29
  1719.8 279.3 reduce-scatter.27
  2003.3 279.2 reduce-scatter.31
where the time goes:
time: 2300 us; the launch traced here: 2290 us
  waiting for transfers between devices  1770 us (77%)
  matrix products  271 us (12%)
  blocking collectives  105 us (5%)
  other arithmetic  64.5 us (3%)
  local copies, waits for them, and re-layouts  62 us (3%)
    reduce_scatter x1, waiting for transfers between devices, body(): lax.psum_scatter(grad_up, 'dp', scatter_dimension=0, tiled=True)  284 us
    reduce_scatter x1, waiting for transfers between devices, body(): lax.psum_scatter(grad_gate, 'dp', scatter_dimension=0, tiled=True)  284 us
    reduce_scatter x1, waiting for transfers between devices, body(): lax.psum_scatter(grad_down, 'dp', scatter_dimension=1, tiled=True)  284 us
    all_gather x1, waiting for transfers between devices, gather_mlp(): lax.all_gather(w_down, 'dp', axis=1, tiled=True)  127 us
    all_gather x1, waiting for transfers between devices, gather_mlp(): lax.all_gather(w_up, 'dp', axis=0, tiled=True)  119 us
    all_gather x1, waiting for transfers between devices, gather_mlp(): lax.all_gather(w_gate, 'dp', axis=0, tiled=True)  112 us
    reduce_scatter x1, waiting for transfers between devices, body(): lax.psum_scatter(grad_query, 'dp', scatter_dimension=0, tiled=True)  92 us
    reduce_scatter x1, waiting for transfers between devices, body(): lax.psum_scatter(grad_output, 'dp', scatter_dimension=1, tiled=True)  91.8 us
  transfers between devices with their start and end apart: 20, of which 19 were waited for; matrix products, arithmetic and copies ran while one was open for 8% of the time, Pallas kernels for 0%

commit v1 on v0

v1 whole, which is shorter than its diff:
```python
import functools

import jax
import jax.numpy as jnp
from jax import lax
from jax.experimental import pallas as pl
from jax.experimental.pallas import tpu as pltpu
from jax.sharding import PartitionSpec as P

HD = 64
LEN = 1024
QB = 256

epsilon = 1e-05
theta = 500000.0
MESH_ID = pl.DeviceIdType.MESH
BF16 = jnp.bfloat16
F32 = jnp.float32


def rope_frequencies():
    half_size = HD // 2
    base_freq = theta ** (-(jnp.arange(half_size, dtype=jnp.float32) * 2.0) / HD)
    wavelength = 2.0 * jnp.pi / base_freq
    smooth = (8192.0 / wavelength - 1.0) / 3.0
    middle = (1.0 - smooth) * base_freq / 32.0 + smooth * base_freq
    return jnp.where(
        wavelength < 2048.0, base_freq, jnp.where(wavelength > 8192.0, base_freq / 32.0, middle)
    )


def rope_tables():
    angles = jnp.arange(LEN, dtype=jnp.float32)[:, None] * rope_frequencies()[None, :]
    cosine, sine = jnp.cos(angles), jnp.sin(angles)
    return (
        jnp.concatenate([cosine] * 4, axis=1),
        jnp.concatenate([-sine, sine, -sine, sine], axis=1),
    )


def lane_index(shape):
    return lax.broadcasted_iota(jnp.int32, shape, 1)


def swap_halves(value):
    low = lane_index(value.shape) % HD < HD // 2
    return jnp.where(low, pltpu.roll(value, 128 - HD // 2, 1), pltpu.roll(value, HD // 2, 1))


def nt_dot(left, right):
    return lax.dot_general(left, right, (((1,), (1,)), ((), ())), preferred_element_type=F32)


def tn_dot(left, right):
    return lax.dot_general(left, right, (((0,), (0,)), ((), ())), preferred_element_type=F32)


def project_kernel(x_ref, wq_ref, wk_ref, wv_ref, cos_ref, sin_ref, q_ref, k_ref, v_ref):
    rows = x_ref[...]
    cosine, sine = cos_ref[...], sin_ref[...]

    def rope(value):
        return (value * cosine + swap_halves(value) * sine).astype(BF16)

    for block in range(q_ref.shape[1] // 256):
        cols = slice(block * 256, (block + 1) * 256)
        value = jnp.dot(rows, wq_ref[:, cols], preferred_element_type=F32)
        for half in range(2):
            start = block * 256 + half * 128
            q_ref[:, start : start + 128] = rope(value[:, half * 128 : half * 128 + 128])
    k_ref[...] = rope(jnp.dot(rows, wk_ref[...], preferred_element_type=F32))
    v_ref[...] = jnp.dot(rows, wv_ref[...], preferred_element_type=F32).astype(BF16)


def project(rows, w_query, w_key, w_value, cosine, sine):
    total, width = rows.shape
    block = 256

    def whole(array):
        return pl.BlockSpec(array.shape, lambda i: (0, 0))

    def by_rows(cols):
        return pl.BlockSpec((block, cols), lambda i: (i, 0))

    shapes = [w_query.shape[1], w_key.shape[1], w_value.shape[1]]
    return pl.pallas_call(
        project_kernel,
        grid=(total // block,),
        out_shape=[jax.ShapeDtypeStruct((total, s), BF16) for s in shapes],
        in_specs=[by_rows(width), whole(w_query), whole(w_key), whole(w_value)]
        + [by_rows(128)] * 2,
        out_specs=[by_rows(s) for s in shapes],
        compiler_params=pltpu.CompilerParams(vmem_limit_bytes=32 << 20),
        cost_estimate=pl.CostEstimate(
            flops=2 * total * width * sum(shapes), bytes_accessed=8 << 20, transcendentals=0
        ),
        name="project",
    )(rows, w_query, w_key, w_value, cosine, sine)


def pick_head(pair, which, kv):
    moved = jnp.where(kv == which, pair, pltpu.roll(pair, HD, 1))
    return jnp.where(lane_index(pair.shape) // HD == kv, moved, jnp.zeros_like(moved))


def join_heads(first, second, kv):
    first = jnp.where(kv == 0, first, pltpu.roll(first, HD, 1))
    second = jnp.where(kv == 1, second, pltpu.roll(second, HD, 1))
    return jnp.where(lane_index(first.shape) < HD, first, second)


def attend_kernel(length_ref, q_ref, k_ref, v_ref, o_ref):
    kv = pl.program_id(0) // 2
    length = length_ref[0]
    for block in range(LEN // QB):
        rows = slice(block * QB, (block + 1) * QB)
        keys = (block + 1) * QB
        pair = (q_ref[rows, :].astype(F32) * HD**-0.5).astype(F32)
        query_pos = block * QB + lax.broadcasted_iota(jnp.int32, (QB, keys), 0)
        key_pos = lax.broadcasted_iota(jnp.int32, (QB, keys), 1)
        allowed = (key_pos <= query_pos) & (key_pos < length)
        outs = []
        for which in range(2):
            query = pick_head(pair, which, kv).astype(BF16)
            scores = jnp.where(allowed, nt_dot(query, k_ref[:keys, :]), -1e30)
            exps = jnp.exp(scores - jnp.max(scores, axis=1, keepdims=True))
            probs = (exps / jnp.sum(exps, axis=1, keepdims=True)).astype(BF16)
            outs.append(jnp.dot(probs, v_ref[:keys, :], preferred_element_type=F32))
        o_ref[rows, :] = join_heads(outs[0], outs[1], kv).astype(BF16)


def attend(queries, keys, values, lengths):
    pairs = queries.shape[1] // 128
    whole = pl.BlockSpec((LEN, 128), lambda i: (0, 0))
    paired = pl.BlockSpec((LEN, 128), lambda i: (0, i))
    return pl.pallas_call(
        attend_kernel,
        grid=(pairs,),
        out_shape=jax.ShapeDtypeStruct(queries.shape, BF16),
        in_specs=[pl.BlockSpec(memory_space=pltpu.SMEM), paired, whole, whole],
        out_specs=paired,
        compiler_params=pltpu.CompilerParams(vmem_limit_bytes=48 << 20),
        cost_estimate=pl.CostEstimate(
            flops=12 << 30, bytes_accessed=4 << 20, transcendentals=8 << 20
        ),
        name="attend",
    )(lengths, queries, keys, values)


def attend_back_kernel(
    length_ref, q_ref, k_ref, v_ref, g_ref, cos_ref, sin_ref, gq_ref, gk_ref, gv_ref, acc_k, acc_v
):
    pair_index = pl.program_id(0)
    kv = pair_index // 2
    length = length_ref[0]

    @pl.when(pair_index == 0)
    def _():
        acc_k[...] = jnp.zeros_like(acc_k)
        acc_v[...] = jnp.zeros_like(acc_v)

    def rope_back(grads, rows):
        return grads * cos_ref[rows, :] + swap_halves(grads) * (-sin_ref[rows, :])

    for block in range(LEN // QB):
        rows = slice(block * QB, (block + 1) * QB)
        keys = (block + 1) * QB
        pair = q_ref[rows, :].astype(F32) * HD**-0.5
        grad_pair = g_ref[rows, :].astype(F32)
        key_pos = lax.broadcasted_iota(jnp.int32, (keys, QB), 0)
        query_pos = block * QB + lax.broadcasted_iota(jnp.int32, (keys, QB), 1)
        allowed = (key_pos <= query_pos) & (key_pos < length)
        key_vecs = k_ref[:keys, :]
        grad_queries = []
        for which in range(2):
            query = pick_head(pair, which, kv).astype(BF16)
            grad = pick_head(grad_pair, which, kv).astype(BF16)
            scores = jnp.where(allowed, nt_dot(key_vecs, query), -1e30)
            exps = jnp.exp(scores - jnp.max(scores, axis=0, keepdims=True))
            probs = exps / jnp.sum(exps, axis=0, keepdims=True)
            grad_probs = nt_dot(v_ref[:keys, :], grad)
            inner = jnp.sum(probs * grad_probs, axis=0, keepdims=True)
            grad_scores = (probs * (grad_probs - inner)).astype(BF16)
            acc_v[:keys, :] += jnp.dot(probs.astype(BF16), grad, preferred_element_type=F32)
            acc_k[:keys, :] += jnp.dot(grad_scores, query, preferred_element_type=F32)
            grad_queries.append(tn_dot(grad_scores, key_vecs) * HD**-0.5)
        joined = join_heads(grad_queries[0], grad_queries[1], kv)
        gq_ref[rows, :] = rope_back(joined, rows).astype(BF16)

    @pl.when(pair_index == pl.num_programs(0) - 1)
    def _():
        gk_ref[...] = rope_back(acc_k[...], slice(None)).astype(BF16)
        gv_ref[...] = acc_v[...].astype(BF16)


def attend_back(queries, keys, values, grad_heads, lengths, cosine, sine):
    pairs = queries.shape[1] // 128
    whole = pl.BlockSpec((LEN, 128), lambda i: (0, 0))
    paired = pl.BlockSpec((LEN, 128), lambda i: (0, i))
    narrow = jax.ShapeDtypeStruct((LEN, 128), BF16)
    return pl.pallas_call(
        attend_back_kernel,
        grid=(pairs,),
        out_shape=[jax.ShapeDtypeStruct(queries.shape, BF16), narrow, narrow],
        in_specs=[pl.BlockSpec(memory_space=pltpu.SMEM), paired, whole, whole, paired]
        + [whole] * 2,
        out_specs=[paired, whole, whole],
        scratch_shapes=[pltpu.VMEM((LEN, 128), F32)] * 2,
        compiler_params=pltpu.CompilerParams(vmem_limit_bytes=48 << 20),
        cost_estimate=pl.CostEstimate(
            flops=24 << 30, bytes_accessed=8 << 20, transcendentals=8 << 20
        ),
        name="attend_back",
    )(lengths, queries, keys, values, grad_heads, cosine, sine)


def ring_place(index, count):
    odd = index % 2
    return (1 - odd) * (index // 2) + odd * (count - 1 - index // 2)


def ring_member(place, count):
    high = place // (count // 2)
    return (1 - high) * (2 * place) + high * (2 * (count - 1 - place) + 1)


def ring_setup(count):
    place = ring_place(lax.axis_index("dp"), count)
    ahead = ring_member((place + 1) % count, count)
    behind = ring_member((place + count - 1) % count, count)
    barrier = pltpu.get_barrier_semaphore()
    for other in (ahead, behind):
        pl.semaphore_signal(barrier, inc=1, device_id={"dp": other}, device_id_type=MESH_ID)
    pl.semaphore_wait(barrier, 2)
    return place, (ahead, behind)


def member_at(place, side, steps, count):
    if side == 0:
        return ring_member((place + count - steps) % count, count)
    return ring_member((place + steps) % count, count)


def piece(ref, shape, axis, member, side, part, parts):
    rows, cols = shape
    sub = rows // (2 * parts)
    start = (side * parts + part) * sub
    if axis is None:
        return ref.at[pl.ds(start, sub), :]
    if axis == 0:
        return ref.at[pl.ds(pl.multiple_of(member * rows + start, sub), sub), :]
    return ref.at[pl.ds(start, sub), pl.ds(pl.multiple_of(member * cols, cols), cols)]


def gather_kernel(count, items, *refs):
    num = len(items)
    shards, outs = refs[:num], refs[num : 2 * num]
    stage = refs[2 * num : 3 * num]
    send_sems, recv_sems, local_sem = refs[3 * num :]
    place, neighbours = ring_setup(count)
    me = lax.axis_index("dp")
    slots = [(k, part) for k in range(num) for part in range(items[k][2])]

    def copy(step, side, slot):
        item, part = slots[slot]
        shape, axis, parts = items[item]
        origin = member_at(place, side, step, count)
        target = piece(outs[item], shape, axis, origin, side, part, parts)
        return target, pltpu.make_async_remote_copy(
            src_ref=target,
            dst_ref=target,
            send_sem=send_sems.at[side, step, slot],
            recv_sem=recv_sems.at[side, step, slot],
            device_id={"dp": neighbours[side]},
            device_id_type=MESH_ID,
        )

    for slot, (item, part) in enumerate(slots):
        shape, axis, parts = items[item]
        for side in range(2):
            pltpu.make_async_remote_copy(
                src_ref=piece(shards[item], shape, None, 0, side, part, parts),
                dst_ref=piece(outs[item], shape, axis, me, side, part, parts),
                send_sem=send_sems.at[side, 0, slot],
                recv_sem=recv_sems.at[side, 0, slot],
                device_id={"dp": neighbours[side]},
                device_id_type=MESH_ID,
            ).start()
    loads = [
        pltpu.make_async_copy(shards[k], stage[k], local_sem.at[k]) for k in range(num)
    ]
    for load in loads:
        load.start()
    stores = []
    for k in range(num):
        loads[k].wait()
        shape, axis, parts = items[k]
        rows, cols = shape
        if axis == 0:
            own = outs[k].at[pl.ds(pl.multiple_of(me * rows, rows), rows), :]
        else:
            own = outs[k].at[:, pl.ds(pl.multiple_of(me * cols, cols), cols)]
        stores.append(pltpu.make_async_copy(stage[k], own, local_sem.at[k]))
        stores[-1].start()

    def hop(step, carry):
        for slot in range(len(slots)):
            for side in range(2):
                copy(step - 1, side, slot)[1].wait_recv()
                copy(step, side, slot)[1].start()
        return carry

    lax.fori_loop(1, count - 1, hop, 0)
    for slot in range(len(slots)):
        for side in range(2):
            copy(count - 2, side, slot)[1].wait_recv()
    for store in stores:
        store.wait()

    def drain(step, carry):
        for slot in range(len(slots)):
            for side in range(2):
                copy(step, side, slot)[1].wait_send()
        return carry

    lax.fori_loop(0, count - 1, drain, 0)


def ring_gather(shards, axes, parts, count, collective_id):
    turned = [a == 1 and s.shape[1] % 128 != 0 for s, a in zip(shards, axes)]
    if any(turned):
        shards = [s.T if t else s for s, t in zip(shards, turned)]
        axes = [0 if t else a for a, t in zip(axes, turned)]
        outs = ring_gather(shards, axes, parts, count, collective_id)
        return [o.T if t else o for o, t in zip(outs, turned)]
    items = tuple((s.shape, a, q) for s, a, q in zip(shards, axes, parts))
    slots = sum(parts)
    outs = [
        jax.ShapeDtypeStruct(
            (s.shape[0] * count, s.shape[1]) if a == 0 else (s.shape[0], s.shape[1] * count),
            s.dtype,
        )
        for s, a in zip(shards, axes)
    ]
    num = len(shards)
    nbytes = sum(s.size * 2 * (count - 1) for s in shards)
    return pl.pallas_call(
        functools.partial(gather_kernel, count, items),
        out_shape=outs,
        in_specs=[pl.BlockSpec(memory_space=pl.ANY)] * num,
        out_specs=[pl.BlockSpec(memory_space=pl.ANY)] * num,
        scratch_shapes=[pltpu.VMEM(s.shape, s.dtype) for s in shards]
        + [
            pltpu.SemaphoreType.DMA((2, count - 1, slots)),
            pltpu.SemaphoreType.DMA((2, count - 1, slots)),
            pltpu.SemaphoreType.DMA((num,)),
        ],
        compiler_params=pltpu.CompilerParams(collective_id=collective_id, has_side_effects=True),
        cost_estimate=pl.CostEstimate(flops=0, bytes_accessed=20 * nbytes, transcendentals=0),
        name=f"ring_gather_{collective_id}",
    )(*shards)


def scatter_kernel(count, items, *refs):
    num = len(items)
    partials, outs = refs[:num], refs[num : 2 * num]
    own = refs[2 * num : 3 * num]
    held = refs[3 * num : 4 * num]
    total = refs[4 * num : 5 * num]
    send_sems, recv_sems, load_sems, store_sems = refs[5 * num :]
    slots = [(k, part) for k in range(num) for part in range(items[k][2])]

    def load(step, side, slot, place):
        item, part = slots[slot]
        shape, axis, parts = items[item]
        member = member_at(place, side, step + 1, count)
        return pltpu.make_async_copy(
            piece(partials[item], shape, axis, member, side, part, parts),
            own[item].at[side, step, part],
            load_sems.at[side, step, slot],
        )

    start_place = ring_place(lax.axis_index("dp"), count)

    def load_all(step, carry):
        for slot in range(len(slots)):
            for side in range(2):
                load(step, side, slot, start_place).start()
        return carry

    lax.fori_loop(0, count, load_all, 0)
    place, neighbours = ring_setup(count)

    def send(step, side, slot, source):
        item, part = slots[slot]
        return pltpu.make_async_remote_copy(
            src_ref=source,
            dst_ref=held[item].at[side, step, part],
            send_sem=send_sems.at[side, step, slot],
            recv_sem=recv_sems.at[side, step, slot],
            device_id={"dp": neighbours[side]},
            device_id_type=MESH_ID,
        )

    for slot, (item, part) in enumerate(slots):
        for side in range(2):
            load(0, side, slot, place).wait()
            send(0, side, slot, own[item].at[side, 0, part]).start()

    def hop(step, carry):
        for slot, (item, part) in enumerate(slots):
            for side in range(2):
                load(step, side, slot, place).wait()
                arrived = held[item].at[side, step - 1, part]
                send(step - 1, side, slot, arrived).wait_recv()
                arrived[...] = (
                    arrived[...].astype(jnp.float32)
                    + own[item][side, step, part].astype(jnp.float32)
                ).astype(jnp.bfloat16)
                send(step, side, slot, arrived).start()
        return carry

    lax.fori_loop(1, count - 1, hop, 0)
    last = count - 1
    stores = []
    for slot, (item, part) in enumerate(slots):
        shape, axis, parts = items[item]
        for side in range(2):
            load(last, side, slot, place).wait()
            arrived = held[item].at[side, last - 1, part]
            send(last - 1, side, slot, arrived).wait_recv()
            total[item][side, part] = arrived[...].astype(jnp.float32) + own[item][
                side, last, part
            ].astype(jnp.float32)
            stores.append(
                pltpu.make_async_copy(
                    total[item].at[side, part],
                    piece(outs[item], shape, None, 0, side, part, parts),
                    store_sems.at[side, slot],
                )
            )
            stores[-1].start()
    for store in stores:
        store.wait()

    def drain(step, carry):
        for slot, (item, part) in enumerate(slots):
            for side in range(2):
                send(step, side, slot, held[item].at[side, 0, part]).wait_send()
        return carry

    lax.fori_loop(0, count - 1, drain, 0)


def ring_scatter(partials, axes, parts, count, collective_id):
    turned = [a == 1 and p.shape[1] // count % 128 != 0 for p, a in zip(partials, axes)]
    if any(turned):
        partials = [p.T if t else p for p, t in zip(partials, turned)]
        axes = [0 if t else a for a, t in zip(axes, turned)]
        outs = ring_scatter(partials, axes, parts, count, collective_id)
        return [o.T if t else o for o, t in zip(outs, turned)]
    shapes = [
        (p.shape[0] // count, p.shape[1]) if a == 0 else (p.shape[0], p.shape[1] // count)
        for p, a in zip(partials, axes)
    ]
    items = tuple((s, a, q) for s, a, q in zip(shapes, axes, parts))
    slots = sum(parts)
    num = len(partials)

    def buffers(depth, dtype):
        return [
            pltpu.VMEM((2,) + depth + (q, s[0] // (2 * q), s[1]), dtype)
            for s, q in zip(shapes, parts)
        ]

    nbytes = sum(p.size * 2 for p in partials)
    return pl.pallas_call(
        functools.partial(scatter_kernel, count, items),
        out_shape=[jax.ShapeDtypeStruct(s, jnp.float32) for s in shapes],
        in_specs=[pl.BlockSpec(memory_space=pl.ANY)] * num,
        out_specs=[pl.BlockSpec(memory_space=pl.ANY)] * num,
        scratch_shapes=buffers((count,), jnp.bfloat16)
        + buffers((count - 1,), jnp.bfloat16)
        + buffers((), jnp.float32)
        + [
            pltpu.SemaphoreType.DMA((2, count - 1, slots)),
            pltpu.SemaphoreType.DMA((2, count - 1, slots)),
            pltpu.SemaphoreType.DMA((2, count, slots)),
            pltpu.SemaphoreType.DMA((2, slots)),
        ],
        compiler_params=pltpu.CompilerParams(
            collective_id=collective_id, has_side_effects=True, vmem_limit_bytes=48 << 20
        ),
        cost_estimate=pl.CostEstimate(flops=0, bytes_accessed=20 * nbytes, transcendentals=0),
        name=f"ring_scatter_{collective_id}",
    )(*partials)


def after(value, *deps):
    return lax.optimization_barrier((value,) + deps)[0]


def gather_rows(value):
    return lax.all_gather(value, "tensor", axis=0, tiled=True)


def scatter_rows(value):
    return lax.psum_scatter(value.astype(BF16), "tensor", scatter_dimension=0, tiled=True).astype(
        F32
    )


def share_kernel(count, group, parts_ref, out_ref, first, sums, second, sems):
    row, col = lax.axis_index("dp"), lax.axis_index("tensor")
    barrier = pltpu.get_barrier_semaphore()

    def in_group(shift):
        return {"tensor": (col + shift) % group}

    def in_column(shift):
        return {"dp": (row + shift) % count}

    def greet(device):
        pl.semaphore_signal(barrier, inc=1, device_id=device, device_id_type=MESH_ID)

    for shift in range(1, group):
        greet(in_group(shift))
    for shift in range(1, count):
        greet(in_column(shift))
    pl.semaphore_wait(barrier, group + count - 2)

    def exchange(shift, slot, source, target, device):
        return pltpu.make_async_remote_copy(
            src_ref=source,
            dst_ref=target,
            send_sem=sems.at[0, slot],
            recv_sem=sems.at[1, slot],
            device_id=device,
            device_id_type=MESH_ID,
        )

    moves = [
        exchange(s, s - 1, parts_ref.at[(col + s) % group], first.at[s - 1], in_group(s))
        for s in range(1, group)
    ]
    for move in moves:
        move.start()
    total = parts_ref[col]
    for shift, move in enumerate(moves):
        move.wait()
        total = total + first[shift]
    sums[...] = total
    moves = [
        exchange(
            s, group + s - 2, sums.at[(row + s) % count], second.at[s - 1], in_column(s)
        )
        for s in range(1, count)
    ]
    for move in moves:
        move.start()
    total = sums[row]
    for shift, move in enumerate(moves):
        move.wait()
        total = total + second[shift]
    out_ref[...] = total


def sum_shares(first, second, count, group, collective_id):
    share = first.shape[0] // (count * group)
    pair = jnp.stack([first, second]).reshape(2, count, group, share)
    parts = jnp.transpose(pair, (2, 1, 0, 3)).reshape(group, count, 1, 2 * share)
    width = (2 * share + 127) // 128 * 128
    parts = jnp.pad(parts, ((0, 0), (0, 0), (0, 7), (0, width - 2 * share)))
    tile = (8, width)
    out = pl.pallas_call(
        functools.partial(share_kernel, count, group),
        out_shape=jax.ShapeDtypeStruct(tile, F32),
        in_specs=[pl.BlockSpec(memory_space=pltpu.VMEM)],
        out_specs=pl.BlockSpec(memory_space=pltpu.VMEM),
        scratch_shapes=[
            pltpu.VMEM((group - 1, count) + tile, F32),
            pltpu.VMEM((count,) + tile, F32),
            pltpu.VMEM((count - 1,) + tile, F32),
            pltpu.SemaphoreType.DMA((2, group + count - 2)),
        ],
        compiler_params=pltpu.CompilerParams(collective_id=collective_id, has_side_effects=True),
        name="sum_shares",
    )(parts)
    return out[0, :share], out[0, share : 2 * share]


def dot(left, right):
    return jnp.dot(left, right, preferred_element_type=F32)


def body(
    count,
    group,
    tokens,
    lengths,
    attn_gain,
    w_query,
    w_key,
    w_value,
    w_output,
    mlp_gain,
    w_gate,
    w_up,
    w_down,
    cotangent,
):
    local_rows = tokens.shape[0]
    token_full = tokens.astype(F32)
    gain_attn = attn_gain.astype(F32)
    gain_mlp = mlp_gain.astype(F32)
    row_pos = lax.axis_index("tensor") * local_rows + jnp.arange(local_rows)
    valid_rows = (row_pos < lengths[0]).astype(F32)
    cot_masked = cotangent.astype(F32) * valid_rows[:, None]
    cosine, sine = rope_tables()

    inv_first = lax.rsqrt(jnp.mean(token_full * token_full, axis=1, keepdims=True) + epsilon)
    normed_attn = (token_full * inv_first * gain_attn).astype(BF16)
    rows_attn = gather_rows(normed_attn)
    query_all, key_all, value_all, output_all = ring_gather(
        [after(w_query, normed_attn), w_key, w_value, w_output],
        (0, 0, 0, 1), (1, 1, 1, 1), count, 0,
    )
    grad_branch = gather_rows(after(cot_masked.astype(BF16), rows_attn))
    queries, keys, values = project(rows_attn, query_all, key_all, value_all, cosine, sine)
    head_out = attend(queries, keys, values, lengths)
    attn_part = dot(head_out, output_all).astype(BF16)
    attn_branch = scatter_rows(attn_part)
    (gate_all,) = ring_gather([after(w_gate, attn_part)], (0,), (2,), count, 1)
    hidden = token_full + attn_branch
    inv_second = lax.rsqrt(jnp.mean(hidden * hidden, axis=1, keepdims=True) + epsilon)
    normed_mlp = (hidden * inv_second * gain_mlp).astype(BF16)
    normed_mlp = after(normed_mlp, gate_all)
    rows_mlp = gather_rows(normed_mlp)
    (up_all,) = ring_gather([after(w_up, normed_mlp)], (0,), (2,), count, 2)
    gate_proj = dot(rows_mlp, after(gate_all, up_all))
    up_proj = dot(rows_mlp, up_all)
    gate_sig = jax.nn.sigmoid(gate_proj)
    activated = (gate_proj * gate_sig * up_proj).astype(BF16)
    (down_all,) = ring_gather([after(w_down, up_all)], (1,), (2,), count, 3)
    mlp_part = dot(activated, down_all).astype(BF16)
    mlp_branch = scatter_rows(mlp_part)
    layer_out = (hidden + mlp_branch).astype(BF16)

    grad_act = nt_dot(grad_branch, after(down_all, mlp_part))
    grad_gate_pre = (grad_act * up_proj * gate_sig * (1.0 + gate_proj * (1.0 - gate_sig))).astype(
        BF16
    )
    grad_up_pre = (grad_act * gate_proj * gate_sig).astype(BF16)
    norm_part = (nt_dot(grad_gate_pre, gate_all) + nt_dot(grad_up_pre, up_all)).astype(BF16)
    down_part = tn_dot(activated, after(grad_branch, norm_part)).astype(BF16)
    grad_norm_two = scatter_rows(after(norm_part, mlp_branch))
    (grad_down,) = ring_scatter([down_part], (1,), (2,), count, 4)
    scaled_two = grad_norm_two * gain_mlp
    gain_two_part = jnp.sum(grad_norm_two * hidden * inv_second, axis=0)
    grad_hidden = (
        cot_masked
        + inv_second * scaled_two
        - hidden * inv_second**3 * jnp.mean(scaled_two * hidden, axis=1, keepdims=True)
    )
    grad_hidden = after(grad_hidden, grad_down)
    grad_attn = gather_rows(grad_hidden.astype(BF16))
    gate_part = tn_dot(rows_mlp, after(grad_gate_pre, grad_hidden)).astype(BF16)
    up_part = tn_dot(rows_mlp, after(grad_up_pre, gate_part)).astype(BF16)
    grad_heads = nt_dot(after(grad_attn, up_part), output_all).astype(BF16)
    grad_qpre, grad_kpre, grad_vpre = attend_back(
        queries, keys, values, grad_heads, lengths, cosine, sine
    )
    token_part = (
        nt_dot(grad_qpre, query_all) + nt_dot(grad_kpre, key_all) + nt_dot(grad_vpre, value_all)
    ).astype(BF16)
    grad_norm_one = scatter_rows(token_part)
    (grad_gate,) = ring_scatter([after(gate_part, token_part)], (0,), (2,), count, 5)
    output_part = tn_dot(head_out, grad_attn).astype(BF16)
    query_part = tn_dot(rows_attn, grad_qpre).astype(BF16)
    key_part = tn_dot(rows_attn, grad_kpre).astype(BF16)
    value_part = tn_dot(rows_attn, grad_vpre).astype(BF16)
    (grad_up,) = ring_scatter([after(up_part, grad_gate)], (0,), (2,), count, 6)
    scaled_one = grad_norm_one * gain_attn
    gain_one_part = jnp.sum(grad_norm_one * token_full * inv_first, axis=0)
    grad_tokens = (
        grad_hidden
        + inv_first * scaled_one
        - token_full * inv_first**3 * jnp.mean(scaled_one * token_full, axis=1, keepdims=True)
    )
    grad_attn_gain, grad_mlp_gain = sum_shares(gain_one_part, gain_two_part, count, group, 8)
    grad_query, grad_key, grad_value, grad_output = ring_scatter(
        [after(query_part, grad_up, grad_attn_gain), key_part, value_part, output_part],
        (0, 0, 0, 1), (1, 1, 1, 1), count, 7,
    )
    return (
        layer_out,
        grad_tokens,
        grad_query,
        grad_key,
        grad_value,
        grad_output,
        grad_gate,
        grad_up,
        grad_down,
        grad_attn_gain,
        grad_mlp_gain,
    )


def solution(mesh):
    rows = P(("dp", "tensor"), None)
    tall = P("dp", "tensor")
    wide = P("tensor", "dp")
    share = P(("dp", "tensor"))
    in_specs = (rows, P("dp"), P(), tall, tall, tall, wide, P(), tall, tall, wide, rows)
    out_specs = (rows, rows, tall, tall, tall, wide, tall, tall, wide, share, share)
    return jax.shard_map(
        functools.partial(body, mesh.shape["dp"], mesh.shape["tensor"]),
        mesh=mesh,
        in_specs=in_specs,
        out_specs=out_specs,
        check_vma=False,
    )
```

time: 2300 us -> 897 us (0.39)
  waiting for transfers between devices: 1770 us -> 8.37 us
  Pallas kernels: 0 us -> 661 us
  matrix products: 271 us -> 154 us
  blocking collectives: 105 us -> 0 us
  local copies, waits for them, and re-layouts: 62 us -> 21.6 us
  other arithmetic: 64.5 us -> 26 us
    reduce_scatter x11 -> x4, waiting for transfers between devices: 1290 us -> 0.06 us  [scatter_rows(): lax.psum_scatter(value.astype(BF16), 'tensor', scatter_dimension=0, tiled...]
    pallas_call x0 -> x12, Pallas kernels: none -> 661 us  [the longest x4 303 us: ring_scatter(): pl.pallas_call(functools.partial(scatter_kernel, count, items), out_shape...]
    all_gather x9 -> x4, waiting for transfers between devices: 471 us -> 7.67 us  [gather_rows(): return lax.all_gather(value, 'tensor', axis=0, tiled=True)]
    dot_general x35 -> x18, matrix products: 271 us -> 154 us  [the longest x7 59 us: nt_dot(): lax.dot_general(left, right, (((1,), (1,)), ((), ())), preferred_element_...]
    all_gather x2 -> x0, blocking collectives: 65 us -> none  [the longest x1 33.1 us: gather_attention(): lax.all_gather(w_key, 'dp', axis=0, tiled=True)]
    dynamic_update_slice x4 -> x0, local copies, waits for them, and re-layouts: 41.4 us -> none  [attend(): results, logsum = lax.map(one_block, jnp.arange(blocks, dtype=jnp.int32))]
    unnamed x1 -> x0, blocking collectives: 39.9 us -> none
    convert_element_type x15 -> x7, other arithmetic: 33 us -> 8.1 us  [the longest x1 2.58 us: body(): normed_mlp = (hidden * inv_second * gain_mlp).astype(BF16)]
  transfers between devices with their start and end apart: 20 -> 8, of which waited for: 19 -> 1; matrix products, arithmetic and copies ran while one was open for 8% -> 11% of each run, Pallas kernels for 0% -> 61%
where the time goes in v1:
time: 897 us; the launch traced here: 888 us
  Pallas kernels  661 us (74%)
  matrix products  154 us (17%)
  other arithmetic  26 us (3%)
  local copies, waits for them, and re-layouts  21.6 us (2%)
  between operations  16 us (2%)
    pallas_call x4, Pallas kernels, ring_scatter(): pl.pallas_call(functools.partial(scatter_kernel, count, items), out_shape...  303 us
    pallas_call x4, Pallas kernels, ring_gather(): pl.pallas_call(functools.partial(gather_kernel, count, items), out_shape=...  298 us
    dot_general x7, matrix products, nt_dot(): lax.dot_general(left, right, (((1,), (1,)), ((), ())), preferred_element_...  59 us
    dot_general x7, matrix products, tn_dot(): lax.dot_general(left, right, (((0,), (0,)), ((), ())), preferred_element_...  50.5 us
    dot_general x4, matrix products, dot(): return jnp.dot(left, right, preferred_element_type=F32)  45 us
    pallas_call x1, Pallas kernels, attend_back(): pl.pallas_call(attend_back_kernel, grid=(pairs,), out_shape=[jax.ShapeDty...  27.9 us
    unnamed x123, local copies, waits for them, and re-layouts  19.3 us
  transfers between devices with their start and end apart: 8, of which 1 were waited for; matrix products, arithmetic and copies ran while one was open for 11% of the time, Pallas kernels for 61%

profile of v1, /device:TPU:0, one launch (start us, length us, event | category | flops | bytes accessed | tf_op | source)
XLA Modules:
  0.0 888.3 jit_solution(13414513959429411457)
XLA Ops:
  7.2 1.5 fusion.10
  8.7 0.6 multiply_multiply_fusion
  9.3 0.7 convert_element_type.94
  10.0 0.6 copy-done.37
  10.6 2.5 fusion.12
  13.9 55.7 %ring_gather_0.1 = (bf16[2048,512]{1,0:T(8,128)(2,1)}, bf16[2048,128]{1,0:T(8,128)(2,1)}, bf16[2048,128]{1,0:T(8,128)(2,1)}, bf16[512,2048]{1,0:T(8,128)(2,1)}) custom-call(bf16[256,512]{1,0:T(8,128)(2,1)} %refs_0_, bf16[256,128]{1,0:T(8,128)(2,1)} %refs_1_.1, bf16[256,128]{1,0:T(8,128)(2,1)} %refs_2_.1, bf16[512,256]{1,0:T(8,128)(2,1)} %refs_3_.1), custom_call_target="tpu_custom_call" | custom-call | bytes 91750400 | tf_op jit(solution)/shard_map/ring_gather_0/pallas_call | solution.py:347
  69.6 2.0 fusion.20
  71.6 0.9 pad_maximum_fusion
  72.5 2.5 copy-done.15
  75.0 1.6 copy-done.17
  76.6 5.0 project.1
  81.7 17.4 %attend.1 = bf16[1024,512]{1,0:T(8,128)(2,1)S(1)} custom-call(s32[1]{0:T(128)} %copy.31.length_ref, bf16[1024,512]{1,0:T(8,128)(2,1)S(1)} %get-tuple-element.46.q_ref, bf16[1024,128]{1,0:T(8,128)(2,1)S(1)} %get-tuple-element.47.k_ref, bf16[1024,128]{1,0:T(8,128)(2,1)S(1)} %get-tuple-element.48.v_ref), custom_call_target="tpu_custom_call" | custom-call | flops 12884901888 | bytes 4194304 | tf_op jit(solution)/shard_map/attend/pallas_call | solution.py:136
  99.1 1.0 copy-done.21
  100.1 4.4 convolution_convert_fusion.4
  104.6 0.6 copy-done.49
  105.2 82.2 %ring_gather_1.1 = bf16[2048,2048]{1,0:T(8,128)(2,1)} custom-call(bf16[256,2048]{1,0:T(8,128)(2,1)} %refs_0_.1), custom_call_target="tpu_custom_call" | custom-call | bytes 146800640 | tf_op jit(solution)/shard_map/ring_gather_1/pallas_call | solution.py:347
  187.5 1.7 multiply_reduce_fusion
  189.2 0.6 multiply_multiply_fusion.1
  190.3 2.6 multiply_convert_fusion.3
  193.7 1.2 fusion.17
  195.0 80.3 %ring_gather_2.1 = bf16[2048,2048]{1,0:T(8,128)(2,1)} custom-call(bf16[256,2048]{1,0:T(8,128)(2,1)} %refs_0_.2), custom_call_target="tpu_custom_call" | custom-call | bytes 146800640 | tf_op jit(solution)/shard_map/ring_gather_2/pallas_call | solution.py:347
  275.3 79.4 %ring_gather_3.1 = bf16[2048,2048]{1,0:T(8,128)(2,1)} custom-call(bf16[2048,256]{1,0:T(8,128)(2,1)} %refs_0_.3), custom_call_target="tpu_custom_call" | custom-call | bytes 146800640 | tf_op jit(solution)/shard_map/ring_gather_3/pallas_call | solution.py:347
  354.8 14.7 %fusion.21 = f32[1024,2048]{1,0:T(8,128)} fusion(bf16[1024,2048]{1,0:T(8,128)(2,1)} %all-gather.7.cloned.1.call-done, bf16[2048,2048]{1,0:T(8,128)(2,1)} %ring_gather_1.1), kind=kOutput, calls=%fused_computation.65 | convolution fusion | flops 8589934592 | bytes 20971520 | tf_op jit(solution)/shard_map/dot_general | solution.py:593
  369.5 13.8 %multiply_convert_fusion.2 = (bf16[1024,2048]{1,0:T(8,128)(2,1)}, f32[1024,2048]{1,0:T(8,128)}) fusion(f32[1024,2048]{1,0:T(8,128)} %fusion.21, bf16[1024,2048]{1,0:T(8,128)(2,1)S(1)} %copy-done.50, bf16[2048,2048]{1,0:T(8,128)(2,1)S(1)} %copy-done.34), kind=kOutput, calls=%fused_computation.4 | convolution fusion | flops 8602517504 | bytes 33554432 | tf_op jit(solution)/shard_map/dot_general | solution.py:593
  383.3 12.1 %convolution_convert_fusion.3 = bf16[1024,2048]{1,0:T(8,128)(2,1)} fusion(bf16[1024,2048]{1,0:T(8,128)(2,1)} %get-tuple-element.90, bf16[2048,2048]{1,0:T(8,128)(2,1)S(1)} %bitcast.45), kind=kOutput, calls=%fused_computation.15 | convolution fusion | flops 8592031744 | bytes 16777216 | tf_op jit(solution)/shard_map/dot_general | solution.py:593
  395.4 19.8 %multiply_convert_fusion = (bf16[1024,2048]{1,0:T(8,128)(2,1)S(1)}, bf16[1024,2048]{1,0:T(8,128)(2,1)}) fusion(f32[1024,2048]{1,0:T(8,128)} %fusion.21, f32[1024,2048]{1,0:T(8,128)} %get-tuple-element.91, bf16[1024,2048]{1,0:T(8,128)(2,1)} %all-gather.9.cloned.1.call-done, bf16[2048,2048]{1,0:T(8,128)(2,1)} %ring_gather_3.1), kind=kOutput, calls=%fused_computation.2 | convolution fusion | flops 8617197568 | bytes 37748736 | tf_op jit(solution)/shard_map/dot_general | solution.py:51
  415.2 14.1 %fusion.22 = f32[1024,2048]{1,0:T(8,128)S(1)} fusion(bf16[1024,2048]{1,0:T(8,128)(2,1)} %get-tuple-element.60, bf16[2048,2048]{1,0:T(8,128)(2,1)} %ring_gather_1.1), kind=kOutput, calls=%fused_computation.66 | convolution fusion | flops 8589934592 | bytes 20971520 | tf_op jit(solution)/shard_map/dot_general | solution.py:51
  429.3 12.9 %add_convert_fusion.1 = bf16[1024,2048]{1,0:T(8,128)(2,1)} fusion(f32[1024,2048]{1,0:T(8,128)S(1)} %fusion.22, bf16[1024,2048]{1,0:T(8,128)(2,1)S(1)} %get-tuple-element.61, bf16[2048,2048]{1,0:T(8,128)(2,1)} %ring_gather_2.1), kind=kOutput, calls=%fused_computation.1 | convolution fusion | flops 8594128896 | bytes 25165824 | tf_op jit(solution)/shard_map/dot_general | solution.py:51
  442.8 14.5 %convolution_convert_fusion.2.refs_0_ = bf16[2048,2048]{1,0:T(8,128)(2,1)} fusion(bf16[1024,2048]{1,0:T(8,128)(2,1)} %get-tuple-element.90, bf16[1024,2048]{1,0:T(8,128)(2,1)} %all-gather.9.cloned.1.call-done), kind=kOutput, calls=%fused_computation.8 | convolution fusion | flops 8594128896 | bytes 16777216 | tf_op jit(solution)/shard_map/dot_general | solution.py:55
  457.3 79.0 %ring_scatter_4.1 = f32[2048,256]{1,0:T(8,128)S(1)} custom-call(bf16[2048,2048]{1,0:T(8,128)(2,1)} %convolution_convert_fusion.2.refs_0_), custom_call_target="tpu_custom_call" | custom-call | bytes 167772160 | tf_op jit(solution)/shard_map/ring_scatter_4/pallas_call | solution.py:477
  536.5 2.3 fusion.9
  538.8 4.2 fusion.6
  542.9 1.3 copy-done.32
  544.3 1.1 convert_element_type.112
  545.5 14.6 %convolution_convert_fusion.1.refs_0_ = bf16[2048,2048]{1,0:T(8,128)(2,1)} fusion(bf16[1024,2048]{1,0:T(8,128)(2,1)} %all-gather.7.cloned.1.call-done, bf16[1024,2048]{1,0:T(8,128)(2,1)} %get-tuple-element.60), kind=kOutput, calls=%fused_computation.7 | convolution fusion | flops 8594128896 | bytes 16777216 | tf_op jit(solution)/shard_map/dot_general | solution.py:55
  560.1 11.4 %convolution_convert_fusion.refs_0_ = bf16[2048,2048]{1,0:T(8,128)(2,1)} fusion(bf16[1024,2048]{1,0:T(8,128)(2,1)S(1)} %copy-done.51, bf16[1024,2048]{1,0:T(8,128)(2,1)S(1)} %copy-done.55), kind=kOutput, calls=%fused_computation.6 | convolution fusion | flops 8594128896 | bytes 16777216 | tf_op jit(solution)/shard_map/dot_general | solution.py:55
  571.5 7.6 all-gather.11.cloned.1.call-done
  579.2 5.3 convolution_convert_fusion.9.g_ref
  584.6 27.9 %attend_back.1 = (bf16[1024,512]{1,0:T(8,128)(2,1)S(1)}, bf16[1024,128]{1,0:T(8,128)(2,1)S(1)}, bf16[1024,128]{1,0:T(8,128)(2,1)S(1)}) custom-call(s32[1]{0:T(128)} %copy.31.length_ref, bf16[1024,512]{1,0:T(8,128)(2,1)S(1)} %copy-done.24, bf16[1024,128]{1,0:T(8,128)(2,1)S(1)} %copy-done.26, bf16[1024,128]{1,0:T(8,128)(2,1)S(1)} %copy-done.28, ...), custom_call_target="tpu_custom_call" | custom-call | flops 25769803776 | bytes 8388608 | tf_op jit(solution)/shard_map/attend_back/pallas_call | solution.py:201
  612.5 2.4 fusion.23
  614.9 1.3 fusion.24
  616.2 3.2 add_convert_fusion
  619.5 83.8 %ring_scatter_5.1 = f32[256,2048]{1,0:T(8,128)S(1)} custom-call(bf16[2048,2048]{1,0:T(8,128)(2,1)} %convolution_convert_fusion.1.refs_0_), custom_call_target="tpu_custom_call" | custom-call | bytes 167772160 | tf_op jit(solution)/shard_map/ring_scatter_5/pallas_call | solution.py:477
  703.3 1.3 copy-done
  704.6 82.8 %ring_scatter_6.1 = f32[256,2048]{1,0:T(8,128)S(1)} custom-call(bf16[2048,2048]{1,0:T(8,128)(2,1)} %convolution_convert_fusion.refs_0_), custom_call_target="tpu_custom_call" | custom-call | bytes 167772160 | tf_op jit(solution)/shard_map/ring_scatter_6/pallas_call | solution.py:477
  787.5 1.3 convolution_convert_fusion.8.refs_1_
  788.8 1.3 convolution_convert_fusion.7.refs_2_
  790.2 0.6 copy-done.52
  790.8 3.7 convolution_convert_fusion.5.refs_3_
  794.5 3.7 convolution_convert_fusion.6.refs_0_
  798.2 2.2 fusion.16
  800.7 0.7 pad.4.parts_ref
  801.3 10.5 %sum_shares.1 = f32[8,128]{1,0:T(8,128)} custom-call(f32[4,8,8,128]{3,2,1,0:T(8,128)} %pad.4.parts_ref), custom_call_target="tpu_custom_call" | custom-call | tf_op jit(solution)/shard_map/sum_shares/pallas_call | solution.py:575
  811.8 1.3 slice_bitcast_fusion
  813.1 1.6 copy-done.4
  814.7 57.4 %ring_scatter_7.1 = (f32[256,512]{1,0:T(8,128)S(1)}, f32[256,128]{1,0:T(8,128)S(1)}, f32[256,128]{1,0:T(8,128)S(1)}, f32[512,256]{1,0:T(8,128)S(1)}) custom-call(bf16[2048,512]{1,0:T(8,128)(2,1)S(1)} %copy-done.4, bf16[2048,128]{1,0:T(8,128)(2,1)S(1)} %convolution_convert_fusion.8.refs_1_, bf16[2048,128]{1,0:T(8,128)(2,1)S(1)} %convolution_convert_fusion.7.refs_2_, ...), custom_call_target="tpu_custom_call" | custom-call | bytes 104857600 | tf_op jit(solution)/shard_map/ring_scatter_7/pallas_call | solution.py:477
  872.2 1.9 fusion.4
  874.1 0.8 copy.32
  874.9 0.7 copy.33
  875.6 0.7 copy.34
  876.2 0.8 copy.35
  877.0 1.3 copy.36
  878.4 1.3 copy.37
  879.7 1.3 copy.38
  (141 shorter events, 2.9 us)
Async XLA Ops:
  7.2 65.3 %all-gather.5.cloned.1.call-start = ((), (), s32[]{:S(2)}) async-start(), calls=%async_computation.4 | async-start | bytes 5242880 | tf_op jit(solution)/shard_map/all_gather | solution.py:504
  9.3 0.7 copy-start.41
  10.0 0.6 copy-start.37
  13.2 174.3 %reduce-scatter.5.cloned.1.call-start = ((), (), s32[]{:S(2)}) async-start(), calls=%async_computation.5 | async-start | bytes 5242880 | tf_op jit(solution)/shard_map/reduce_scatter | solution.py:508
  69.5 3.0 copy-start.5
  69.6 3.0 copy-start.7
  72.4 9.2 %copy-start.9 = (f32[1024,128]{1,0:T(8,128)}, f32[1024,128]{1,0:T(8,128)S(1)}, u32[]{:S(2)}) copy-start(f32[1024,128]{1,0:T(8,128)S(1)} %get-tuple-element.92.cos_ref) | copy-start | bytes 1572868
  72.5 9.2 %copy-start.11 = (f32[1024,128]{1,0:T(8,128)}, f32[1024,128]{1,0:T(8,128)S(1)}, u32[]{:S(2)}) copy-start(f32[1024,128]{1,0:T(8,128)S(1)} %get-tuple-element.93.sin_ref) | copy-start | bytes 1572868
  72.5 2.5 copy-start.15
  75.0 1.6 copy-start.17
  81.7 17.4 %copy-start.23 = (bf16[1024,512]{1,0:T(8,128)(2,1)}, bf16[1024,512]{1,0:T(8,128)(2,1)S(1)}, u32[]{:S(2)}) copy-start(bf16[1024,512]{1,0:T(8,128)(2,1)S(1)} %get-tuple-element.46.q_ref) | copy-start | bytes 3145732
  81.7 17.4 %copy-start.25 = (bf16[1024,128]{1,0:T(8,128)(2,1)}, bf16[1024,128]{1,0:T(8,128)(2,1)S(1)}, u32[]{:S(2)}) copy-start(bf16[1024,128]{1,0:T(8,128)(2,1)S(1)} %get-tuple-element.47.k_ref) | copy-start | bytes 786436
  81.7 17.4 %copy-start.27 = (bf16[1024,128]{1,0:T(8,128)(2,1)}, bf16[1024,128]{1,0:T(8,128)(2,1)S(1)}, u32[]{:S(2)}) copy-start(bf16[1024,128]{1,0:T(8,128)(2,1)S(1)} %get-tuple-element.48.v_ref) | copy-start | bytes 786436
  81.7 18.4 %copy-start.53 = (bf16[512,2048]{1,0:T(8,128)(2,1)S(1)}, bf16[512,2048]{1,0:T(8,128)(2,1)}, u32[]{:S(2)}) copy-start(bf16[512,2048]{1,0:T(8,128)(2,1)} %get-tuple-element.49) | copy-start | bytes 6291460
  99.1 1.0 copy-start.21
  104.5 0.7 copy-start.49
  104.5 250.2 %all-gather.7.cloned.1.call-start = ((), (), s32[]{:S(2)}) async-start(), calls=%async_computation.6 | async-start | bytes 5242880 | tf_op jit(solution)/shard_map/all_gather | solution.py:504
  105.2 84.6 %copy-start.39 = (f32[2048]{0:T(1024)}, f32[2048]{0:T(1024)S(1)}, u32[]{:S(2)}) copy-start(f32[2048]{0:T(1024)S(1)} %convert_element_type.98) | copy-start | bytes 24580
  105.2 82.2 %copy-start.29 = (bf16[256,2048]{1,0:T(8,128)(2,1)S(1)}, bf16[256,2048]{1,0:T(8,128)(2,1)}, u32[]{:S(2)}) copy-start(bf16[256,2048]{1,0:T(8,128)(2,1)} %param.12) | copy-start | bytes 3145732
  187.4 6.3 copy-start.36
  192.9 202.5 %all-gather.9.cloned.1.call-start = ((), (), s32[]{:S(2)}) async-start(), calls=%async_computation.8 | async-start | bytes 5242880 | tf_op jit(solution)/shard_map/all_gather | solution.py:504
  194.9 341.5 %reduce-scatter.9.cloned.1.call-start = ((), (), s32[]{:S(2)}) async-start(), calls=%async_computation.9 | async-start | bytes 5242880 | tf_op jit(solution)/shard_map/reduce_scatter | solution.py:508
  354.8 14.7 %copy-start.34 = (bf16[2048,2048]{1,0:T(8,128)(2,1)S(1)}, bf16[2048,2048]{1,0:T(8,128)(2,1)}, u32[]{:S(2)}) copy-start(bf16[2048,2048]{1,0:T(8,128)(2,1)} %ring_gather_2.1) | copy-start | bytes 25165828
  354.8 14.7 %copy-start.50 = (bf16[1024,2048]{1,0:T(8,128)(2,1)S(1)}, bf16[1024,2048]{1,0:T(8,128)(2,1)}, u32[]{:S(2)}) copy-start(bf16[1024,2048]{1,0:T(8,128)(2,1)} %all-gather.7.cloned.1.call-done) | copy-start | bytes 12582916
  354.8 28.5 %slice-start = ((s8[8388608]{0:T(1024)(128)(4,1)}), s8[4194304]{0:T(1024)(128)(4,1)S(1)}, s32[]{:S(2)}) async-start(s8[8388608]{0:T(1024)(128)(4,1)} %bitcast.44), calls=%async_computation.12 | async-start | bytes 8388608
  369.5 13.8 %slice-start.1 = ((s8[8388608]{0:T(1024)(128)(4,1)}), s8[4194304]{0:T(1024)(128)(4,1)S(1)}, s32[]{:S(2)}) async-start(s8[8388608]{0:T(1024)(128)(4,1)} %bitcast.44), calls=%async_computation.13 | async-start | bytes 8388608
  415.2 14.1 %copy-start.54 = (bf16[1024,2048]{1,0:T(8,128)(2,1)}, bf16[1024,2048]{1,0:T(8,128)(2,1)S(1)}, u32[]{:S(2)}) copy-start(bf16[1024,2048]{1,0:T(8,128)(2,1)S(1)} %get-tuple-element.61) | copy-start | bytes 12582916
  442.2 96.5 %reduce-scatter.7.cloned.1.call-start = ((), (), s32[]{:S(2)}) async-start(), calls=%async_computation.7 | async-start | bytes 5242880 | tf_op jit(solution)/shard_map/reduce_scatter | solution.py:508
  442.8 136.4 %all-gather.11.cloned.1.call-start = ((), (), s32[]{:S(2)}) async-start(), calls=%async_computation.10 | async-start | bytes 5242880 | tf_op jit(solution)/shard_map/all_gather | solution.py:504
  457.3 79.1 %copy-start.30 = (bf16[256,2048]{1,0:T(8,128)(2,1)S(1)}, bf16[256,2048]{1,0:T(8,128)(2,1)}, u32[]{:S(2)}) copy-start(bf16[256,2048]{1,0:T(8,128)(2,1)} %param.12) | copy-start | bytes 3145732
  457.3 79.1 %copy-start.40 = (f32[2048]{0:T(1024)S(1)}, f32[2048]{0:T(1024)}, u32[]{:S(2)}) copy-start(f32[2048]{0:T(1024)} %copy-done.39) | copy-start | bytes 24580
  457.3 79.1 %copy-start.44 = (f32[256]{0:T(256)S(1)}, f32[256]{0:T(256)}, u32[]{:S(2)}) copy-start(f32[256]{0:T(256)} %copy-done.43) | copy-start | bytes 3076
  457.3 81.4 %copy-start.46 = (f32[256]{0:T(256)S(1)}, f32[256]{0:T(256)}, u32[]{:S(2)}) copy-start(f32[256]{0:T(256)} %copy-done.45) | copy-start | bytes 3076
  457.3 81.4 %copy-start.48 = (f32[256]{0:T(256)S(1)}, f32[256]{0:T(256)}, u32[]{:S(2)}) copy-start(f32[256]{0:T(256)} %get-tuple-element.85) | copy-start | bytes 3076
  542.9 1.3 copy-start.32
  545.4 252.8 %reduce-scatter.11.cloned.1.call-start = ((), (), s32[]{:S(2)}) async-start(), calls=%async_computation.11 | async-start | bytes 5242880 | tf_op jit(solution)/shard_map/reduce_scatter | solution.py:508
  545.4 14.6 %copy-start.51 = (bf16[1024,2048]{1,0:T(8,128)(2,1)S(1)}, bf16[1024,2048]{1,0:T(8,128)(2,1)}, u32[]{:S(2)}) copy-start(bf16[1024,2048]{1,0:T(8,128)(2,1)} %all-gather.7.cloned.1.call-done) | copy-start | bytes 12582916
  545.5 14.6 %copy-start.55 = (bf16[1024,2048]{1,0:T(8,128)(2,1)S(1)}, bf16[1024,2048]{1,0:T(8,128)(2,1)}, u32[]{:S(2)}) copy-start(bf16[1024,2048]{1,0:T(8,128)(2,1)} %copy-done.54) | copy-start | bytes 12582916
  571.5 13.0 %copy-start.10 = (f32[1024,128]{1,0:T(8,128)S(1)}, f32[1024,128]{1,0:T(8,128)}, u32[]{:S(2)}) copy-start(f32[1024,128]{1,0:T(8,128)} %copy-done.9) | copy-start | bytes 1572868
  571.5 13.0 %copy-start.12 = (f32[1024,128]{1,0:T(8,128)S(1)}, f32[1024,128]{1,0:T(8,128)}, u32[]{:S(2)}) copy-start(f32[1024,128]{1,0:T(8,128)} %copy-done.11) | copy-start | bytes 1572868
  579.2 5.4 copy-start.24
  579.2 5.4 copy-start.26
  579.2 5.4 copy-start.28
  584.5 27.9 %copy-start.18 = (bf16[2048,512]{1,0:T(8,128)(2,1)S(1)}, bf16[2048,512]{1,0:T(8,128)(2,1)}, u32[]{:S(2)}) copy-start(bf16[2048,512]{1,0:T(8,128)(2,1)} %get-tuple-element.43.wq_ref) | copy-start | bytes 6291460
  612.4 2.4 copy-start.19
  612.5 3.7 copy-start.13
  612.5 2.4 copy-start.8
  614.9 1.3 copy-start.6
  703.3 1.3 copy-start
  704.6 82.8 %copy-start.16 = (bf16[1024,2048]{1,0:T(8,128)(2,1)S(1)}, bf16[1024,2048]{1,0:T(8,128)(2,1)}, u32[]{:S(2)}) copy-start(bf16[1024,2048]{1,0:T(8,128)(2,1)} %all-gather.5.cloned.1.call-done.x_ref) | copy-start | bytes 12582916
  787.5 2.7 copy-start.2
  787.5 1.4 copy-start.14
  787.5 2.7 copy-start.22
  787.5 3.3 copy-start.52
  790.8 3.7 copy-start.20
  794.5 3.7 copy-start.38
  794.5 3.7 copy-start.42
  798.2 73.9 %copy-start.47 = (f32[256]{0:T(256)S(1)}, f32[256]{0:T(256)}, u32[]{:S(2)}) copy-start(f32[256]{0:T(256)} %get-tuple-element.83) | copy-start | bytes 3076
  813.1 1.6 copy-start.4
  814.7 57.4 %copy-start.31 = (bf16[256,2048]{1,0:T(8,128)(2,1)S(1)}, bf16[256,2048]{1,0:T(8,128)(2,1)}, u32[]{:S(2)}) copy-start(bf16[256,2048]{1,0:T(8,128)(2,1)} %param.12) | copy-start | bytes 3145732
  814.7 57.4 %copy-start.33 = (f32[256,2048]{1,0:T(8,128)S(1)}, f32[256,2048]{1,0:T(8,128)}, u32[]{:S(2)}) copy-start(f32[256,2048]{1,0:T(8,128)} %copy-done.32) | copy-start | bytes 6291460
  814.7 57.5 %copy-start.35 = (bf16[256,2048]{1,0:T(8,128)(2,1)S(1)}, bf16[256,2048]{1,0:T(8,128)(2,1)}, u32[]{:S(2)}) copy-start(bf16[256,2048]{1,0:T(8,128)(2,1)} %reduce-scatter.11.cloned.1.call-done) | copy-start | bytes 3145732
  872.2 4.8 copy-start.1
  874.1 4.2 copy-start.3
  (2 other events, 1.1 us)
Sparse Core Ops, SparseCore 0:
  13.3 37.1 all-gather.4
  104.7 44.6 reduce-scatter.4
  193.0 33.4 all-gather.6
  228.6 34.4 all-gather.8
  442.3 43.6 reduce-scatter.8
  488.4 44.5 reduce-scatter.6
  545.5 33.5 all-gather.10
  619.6 44.5 reduce-scatter.10

commit v2 on v1

--- a/solution.py
+++ b/solution.py
@@ -496,6 +496,529 @@
     )(*partials)
 
 
+def scatter_dot_kernel(count, items, parts, extra, *refs):
+    num = len(items)
+    base = 6 * num + 5
+    beside = None
+    if extra is not None:
+        builder, takes, gives = extra
+        given, refs = refs[2 * num : 2 * num + takes], refs[: 2 * num] + refs[2 * num + takes :]
+        made, refs = refs[3 * num : 3 * num + gives], refs[: 3 * num] + refs[3 * num + gives :]
+        spare, refs = refs[3 * num + base :], refs[: 3 * num + base]
+    lefts, rights, outs = refs[:num], refs[num : 2 * num], refs[2 * num : 3 * num]
+    refs = refs[3 * num :]
+    left_bufs, right_bufs = refs[:num], refs[num : 2 * num]
+    firsts, owns, helds, totals = (refs[(2 + i) * num : (3 + i) * num] for i in range(4))
+    send_sems, recv_sems, left_sems, right_sems, store_sems = refs[6 * num :]
+    entry_place = ring_place(lax.axis_index("dp"), count)
+
+    def load_right(item):
+        return pltpu.make_async_copy(rights[item], right_bufs[item], right_sems.at[item])
+
+    def load_left(step, side, item, place):
+        block, _ = items[item]
+        member = member_at(place, side, step + 1, count)
+        slot = step % 2
+        return pltpu.make_async_copy(
+            lefts[item].at[:, pl.ds(pl.multiple_of(member * block, block), block)],
+            left_bufs[item].at[side, slot],
+            left_sems.at[side, slot, item],
+        )
+
+    for item in range(num):
+        load_right(item).start()
+        for side in range(2):
+            load_left(0, side, item, entry_place).start()
+    if extra is not None:
+        beside = builder(count, given, made, spare, right_bufs)
+        beside.begin()
+    place, neighbours = ring_setup(count)
+    pairs = [(item, side) for item in range(num) for side in range(2)]
+
+    def own_sum(step, side, item):
+        _, half = items[item]
+        return tn_dot(
+            left_bufs[item][side, step % 2], right_bufs[item][:, side * half : (side + 1) * half]
+        )
+
+    def send(step, side, item, part, source):
+        return pltpu.make_async_remote_copy(
+            src_ref=source.at[part],
+            dst_ref=helds[item].at[side, step, part],
+            send_sem=send_sems.at[side, step, item * parts + part],
+            recv_sem=recv_sems.at[side, step, item * parts + part],
+            device_id={"dp": neighbours[side]},
+            device_id_type=MESH_ID,
+        )
+
+    def prefetch(step):
+        for item, side in pairs:
+            load_left(step, side, item, place).start()
+
+    prefetch(1)
+    for item in range(num):
+        load_right(item).wait()
+    for item, side in pairs:
+        load_left(0, side, item, place).wait()
+        firsts[item][side] = own_sum(0, side, item).astype(BF16).reshape(firsts[item].shape[1:])
+        for part in range(parts):
+            send(0, side, item, part, firsts[item].at[side]).start()
+    if beside:
+        beside.compute(0)
+
+    def hop(step, carry):
+        prefetch(step + 1)
+        for item, side in pairs:
+            load_left(step, side, item, place).wait()
+            owns[item][side] = own_sum(step, side, item).reshape(owns[item].shape[1:])
+        if beside:
+            beside.compute(step)
+        for part in range(parts):
+            for item, side in pairs:
+                arrived = helds[item].at[side, step - 1]
+                send(step - 1, side, item, part, arrived).wait_recv()
+                arrived[part] = (
+                    arrived[part].astype(F32) + owns[item][side, part]
+                ).astype(BF16)
+                send(step, side, item, part, arrived).start()
+        return carry
+
+    lax.fori_loop(1, count - 1, hop, 0)
+    last = count - 1
+    for item, side in pairs:
+        load_left(last, side, item, place).wait()
+        owns[item][side] = own_sum(last, side, item).reshape(owns[item].shape[1:])
+    if beside:
+        beside.compute(last)
+    stores = []
+    for part in range(parts):
+        for item, side in pairs:
+            block, half = items[item]
+            arrived = helds[item].at[side, last - 1]
+            send(last - 1, side, item, part, arrived).wait_recv()
+            totals[item][side, part] = arrived[part].astype(F32) + owns[item][side, part]
+            stores.append(
+                pltpu.make_async_copy(
+                    totals[item].at[side, part],
+                    outs[item].at[
+                        pl.ds(part * (block // parts), block // parts),
+                        pl.ds(side * half, half),
+                    ],
+                    store_sems.at[side, item * parts + part],
+                )
+            )
+            stores[-1].start()
+    for store in stores:
+        store.wait()
+    if beside:
+        beside.finish()
+
+    def drain(step, carry):
+        for part in range(parts):
+            for item, side in pairs:
+                send(step, side, item, part, helds[item].at[side, 0]).wait_send()
+        return carry
+
+    lax.fori_loop(0, count - 1, drain, 0)
+
+
+def ring_scatter_dots(jobs, parts, count, collective_id, extra=None):
+    builder, given, made, spare = extra or (None, [], [], [])
+    lefts, rights = [j[0] for j in jobs], [j[1] for j in jobs]
+    rows = lefts[0].shape[0]
+    items = tuple((l.shape[1] // count, r.shape[1] // 2) for l, r in jobs)
+    num = len(jobs)
+
+    def buffers(depth, dtype):
+        return [pltpu.VMEM(depth + (parts, b // parts, h), dtype) for b, h in items]
+
+    slots = num * parts
+    flops = sum(2 * rows * l.shape[1] * r.shape[1] for l, r in jobs)
+    nbytes = sum(2 * l.shape[1] * r.shape[1] for l, r in jobs)
+    return pl.pallas_call(
+        functools.partial(
+            scatter_dot_kernel,
+            count,
+            items,
+            parts,
+            (builder, len(given), len(made)) if extra else None,
+        ),
+        out_shape=[jax.ShapeDtypeStruct((b, 2 * h), F32) for b, h in items] + made,
+        in_specs=[pl.BlockSpec(memory_space=pl.ANY)] * (2 * num + len(given)),
+        out_specs=[pl.BlockSpec(memory_space=pl.ANY)] * (num + len(made)),
+        scratch_shapes=[pltpu.VMEM((2, 2, rows, b), BF16) for b, _ in items]
+        + [pltpu.VMEM(r.shape, BF16) for r in rights]
+        + buffers((2,), BF16)
+        + buffers((2,), F32)
+        + buffers((2, count - 1), BF16)
+        + buffers((2,), F32)
+        + [
+            pltpu.SemaphoreType.DMA((2, count - 1, slots)),
+            pltpu.SemaphoreType.DMA((2, count - 1, slots)),
+            pltpu.SemaphoreType.DMA((2, 2, num)),
+            pltpu.SemaphoreType.DMA((num,)),
+            pltpu.SemaphoreType.DMA((2, slots)),
+        ]
+        + spare,
+        compiler_params=pltpu.CompilerParams(
+            collective_id=collective_id, has_side_effects=True, vmem_limit_bytes=60 << 20
+        ),
+        cost_estimate=pl.CostEstimate(
+            flops=flops, bytes_accessed=20 * nbytes, transcendentals=0
+        ),
+        name=f"ring_scatter_{collective_id}",
+    )(*lefts, *rights, *given)
+
+
+class NormWork:
+    def __init__(self, count, given, made, spare, rights):
+        self.grads, self.weights, self.down = given[:2], given[2:4], given[4]
+        self.outs = made
+        self.grad_bufs, self.row_bufs, self.down_bufs, self.stage = spare[0], *spare[1:4]
+        self.grad_sems, self.row_sems, self.down_sems, self.out_sems = spare[4:]
+        self.act = rights[0]
+        self.count = count
+        self.block = self.row_bufs.shape[2]
+
+    def load_grad(self, which):
+        return pltpu.make_async_copy(
+            self.grads[which], self.grad_bufs.at[which], self.grad_sems.at[which]
+        )
+
+    def spot(self, step):
+        return pl.ds(pl.multiple_of(step * self.block, self.block), self.block)
+
+    def loads(self, step):
+        slot = step % 2
+        rows = [
+            pltpu.make_async_copy(
+                self.weights[which].at[self.spot(step), :],
+                self.row_bufs.at[which, slot],
+                self.row_sems.at[which, slot],
+            )
+            for which in range(2)
+        ]
+        down = pltpu.make_async_copy(
+            self.down.at[:, self.spot(step)], self.down_bufs.at[slot], self.down_sems.at[slot]
+        )
+        return rows + [down]
+
+    def store(self, which, step):
+        slot = step % 2
+        return pltpu.make_async_copy(
+            self.stage.at[which, slot],
+            self.outs[which].at[:, self.spot(step)],
+            self.out_sems.at[which, slot],
+        )
+
+    def begin(self):
+        for which in range(2):
+            self.load_grad(which).start()
+        for copy in self.loads(0):
+            copy.start()
+
+    def compute(self, step):
+        last = self.count - 1
+        if isinstance(step, int):
+            if step < last:
+                for copy in self.loads(step + 1):
+                    copy.start()
+            if step == 0:
+                for which in range(2):
+                    self.load_grad(which).wait()
+            if step >= 2:
+                for which in range(2):
+                    self.store(which, step - 2).wait()
+        else:
+            for copy in self.loads(step + 1):
+                copy.start()
+
+            @pl.when(step >= 2)
+            def _():
+                for which in range(2):
+                    self.store(which, step - 2).wait()
+
+        for copy in self.loads(step):
+            copy.wait()
+        slot = step % 2
+        for top in range(0, self.act.shape[0], 256):
+            band = pl.ds(top, 256)
+            norm = nt_dot(self.grad_bufs[0, band, :], self.row_bufs[0, slot])
+            norm += nt_dot(self.grad_bufs[1, band, :], self.row_bufs[1, slot])
+            self.stage[0, slot, band, :] = norm.astype(BF16)
+            value = jnp.dot(
+                self.act[band, :], self.down_bufs[slot], preferred_element_type=F32
+            )
+            self.stage[1, slot, band, :] = value.astype(BF16)
+        for which in range(2):
+            self.store(which, step).start()
+
+    def finish(self):
+        for step in range(max(self.count - 2, 0), self.count):
+            for which in range(2):
+                self.store(which, step).wait()
+
+
+def down_ring(grad_branch, activated, grad_gate, grad_up, gate_all, up_all, down_all, count, cid):
+    rows, hidden = activated.shape
+    width = gate_all.shape[0]
+    block = width // count
+    wide = jax.ShapeDtypeStruct((rows, width), BF16)
+    spare = [
+        pltpu.VMEM((2, rows, hidden), BF16),
+        pltpu.VMEM((2, 2, block, hidden), BF16),
+        pltpu.VMEM((2, hidden, block), BF16),
+        pltpu.VMEM((2, 2, rows, block), BF16),
+        pltpu.SemaphoreType.DMA((2,)),
+        pltpu.SemaphoreType.DMA((2, 2)),
+        pltpu.SemaphoreType.DMA((2,)),
+        pltpu.SemaphoreType.DMA((2, 2)),
+    ]
+    given = [grad_gate, grad_up, gate_all, up_all, down_all]
+    return ring_scatter_dots(
+        [(grad_branch, activated)], 2, count, cid, (NormWork, given, [wide, wide], spare)
+    )
+
+
+def mlp_kernel(count, *refs):
+    x_hbm, wg_hbm, wu_hbm, shard, gb_hbm = refs[:5]
+    act_hbm, gg_hbm, gu_hbm, down_all = refs[5:9]
+    x_buf, gb_buf, w_bufs, gate_slope, up_slope, acc, half_bufs, stage, own_stage = refs[9:18]
+    send_sems, recv_sems, w_sems, in_sems, half_sems, out_sems, local_sem = refs[18:]
+    rows, width = x_buf.shape
+    hidden = acc.shape[1]
+    block = width // count
+    cols = w_bufs.shape[-1]
+    steps = hidden // cols
+    half = hidden // 2
+    parts = send_sems.shape[2]
+    me = lax.axis_index("dp")
+
+    def load_weights(step, which):
+        source = (wg_hbm, wu_hbm)[which]
+        return pltpu.make_async_copy(
+            source.at[:, pl.ds(pl.multiple_of(step * cols, cols), cols)],
+            w_bufs.at[which, step % 2],
+            w_sems.at[which, step % 2],
+        )
+
+    load_x = pltpu.make_async_copy(x_hbm, x_buf, in_sems.at[0])
+    load_gb = pltpu.make_async_copy(gb_hbm, gb_buf, in_sems.at[1])
+    load_own = pltpu.make_async_copy(shard, own_stage, local_sem)
+    load_x.start()
+    for which in range(2):
+        load_weights(0, which).start()
+    load_own.start()
+    load_gb.start()
+    place, neighbours = ring_setup(count)
+
+    def target(ref, member, side, part):
+        return piece(ref, (hidden, block), 1, member, side, part, parts)
+
+    def hop(step, side, part):
+        ref = target(down_all, member_at(place, side, step, count), side, part)
+        return pltpu.make_async_remote_copy(
+            src_ref=ref,
+            dst_ref=ref,
+            send_sem=send_sems.at[side, step, part],
+            recv_sem=recv_sems.at[side, step, part],
+            device_id={"dp": neighbours[side]},
+            device_id_type=MESH_ID,
+        )
+
+    for part in range(parts):
+        for side in range(2):
+            pltpu.make_async_remote_copy(
+                src_ref=piece(shard, (hidden, block), None, 0, side, part, parts),
+                dst_ref=target(down_all, me, side, part),
+                send_sem=send_sems.at[side, 0, part],
+                recv_sem=recv_sems.at[side, 0, part],
+                device_id={"dp": neighbours[side]},
+                device_id_type=MESH_ID,
+            ).start()
+
+    def pump(step):
+        for part in range(parts):
+            for side in range(2):
+                hop(step - 1, side, part).wait_recv()
+                hop(step, side, part).start()
+
+    load_own.wait()
+    store_own = pltpu.make_async_copy(
+        own_stage, down_all.at[:, pl.ds(pl.multiple_of(me * block, block), block)], local_sem
+    )
+    store_own.start()
+    load_x.wait()
+
+    def store(ref, which, step):
+        return pltpu.make_async_copy(
+            stage.at[which, step % 2],
+            ref.at[:, pl.ds(pl.multiple_of(step * cols, cols), cols)],
+            out_sems.at[which, step % 2],
+        )
+
+    def forward(step, carry):
+        @pl.when(step + 1 < steps)
+        def _():
+            for which in range(2):
+                load_weights(step + 1, which).start()
+
+        @pl.when(step >= 2)
+        def _():
+            store(act_hbm, 0, step - 2).wait()
+
+        for which in range(2):
+            load_weights(step, which).wait()
+        here = pl.ds(pl.multiple_of(step * cols, cols), cols)
+        for top in range(0, rows, 256):
+            band = pl.ds(top, 256)
+            lines = x_buf[band, :]
+            gate = jnp.dot(lines, w_bufs[0, step % 2], preferred_element_type=F32)
+            up = jnp.dot(lines, w_bufs[1, step % 2], preferred_element_type=F32)
+            sig = jax.nn.sigmoid(gate)
+            silu = gate * sig
+            stage[0, step % 2, band, :] = (silu * up).astype(BF16)
+            gate_slope[band, here] = up * sig * (1.0 + gate * (1.0 - sig))
+            up_slope[band, here] = silu
+        store(act_hbm, 0, step).start()
+
+        turn = step // 2
+
+        @pl.when((step % 2 == 0) & (turn >= 1) & (turn <= count - 2))
+        def _():
+            pump(turn)
+
+        return carry
+
+    lax.fori_loop(0, steps, forward, 0)
+    for step in range(max(steps - 2, 0), steps):
+        store(act_hbm, 0, step).wait()
+    pumped = min((steps - 1) // 2, count - 2)
+    load_gb.wait()
+
+    def load_half(step, side):
+        member = member_at(place, side, step, count)
+        return pltpu.make_async_copy(
+            down_all.at[
+                pl.ds(side * half, half), pl.ds(pl.multiple_of(member * block, block), block)
+            ],
+            half_bufs.at[side],
+            half_sems.at[side],
+        )
+
+    def backward(step, carry):
+        @pl.when((step > pumped) & (step <= count - 2))
+        def _():
+            pump(step)
+
+        @pl.when(step == count - 1)
+        def _():
+            for part in range(parts):
+                for side in range(2):
+                    hop(count - 2, side, part).wait_recv()
+
+        for side in range(2):
+            load_half(step, side).start()
+        for side in range(2):
+            member = member_at(place, side, step, count)
+            load_half(step, side).wait()
+            for top in range(0, rows, 256):
+                band = pl.ds(top, 256)
+                lines = gb_buf[band, pl.ds(pl.multiple_of(member * block, block), block)]
+                value = nt_dot(lines, half_bufs[side])
+                spot = (band, pl.ds(side * half, half))
+
+                @pl.when(step == 0)
+                def _():
+                    acc[spot] = value
+
+                @pl.when(step > 0)
+                def _():
+                    acc[spot] += value
+
+        return carry
+
+    store_own.wait()
+    lax.fori_loop(0, count, backward, 0)
+
+    def slopes(step, carry):
+        @pl.when(step >= 2)
+        def _():
+            store(gg_hbm, 1, step - 2).wait()
+            store(gu_hbm, 2, step - 2).wait()
+
+        here = pl.ds(pl.multiple_of(step * cols, cols), cols)
+        for top in range(0, rows, 256):
+            band = pl.ds(top, 256)
+            value = acc[band, here]
+            stage[1, step % 2, band, :] = (value * gate_slope[band, here]).astype(BF16)
+            stage[2, step % 2, band, :] = (value * up_slope[band, here]).astype(BF16)
+        store(gg_hbm, 1, step).start()
+        store(gu_hbm, 2, step).start()
+        return carry
+
+    lax.fori_loop(0, steps, slopes, 0)
+    for step in range(max(steps - 2, 0), steps):
+        store(gg_hbm, 1, step).wait()
+        store(gu_hbm, 2, step).wait()
+
+    def drain(step, carry):
+        for part in range(parts):
+            for side in range(2):
+                hop(step, side, part).wait_send()
+        return carry
+
+    lax.fori_loop(0, count - 1, drain, 0)
+
+
+def mlp_ring(rows_mlp, gate_all, up_all, w_down, grad_branch, count, collective_id):
+    rows, width = rows_mlp.shape
+    hidden, block = w_down.shape
+    cols, parts = 256, 2
+    wide = jax.ShapeDtypeStruct((rows, hidden), BF16)
+    return pl.pallas_call(
+        functools.partial(mlp_kernel, count),
+        out_shape=[wide] * 3 + [jax.ShapeDtypeStruct((hidden, width), BF16)],
+        in_specs=[pl.BlockSpec(memory_space=pl.ANY)] * 5,
+        out_specs=[pl.BlockSpec(memory_space=pl.ANY)] * 4,
+        scratch_shapes=[
+            pltpu.VMEM((rows, width), BF16),
+            pltpu.VMEM((rows, width), BF16),
+            pltpu.VMEM((2, 2, width, cols), BF16),
+            pltpu.VMEM((rows, hidden), F32),
+            pltpu.VMEM((rows, hidden), F32),
+            pltpu.VMEM((rows, hidden), F32),
+            pltpu.VMEM((2, hidden // 2, block), BF16),
+            pltpu.VMEM((3, 2, rows, cols), BF16),
+            pltpu.VMEM((hidden, block), BF16),
+            pltpu.SemaphoreType.DMA((2, count - 1, parts)),
+            pltpu.SemaphoreType.DMA((2, count - 1, parts)),
+            pltpu.SemaphoreType.DMA((2, 2)),
+            pltpu.SemaphoreType.DMA((2,)),
+            pltpu.SemaphoreType.DMA((2,)),
+            pltpu.SemaphoreType.DMA((3, 2)),
+            pltpu.SemaphoreType.DMA,
+        ],
+        compiler_params=pltpu.CompilerParams(
+            collective_id=collective_id, has_side_effects=True, vmem_limit_bytes=60 << 20
+        ),
+        cost_estimate=pl.CostEstimate(
+            flops=6 * rows * width * hidden,
+            bytes_accessed=40 * hidden * width,
+            transcendentals=rows * hidden,
+        ),
+        name="mlp_ring",
+    )(rows_mlp, gate_all, up_all, w_down, grad_branch)
+
+
+def ring_weight_grads(jobs, parts, count, collective_id):
+    if all(left.shape[1] // count % 128 == 0 for left, _ in jobs):
+        return ring_scatter_dots(jobs, parts, count, collective_id)
+    partials = [tn_dot(left, right).astype(BF16) for left, right in jobs]
+    num = len(jobs)
+    return ring_scatter(partials, [0] * num, [parts] * num, count, collective_id)
+
+
 def after(value, *deps):
     return lax.optimization_barrier((value,) + deps)[0]
 
@@ -637,24 +1160,34 @@
     normed_mlp = after(normed_mlp, gate_all)
     rows_mlp = gather_rows(normed_mlp)
     (up_all,) = ring_gather([after(w_up, normed_mlp)], (0,), (2,), count, 2)
-    gate_proj = dot(rows_mlp, after(gate_all, up_all))
-    up_proj = dot(rows_mlp, up_all)
-    gate_sig = jax.nn.sigmoid(gate_proj)
-    activated = (gate_proj * gate_sig * up_proj).astype(BF16)
-    (down_all,) = ring_gather([after(w_down, up_all)], (1,), (2,), count, 3)
-    mlp_part = dot(activated, down_all).astype(BF16)
-    mlp_branch = scatter_rows(mlp_part)
+    if w_down.shape[1] % 128 == 0:
+        activated, grad_gate_pre, grad_up_pre, down_all = mlp_ring(
+            rows_mlp, gate_all, after(up_all, rows_mlp), w_down, grad_branch, count, 3
+        )
+        grad_down, norm_part, mlp_part = down_ring(
+            grad_branch, activated, grad_gate_pre, grad_up_pre, gate_all, up_all, down_all,
+            count, 4,
+        )
+    else:
+        gate_proj = dot(rows_mlp, gate_all)
+        up_proj = dot(rows_mlp, up_all)
+        gate_sig = jax.nn.sigmoid(gate_proj)
+        activated = (gate_proj * gate_sig * up_proj).astype(BF16)
+        (down_all,) = ring_gather([after(w_down, up_all)], (1,), (2,), count, 3)
+        mlp_part = dot(activated, down_all).astype(BF16)
+        grad_act = nt_dot(grad_branch, down_all)
+        grad_gate_pre = (
+            grad_act * up_proj * gate_sig * (1.0 + gate_proj * (1.0 - gate_sig))
+        ).astype(BF16)
+        grad_up_pre = (grad_act * gate_proj * gate_sig).astype(BF16)
+        norm_part = (nt_dot(grad_gate_pre, gate_all) + nt_dot(grad_up_pre, up_all)).astype(BF16)
+        (grad_down,) = ring_weight_grads([(grad_branch, activated)], 2, count, 4)
+    grad_norm_two = scatter_rows(norm_part)
+    (grad_gate,) = ring_weight_grads(
+        [(after(rows_mlp, norm_part), grad_gate_pre)], 2, count, 5
+    )
+    mlp_branch = scatter_rows(after(mlp_part, grad_norm_two, grad_gate))
     layer_out = (hidden + mlp_branch).astype(BF16)
-
-    grad_act = nt_dot(grad_branch, after(down_all, mlp_part))
-    grad_gate_pre = (grad_act * up_proj * gate_sig * (1.0 + gate_proj * (1.0 - gate_sig))).astype(
-        BF16
-    )
-    grad_up_pre = (grad_act * gate_proj * gate_sig).astype(BF16)
-    norm_part = (nt_dot(grad_gate_pre, gate_all) + nt_dot(grad_up_pre, up_all)).astype(BF16)
-    down_part = tn_dot(activated, after(grad_branch, norm_part)).astype(BF16)
-    grad_norm_two = scatter_rows(after(norm_part, mlp_branch))
-    (grad_down,) = ring_scatter([down_part], (1,), (2,), count, 4)
     scaled_two = grad_norm_two * gain_mlp
     gain_two_part = jnp.sum(grad_norm_two * hidden * inv_second, axis=0)
     grad_hidden = (
@@ -662,11 +1195,12 @@
         + inv_second * scaled_two
         - hidden * inv_second**3 * jnp.mean(scaled_two * hidden, axis=1, keepdims=True)
     )
-    grad_hidden = after(grad_hidden, grad_down)
+    grad_hidden = after(grad_hidden, grad_gate)
     grad_attn = gather_rows(grad_hidden.astype(BF16))
-    gate_part = tn_dot(rows_mlp, after(grad_gate_pre, grad_hidden)).astype(BF16)
-    up_part = tn_dot(rows_mlp, after(grad_up_pre, gate_part)).astype(BF16)
-    grad_heads = nt_dot(after(grad_attn, up_part), output_all).astype(BF16)
+    (grad_up,) = ring_weight_grads(
+        [(after(rows_mlp, grad_hidden), grad_up_pre)], 2, count, 6
+    )
+    grad_heads = nt_dot(after(grad_attn, grad_up), output_all).astype(BF16)
     grad_qpre, grad_kpre, grad_vpre = attend_back(
         queries, keys, values, grad_heads, lengths, cosine, sine
     )
@@ -674,12 +1208,7 @@
         nt_dot(grad_qpre, query_all) + nt_dot(grad_kpre, key_all) + nt_dot(grad_vpre, value_all)
     ).astype(BF16)
     grad_norm_one = scatter_rows(token_part)
-    (grad_gate,) = ring_scatter([after(gate_part, token_part)], (0,), (2,), count, 5)
-    output_part = tn_dot(head_out, grad_attn).astype(BF16)
-    query_part = tn_dot(rows_attn, grad_qpre).astype(BF16)
-    key_part = tn_dot(rows_attn, grad_kpre).astype(BF16)
-    value_part = tn_dot(rows_attn, grad_vpre).astype(BF16)
-    (grad_up,) = ring_scatter([after(up_part, grad_gate)], (0,), (2,), count, 6)
+    grad_qkv = jnp.concatenate([grad_qpre, grad_kpre, grad_vpre], axis=1)
     scaled_one = grad_norm_one * gain_attn
     gain_one_part = jnp.sum(grad_norm_one * token_full * inv_first, axis=0)
     grad_tokens = (
@@ -687,11 +1216,17 @@
         + inv_first * scaled_one
         - token_full * inv_first**3 * jnp.mean(scaled_one * token_full, axis=1, keepdims=True)
     )
-    grad_attn_gain, grad_mlp_gain = sum_shares(gain_one_part, gain_two_part, count, group, 8)
-    grad_query, grad_key, grad_value, grad_output = ring_scatter(
-        [after(query_part, grad_up, grad_attn_gain), key_part, value_part, output_part],
-        (0, 0, 0, 1), (1, 1, 1, 1), count, 7,
-    )
+    attn_grads, grad_output = ring_weight_grads(
+        [(after(rows_attn, token_part), grad_qkv), (grad_attn, head_out)], 1, count, 7
+    )
+    grad_attn_gain, grad_mlp_gain = sum_shares(
+        after(gain_one_part, attn_grads), gain_two_part, count, group, 8
+    )
+    query_cols, key_cols = grad_qpre.shape[1], grad_kpre.shape[1]
+    grad_query = attn_grads[:, :query_cols]
+    grad_key = attn_grads[:, query_cols : query_cols + key_cols]
+    grad_value = attn_grads[:, query_cols + key_cols :]
+    grad_output, grad_down = grad_output.T, grad_down.T
     return (
         layer_out,
         grad_tokens,

time: 897 us -> 818 us (0.912)
  matrix products: 154 us -> 16.6 us
  waiting for transfers between devices: 8.37 us -> 42.3 us
  Pallas kernels: 661 us -> 685 us
    pallas_call x4 -> x5, Pallas kernels: 303 us -> 406 us  [the longest x4 307 us: ring_scatter_dots(): pl.pallas_call(functools.partial(scatter_dot_kernel, count, items, parts,...]
    pallas_call x4 -> x3, Pallas kernels: 298 us -> 218 us  [ring_gather(): pl.pallas_call(functools.partial(gather_kernel, count, items), out_shape=...]
    dot_general x7 -> x0, matrix products: 50.5 us -> none  [tn_dot(): lax.dot_general(left, right, (((0,), (0,)), ((), ())), preferred_element_...]
    dot_general x7 -> x4, matrix products: 59 us -> 12.2 us  [nt_dot(): lax.dot_general(left, right, (((1,), (1,)), ((), ())), preferred_element_...]
    reduce_scatter x4, waiting for transfers between devices: 0.06 us -> 42 us  [scatter_rows(): lax.psum_scatter(value.astype(BF16), 'tensor', scatter_dimension=0, tiled...]
    dot_general x4 -> x1, matrix products: 45 us -> 4.34 us  [dot(): return jnp.dot(left, right, preferred_element_type=F32)]
    unnamed x123 -> x46, local copies, waits for them, and re-layouts: 19.3 us -> 15.6 us
  transfers between devices with their start and end apart: 8 -> 8, of which waited for: 1 -> 1; matrix products, arithmetic and copies ran while one was open for 11% -> 2% of each run, Pallas kernels for 61% -> 54%
where the time goes in v2:
time: 818 us; the launch traced here: 809 us
  Pallas kernels  685 us (84%)
  waiting for transfers between devices  42.3 us (5%)
  other arithmetic  27.3 us (3%)
  local copies, waits for them, and re-layouts  21.6 us (3%)
  matrix products  16.6 us (2%)
  between operations  15.6 us (2%)
    pallas_call x4, Pallas kernels, ring_scatter_dots(): pl.pallas_call(functools.partial(scatter_dot_kernel, count, items, parts,...  307 us
    pallas_call x3, Pallas kernels, ring_gather(): pl.pallas_call(functools.partial(gather_kernel, count, items), out_shape=...  218 us
    pallas_call x1, Pallas kernels, mlp_ring(): pl.pallas_call(functools.partial(mlp_kernel, count), out_shape=[wide] * 3...  98.7 us
    reduce_scatter x4, waiting for transfers between devices, scatter_rows(): lax.psum_scatter(value.astype(BF16), 'tensor', scatter_dimension=0, tiled...  42 us
    pallas_call x1, Pallas kernels, attend_back(): pl.pallas_call(attend_back_kernel, grid=(pairs,), out_shape=[jax.ShapeDty...  27.9 us
    pallas_call x1, Pallas kernels, attend(): pl.pallas_call(attend_kernel, grid=(pairs,), out_shape=jax.ShapeDtypeStru...  17.4 us
  transfers between devices with their start and end apart: 8, of which 1 were waited for; matrix products, arithmetic and copies ran while one was open for 2% of the time, Pallas kernels for 54%

profile of v2, /device:TPU:0, one launch (start us, length us, event | category | flops | bytes accessed | tf_op | source)
XLA Modules:
  0.0 808.7 jit_solution(8520007111428390136)
XLA Ops:
  7.2 0.0 all-gather.5.cloned.1.call-start
  7.2 1.5 fusion.3
  8.7 0.7 convert_element_type.58
  9.4 2.5 fusion.5
  12.0 0.0 reduce-scatter.5.cloned.1.call-start
  12.7 55.7 %ring_gather_0.1 = (bf16[2048,512]{1,0:T(8,128)(2,1)}, bf16[2048,128]{1,0:T(8,128)(2,1)}, bf16[2048,128]{1,0:T(8,128)(2,1)}, bf16[512,2048]{1,0:T(8,128)(2,1)}) custom-call(bf16[256,512]{1,0:T(8,128)(2,1)} %refs_0_, bf16[256,128]{1,0:T(8,128)(2,1)} %refs_1_.1, bf16[256,128]{1,0:T(8,128)(2,1)} %refs_2_.1, bf16[512,256]{1,0:T(8,128)(2,1)} %refs_3_.2), custom_call_target="tpu_custom_call" | custom-call | bytes 91750400 | tf_op jit(solution)/shard_map/ring_gather_0/pallas_call | solution.py:347
  68.4 2.0 fusion.13
  70.4 0.9 pad_maximum_fusion.1
  71.3 0.0 all-gather.5.cloned.1.call-done.x_ref.refs_0_
  71.3 2.3 copy-done.4
  73.6 1.6 copy-done.5
  75.2 5.0 project.1
  80.3 17.4 %attend.1.refs_3_ = bf16[1024,512]{1,0:T(8,128)(2,1)S(1)} custom-call(s32[1]{0:T(128)} %copy.30.length_ref, bf16[1024,512]{1,0:T(8,128)(2,1)S(1)} %get-tuple-element.47.q_ref, bf16[1024,128]{1,0:T(8,128)(2,1)S(1)} %get-tuple-element.48.k_ref, bf16[1024,128]{1,0:T(8,128)(2,1)S(1)} %get-tuple-element.49.v_ref), custom_call_target="tpu_custom_call" | custom-call | flops 12884901888 | bytes 4194304 | tf_op jit(solution)/shard_map/attend/pallas_call | solution.py:136
  97.7 1.0 copy-done.9
  98.7 4.3 convolution_convert_fusion
  103.1 0.0 all-gather.9.cloned.1.call-start
  103.1 0.6 copy-done.19
  103.7 82.2 %ring_gather_1.1.refs_1_.refs_4_ = bf16[2048,2048]{1,0:T(8,128)(2,1)} custom-call(bf16[256,2048]{1,0:T(8,128)(2,1)} %refs_0_.1), custom_call_target="tpu_custom_call" | custom-call | bytes 146800640 | tf_op jit(solution)/shard_map/ring_gather_1/pallas_call | solution.py:347
  185.9 0.0 reduce-scatter.5.cloned.1.call-done
  186.0 1.7 multiply_reduce_fusion.2
  187.7 1.5 multiply_convert_fusion
  189.2 0.3 all-gather.7.cloned.1.call-start
  189.5 2.4 fusion.10
  192.0 0.0 reduce-scatter.7.cloned.1.call-start
  192.0 80.3 %ring_gather_2.1.refs_2_.refs_5_ = bf16[2048,2048]{1,0:T(8,128)(2,1)} custom-call(bf16[256,2048]{1,0:T(8,128)(2,1)} %refs_0_.2), custom_call_target="tpu_custom_call" | custom-call | bytes 146800640 | tf_op jit(solution)/shard_map/ring_gather_2/pallas_call | solution.py:347
  272.3 0.0 all-gather.9.cloned.1.call-done.refs_0_
  272.3 0.0 all-gather.7.cloned.1.call-done.refs_4_.refs_0_
  272.4 98.7 %mlp_ring.1 = (bf16[1024,2048]{1,0:T(8,128)(2,1)}, bf16[1024,2048]{1,0:T(8,128)(2,1)}, bf16[1024,2048]{1,0:T(8,128)(2,1)}, bf16[2048,2048]{1,0:T(8,128)(2,1)}) custom-call(bf16[1024,2048]{1,0:T(8,128)(2,1)} %all-gather.9.cloned.1.call-done.refs_0_, bf16[2048,2048]{1,0:T(8,128)(2,1)} %ring_gather_1.1.refs_1_.refs_4_, ...), custom_call_target="tpu_custom_call" | custom-call | flops 25769803776 | bytes 167772160 | tf_op jit(solution)/shard_map/mlp_ring/pallas_call | solution.py:979
  371.1 84.7 %ring_scatter_4.1 = (f32[256,2048]{1,0:T(8,128)}, bf16[1024,2048]{1,0:T(8,128)(2,1)}, bf16[1024,2048]{1,0:T(8,128)(2,1)}) custom-call(bf16[1024,2048]{1,0:T(8,128)(2,1)} %all-gather.7.cloned.1.call-done.refs_4_.refs_0_, bf16[1024,2048]{1,0:T(8,128)(2,1)} %get-tuple-element.56.refs_1_, bf16[1024,2048]{1,0:T(8,128)(2,1)} %get-tuple-element.57.refs_2_.refs_1_, ...), custom_call_target="tpu_custom_call" | custom-call | flops 8589934592 | bytes 167772160 | tf_op jit(solution)/shard_map/ring_scatter_4/pallas_call | solution.py:638
  455.9 0.0 reduce-scatter.7.cloned.1.call-update
  455.9 0.0 reduce-scatter.9.cloned.1.call-start
  455.9 81.7 %ring_scatter_5.1 = f32[256,2048]{1,0:T(8,128)} custom-call(bf16[1024,2048]{1,0:T(8,128)(2,1)} %all-gather.9.cloned.1.call-done.refs_0_, bf16[1024,2048]{1,0:T(8,128)(2,1)} %get-tuple-element.57.refs_2_.refs_1_), custom_call_target="tpu_custom_call" | custom-call | flops 8589934592 | bytes 167772160 | tf_op jit(solution)/shard_map/ring_scatter_5/pallas_call | solution.py:638
  537.6 0.2 all-gather.11.cloned.1.call-start
  537.8 0.0 reduce-scatter.7.cloned.1.call-done
  537.9 2.3 multiply_reduce_fusion
  540.2 42.0 %reduce-scatter.9.cloned.1.call-done = bf16[256,2048]{1,0:T(8,128)(2,1)} async-done(((bf16[1024,2048]{1,0:T(8,128)(2,1)}), bf16[256,2048]{1,0:T(8,128)(2,1)}) %reduce-scatter.9.cloned.1.call-update) | async-done | bytes 1048592 | tf_op jit(solution)/shard_map/reduce_scatter | solution.py:1031
  582.2 4.2 multiply_subtract_fusion
  586.3 1.3 copy-done.14
  587.6 1.1 convert_element_type.70
  588.8 0.0 reduce-scatter.11.cloned.1.call-start
  588.8 85.9 %ring_scatter_6.1 = f32[256,2048]{1,0:T(8,128)} custom-call(bf16[1024,2048]{1,0:T(8,128)(2,1)} %all-gather.9.cloned.1.call-done.refs_0_, bf16[1024,2048]{1,0:T(8,128)(2,1)} %get-tuple-element.58.refs_3_.refs_1_), custom_call_target="tpu_custom_call" | custom-call | flops 8589934592 | bytes 167772160 | tf_op jit(solution)/shard_map/ring_scatter_6/pallas_call | solution.py:638
  674.8 0.0 all-gather.11.cloned.1.call-done.refs_1_
  674.8 5.3 convolution_convert_fusion.1.g_ref
  680.2 27.9 %attend_back.1 = (bf16[1024,512]{1,0:T(8,128)(2,1)S(1)}, bf16[1024,128]{1,0:T(8,128)(2,1)S(1)}, bf16[1024,128]{1,0:T(8,128)(2,1)S(1)}) custom-call(s32[1]{0:T(128)} %copy.30.length_ref, bf16[1024,512]{1,0:T(8,128)(2,1)S(1)} %copy-done.8, bf16[1024,128]{1,0:T(8,128)(2,1)S(1)} %get-tuple-element.48.k_ref, bf16[1024,128]{1,0:T(8,128)(2,1)S(1)} %copy-done.11, ...), custom_call_target="tpu_custom_call" | custom-call | flops 25769803776 | bytes 8388608 | tf_op jit(solution)/shard_map/attend_back/pallas_call | solution.py:201
  708.1 2.4 fusion.15
  710.5 1.3 fusion.16
  711.7 3.3 add_convert_fusion
  715.0 2.9 copy.27
  717.9 0.1 stack.10
  718.0 1.3 pad_maximum_fusion.refs_2_
  719.3 55.0 %ring_scatter_7.1 = (f32[256,768]{1,0:T(8,128)}, f32[256,512]{1,0:T(8,128)}) custom-call(bf16[1024,2048]{1,0:T(8,128)(2,1)} %all-gather.5.cloned.1.call-done.x_ref.refs_0_, bf16[1024,2048]{1,0:T(8,128)(2,1)} %all-gather.11.cloned.1.call-done.refs_1_, bf16[1024,768]{1,0:T(8,128)(2,1)} %pad_maximum_fusion.refs_2_, bf16[1024,512]{1,0:T(8,128)(2,1)} %copy-done.9), custom_call_target="tpu_custom_call" | custom-call | flops 5368709120 | bytes 104857600 | tf_op jit(solution)/shard_map/ring_scatter_7/pallas_call | solution.py:638
  774.3 2.1 copy.26
  776.4 2.0 slice.15
  778.4 1.7 fusion.14
  780.1 1.9 fusion.9
  782.0 0.1 stack.9
  782.1 0.1 reshape.97
  782.2 0.7 pad.4.parts_ref
  782.9 10.3 %sum_shares.1 = f32[8,128]{1,0:T(8,128)} custom-call(f32[4,8,8,128]{3,2,1,0:T(8,128)} %pad.4.parts_ref), custom_call_target="tpu_custom_call" | custom-call | tf_op jit(solution)/shard_map/sum_shares/pallas_call | solution.py:1098
  793.2 1.3 slice_bitcast_fusion
  794.5 3.3 fusion.2
  797.8 1.3 copy.31
  799.2 1.0 copy-done.18
  800.2 1.3 copy.32
  (53 shorter events, 0.3 us)
Async XLA Ops:
  7.2 64.1 %all-gather.5.cloned.1.call-start = ((), (), s32[]{:S(2)}) async-start(), calls=%async_computation.4 | async-start | bytes 5242880 | tf_op jit(solution)/shard_map/all_gather | solution.py:1027
  12.0 174.0 %reduce-scatter.5.cloned.1.call-start = ((), (), s32[]{:S(2)}) async-start(), calls=%async_computation.5 | async-start | bytes 5242880 | tf_op jit(solution)/shard_map/reduce_scatter | solution.py:1031
  68.4 2.9 copy-start
  68.4 2.9 copy-start.1
  71.2 9.0 %copy-start.2 = (f32[1024,128]{1,0:T(8,128)}, f32[1024,128]{1,0:T(8,128)S(1)}, u32[]{:S(2)}) copy-start(f32[1024,128]{1,0:T(8,128)S(1)} %get-tuple-element.115.sin_ref) | copy-start | bytes 1572868
  71.3 2.3 copy-start.4
  73.6 1.6 copy-start.5
  80.3 17.4 %copy-start.7 = (bf16[1024,512]{1,0:T(8,128)(2,1)}, bf16[1024,512]{1,0:T(8,128)(2,1)S(1)}, u32[]{:S(2)}) copy-start(bf16[1024,512]{1,0:T(8,128)(2,1)S(1)} %get-tuple-element.47.q_ref) | copy-start | bytes 3145732
  80.3 17.4 %copy-start.10 = (bf16[1024,128]{1,0:T(8,128)(2,1)}, bf16[1024,128]{1,0:T(8,128)(2,1)S(1)}, u32[]{:S(2)}) copy-start(bf16[1024,128]{1,0:T(8,128)(2,1)S(1)} %get-tuple-element.49.v_ref) | copy-start | bytes 786436
  80.3 18.4 %copy-start.20 = (bf16[512,2048]{1,0:T(8,128)(2,1)S(1)}, bf16[512,2048]{1,0:T(8,128)(2,1)}, u32[]{:S(2)}) copy-start(bf16[512,2048]{1,0:T(8,128)(2,1)} %get-tuple-element.50) | copy-start | bytes 6291460
  97.7 1.0 copy-start.9
  103.0 0.7 copy-start.19
  103.1 169.3 %all-gather.9.cloned.1.call-start = ((), (), s32[]{:S(2)}) async-start(), calls=%async_computation.7 | async-start | bytes 5242880 | tf_op jit(solution)/shard_map/all_gather | solution.py:1027
  103.7 82.2 %copy-start.12 = (bf16[256,2048]{1,0:T(8,128)(2,1)S(1)}, bf16[256,2048]{1,0:T(8,128)(2,1)}, u32[]{:S(2)}) copy-start(bf16[256,2048]{1,0:T(8,128)(2,1)} %param.12) | copy-start | bytes 3145732
  186.0 1.8 copy-start.16
  189.2 83.1 %all-gather.7.cloned.1.call-start = ((), (), s32[]{:S(2)}) async-start(), calls=%async_computation.6 | async-start | bytes 5242880 | tf_op jit(solution)/shard_map/all_gather | solution.py:1027
  192.0 345.9 %reduce-scatter.7.cloned.1.call-start = ((), (), s32[]{:S(2)}) async-start(), calls=%async_computation.8 | async-start | bytes 5242880 | tf_op jit(solution)/shard_map/reduce_scatter | solution.py:1031
  455.9 126.3 %reduce-scatter.9.cloned.1.call-start = ((), (), s32[]{:S(2)}) async-start(), calls=%async_computation.9 | async-start | bytes 5242880 | tf_op jit(solution)/shard_map/reduce_scatter | solution.py:1031
  537.6 137.2 %all-gather.11.cloned.1.call-start = ((), (), s32[]{:S(2)}) async-start(), calls=%async_computation.10 | async-start | bytes 5242880 | tf_op jit(solution)/shard_map/all_gather | solution.py:1027
  586.3 1.3 copy-start.14
  588.8 191.4 %reduce-scatter.11.cloned.1.call-start = ((), (), s32[]{:S(2)}) async-start(), calls=%async_computation.11 | async-start | bytes 5242880 | tf_op jit(solution)/shard_map/reduce_scatter | solution.py:1031
  674.8 5.4 copy-start.3
  674.8 5.4 copy-start.8
  674.8 5.4 copy-start.11
  680.2 27.9 %copy-start.6 = (bf16[2048,512]{1,0:T(8,128)(2,1)S(1)}, bf16[2048,512]{1,0:T(8,128)(2,1)}, u32[]{:S(2)}) copy-start(bf16[2048,512]{1,0:T(8,128)(2,1)} %get-tuple-element.44.wq_ref) | copy-start | bytes 6291460
  774.3 5.8 copy-start.13
  776.4 18.1 %copy-start.15 = (f32[256,2048]{1,0:T(8,128)S(1)}, f32[256,2048]{1,0:T(8,128)}, u32[]{:S(2)}) copy-start(f32[256,2048]{1,0:T(8,128)} %copy-done.14) | copy-start | bytes 6291460
  794.5 3.3 copy-start.17
  797.8 2.3 copy-start.18
Sparse Core Ops, SparseCore 0:
  12.1 37.1 all-gather.4
  103.2 44.6 reduce-scatter.4
  189.3 33.4 all-gather.8
  224.9 34.4 all-gather.6
  456.0 43.5 reduce-scatter.6
  537.7 44.3 reduce-scatter.8
  588.9 34.4 all-gather.10
  715.2 43.6 reduce-scatter.10

commit v3 on v2

--- a/solution.py
+++ b/solution.py
@@ -15,6 +15,7 @@
 theta = 500000.0
 MESH_ID = pl.DeviceIdType.MESH
 BF16 = jnp.bfloat16
+ANY = pl.BlockSpec(memory_space=pl.ANY)
 F32 = jnp.float32
 
 
@@ -55,21 +56,31 @@
     return lax.dot_general(left, right, (((0,), (0,)), ((), ())), preferred_element_type=F32)
 
 
-def project_kernel(x_ref, wq_ref, wk_ref, wv_ref, cos_ref, sin_ref, q_ref, k_ref, v_ref):
-    rows = x_ref[...]
-    cosine, sine = cos_ref[...], sin_ref[...]
-
-    def rope(value):
-        return (value * cosine + swap_halves(value) * sine).astype(BF16)
-
+def rope(value, cosine, sine):
+    return (value * cosine + swap_halves(value) * sine).astype(BF16)
+
+
+def rope_back(grads, cosine, sine):
+    return (grads * cosine - swap_halves(grads) * sine).astype(BF16)
+
+
+def project_rows(rows, wq_ref, wk_ref, wv_ref, cosine, sine, q_ref, k_ref, v_ref):
     for block in range(q_ref.shape[1] // 256):
         cols = slice(block * 256, (block + 1) * 256)
         value = jnp.dot(rows, wq_ref[:, cols], preferred_element_type=F32)
         for half in range(2):
             start = block * 256 + half * 128
-            q_ref[:, start : start + 128] = rope(value[:, half * 128 : half * 128 + 128])
-    k_ref[...] = rope(jnp.dot(rows, wk_ref[...], preferred_element_type=F32))
+            q_ref[:, start : start + 128] = rope(
+                value[:, half * 128 : half * 128 + 128], cosine, sine
+            )
+    k_ref[...] = rope(jnp.dot(rows, wk_ref[...], preferred_element_type=F32), cosine, sine)
     v_ref[...] = jnp.dot(rows, wv_ref[...], preferred_element_type=F32).astype(BF16)
+
+
+def project_kernel(x_ref, wq_ref, wk_ref, wv_ref, cos_ref, sin_ref, q_ref, k_ref, v_ref):
+    project_rows(
+        x_ref[...], wq_ref, wk_ref, wv_ref, cos_ref[...], sin_ref[...], q_ref, k_ref, v_ref
+    )
 
 
 def project(rows, w_query, w_key, w_value, cosine, sine):
@@ -109,13 +120,11 @@
     return jnp.where(lane_index(first.shape) < HD, first, second)
 
 
-def attend_kernel(length_ref, q_ref, k_ref, v_ref, o_ref):
-    kv = pl.program_id(0) // 2
-    length = length_ref[0]
+def attend_pair(length, kv, q_ref, k_ref, v_ref, o_ref):
     for block in range(LEN // QB):
         rows = slice(block * QB, (block + 1) * QB)
         keys = (block + 1) * QB
-        pair = (q_ref[rows, :].astype(F32) * HD**-0.5).astype(F32)
+        pair = q_ref[rows, :].astype(F32) * HD**-0.5
         query_pos = block * QB + lax.broadcasted_iota(jnp.int32, (QB, keys), 0)
         key_pos = lax.broadcasted_iota(jnp.int32, (QB, keys), 1)
         allowed = (key_pos <= query_pos) & (key_pos < length)
@@ -127,6 +136,10 @@
             probs = (exps / jnp.sum(exps, axis=1, keepdims=True)).astype(BF16)
             outs.append(jnp.dot(probs, v_ref[:keys, :], preferred_element_type=F32))
         o_ref[rows, :] = join_heads(outs[0], outs[1], kv).astype(BF16)
+
+
+def attend_kernel(length_ref, q_ref, k_ref, v_ref, o_ref):
+    attend_pair(length_ref[0], pl.program_id(0) // 2, q_ref, k_ref, v_ref, o_ref)
 
 
 def attend(queries, keys, values, lengths):
@@ -147,21 +160,9 @@
     )(lengths, queries, keys, values)
 
 
-def attend_back_kernel(
-    length_ref, q_ref, k_ref, v_ref, g_ref, cos_ref, sin_ref, gq_ref, gk_ref, gv_ref, acc_k, acc_v
+def attend_back_pair(
+    length, kv, q_ref, k_ref, v_ref, g_ref, cos_ref, sin_ref, gq_ref, acc_k, acc_v
 ):
-    pair_index = pl.program_id(0)
-    kv = pair_index // 2
-    length = length_ref[0]
-
-    @pl.when(pair_index == 0)
-    def _():
-        acc_k[...] = jnp.zeros_like(acc_k)
-        acc_v[...] = jnp.zeros_like(acc_v)
-
-    def rope_back(grads, rows):
-        return grads * cos_ref[rows, :] + swap_halves(grads) * (-sin_ref[rows, :])
-
     for block in range(LEN // QB):
         rows = slice(block * QB, (block + 1) * QB)
         keys = (block + 1) * QB
@@ -185,11 +186,27 @@
             acc_k[:keys, :] += jnp.dot(grad_scores, query, preferred_element_type=F32)
             grad_queries.append(tn_dot(grad_scores, key_vecs) * HD**-0.5)
         joined = join_heads(grad_queries[0], grad_queries[1], kv)
-        gq_ref[rows, :] = rope_back(joined, rows).astype(BF16)
+        gq_ref[rows, :] = rope_back(joined, cos_ref[rows, :], sin_ref[rows, :])
+
+
+def attend_back_kernel(
+    length_ref, q_ref, k_ref, v_ref, g_ref, cos_ref, sin_ref, gq_ref, gk_ref, gv_ref, acc_k, acc_v
+):
+    pair_index = pl.program_id(0)
+
+    @pl.when(pair_index == 0)
+    def _():
+        acc_k[...] = jnp.zeros_like(acc_k)
+        acc_v[...] = jnp.zeros_like(acc_v)
+
+    attend_back_pair(
+        length_ref[0], pair_index // 2, q_ref, k_ref, v_ref, g_ref, cos_ref, sin_ref, gq_ref,
+        acc_k, acc_v,
+    )
 
     @pl.when(pair_index == pl.num_programs(0) - 1)
     def _():
-        gk_ref[...] = rope_back(acc_k[...], slice(None)).astype(BF16)
+        gk_ref[...] = rope_back(acc_k[...], cos_ref[...], sin_ref[...])
         gv_ref[...] = acc_v[...].astype(BF16)
 
 
@@ -623,7 +640,7 @@
 
 
 def ring_scatter_dots(jobs, parts, count, collective_id, extra=None):
-    builder, given, made, spare = extra or (None, [], [], [])
+    builder, given, given_specs, made, spare = extra or (None, [], [], [], [])
     lefts, rights = [j[0] for j in jobs], [j[1] for j in jobs]
     rows = lefts[0].shape[0]
     items = tuple((l.shape[1] // count, r.shape[1] // 2) for l, r in jobs)
@@ -644,7 +661,7 @@
             (builder, len(given), len(made)) if extra else None,
         ),
         out_shape=[jax.ShapeDtypeStruct((b, 2 * h), F32) for b, h in items] + made,
-        in_specs=[pl.BlockSpec(memory_space=pl.ANY)] * (2 * num + len(given)),
+        in_specs=[pl.BlockSpec(memory_space=pl.ANY)] * (2 * num) + given_specs,
         out_specs=[pl.BlockSpec(memory_space=pl.ANY)] * (num + len(made)),
         scratch_shapes=[pltpu.VMEM((2, 2, rows, b), BF16) for b, _ in items]
         + [pltpu.VMEM(r.shape, BF16) for r in rights]
@@ -672,7 +689,8 @@
 
 class NormWork:
     def __init__(self, count, given, made, spare, rights):
-        self.grads, self.weights, self.down = given[:2], given[2:4], given[4]
+        self.grads, self.gates = given[:2], tuple(given[2:4])
+        self.up, self.down = given[4:]
         self.outs = made
         self.grad_bufs, self.row_bufs, self.down_bufs, self.stage = spare[0], *spare[1:4]
         self.grad_sems, self.row_sems, self.down_sems, self.out_sems = spare[4:]
@@ -690,13 +708,14 @@
 
     def loads(self, step):
         slot = step % 2
+        edge = self.gates[0].shape[1]
+        gate = self.row_bufs.at[0, slot]
+        targets = [gate.at[:, :edge], gate.at[:, edge:], self.row_bufs.at[1, slot]]
         rows = [
             pltpu.make_async_copy(
-                self.weights[which].at[self.spot(step), :],
-                self.row_bufs.at[which, slot],
-                self.row_sems.at[which, slot],
+                source.at[self.spot(step), :], target, self.row_sems.at[which, slot]
             )
-            for which in range(2)
+            for which, (source, target) in enumerate(zip(self.gates + (self.up,), targets))
         ]
         down = pltpu.make_async_copy(
             self.down.at[:, self.spot(step)], self.down_bufs.at[slot], self.down_sems.at[slot]
@@ -759,9 +778,9 @@
                 self.store(which, step).wait()
 
 
-def down_ring(grad_branch, activated, grad_gate, grad_up, gate_all, up_all, down_all, count, cid):
+def down_ring(grad_branch, activated, grad_gate, grad_up, gates, up_all, down_all, count, cid):
     rows, hidden = activated.shape
-    width = gate_all.shape[0]
+    width = up_all.shape[0]
     block = width // count
     wide = jax.ShapeDtypeStruct((rows, width), BF16)
     spare = [
@@ -770,21 +789,21 @@
         pltpu.VMEM((2, hidden, block), BF16),
         pltpu.VMEM((2, 2, rows, block), BF16),
         pltpu.SemaphoreType.DMA((2,)),
-        pltpu.SemaphoreType.DMA((2, 2)),
+        pltpu.SemaphoreType.DMA((3, 2)),
         pltpu.SemaphoreType.DMA((2,)),
         pltpu.SemaphoreType.DMA((2, 2)),
     ]
-    given = [grad_gate, grad_up, gate_all, up_all, down_all]
+    given = [grad_gate, grad_up, *gates, up_all, down_all]
     return ring_scatter_dots(
-        [(grad_branch, activated)], 2, count, cid, (NormWork, given, [wide, wide], spare)
+        [(grad_branch, activated)], 2, count, cid, (NormWork, given, [ANY] * 6, [wide, wide], spare)
     )
 
 
 def mlp_kernel(count, *refs):
-    x_hbm, wg_hbm, wu_hbm, shard, gb_hbm = refs[:5]
-    act_hbm, gg_hbm, gu_hbm, down_all = refs[5:9]
-    x_buf, gb_buf, w_bufs, gate_slope, up_slope, acc, half_bufs, stage, own_stage = refs[9:18]
-    send_sems, recv_sems, w_sems, in_sems, half_sems, out_sems, local_sem = refs[18:]
+    x_hbm, wg_hbm, wg_rest, wu_hbm, shard, gb_hbm = refs[:6]
+    act_hbm, gg_hbm, gu_hbm, down_all = refs[6:10]
+    x_buf, gb_buf, w_bufs, gate_slope, up_slope, acc, half_bufs, stage, own_stage = refs[10:19]
+    send_sems, recv_sems, w_sems, in_sems, half_sems, out_sems, local_sem = refs[19:]
     rows, width = x_buf.shape
     hidden = acc.shape[1]
     block = width // count
@@ -794,13 +813,27 @@
     parts = send_sems.shape[2]
     me = lax.axis_index("dp")
 
-    def load_weights(step, which):
-        source = (wg_hbm, wu_hbm)[which]
+    gate_steps = wg_hbm.shape[1] // cols
+
+    def load_weights(step, which, source=None):
+        start = step - gate_steps if source is wg_rest else step
+        source = (wg_hbm, wu_hbm)[which] if source is None else source
         return pltpu.make_async_copy(
-            source.at[:, pl.ds(pl.multiple_of(step * cols, cols), cols)],
+            source.at[:, pl.ds(pl.multiple_of(start * cols, cols), cols)],
             w_bufs.at[which, step % 2],
             w_sems.at[which, step % 2],
         )
+
+    def fetch(step):
+        load_weights(step, 1).start()
+
+        @pl.when(step < gate_steps)
+        def _():
+            load_weights(step, 0).start()
+
+        @pl.when(step >= gate_steps)
+        def _():
+            load_weights(step, 0, wg_rest).start()
 
     load_x = pltpu.make_async_copy(x_hbm, x_buf, in_sems.at[0])
     load_gb = pltpu.make_async_copy(gb_hbm, gb_buf, in_sems.at[1])
@@ -860,15 +893,22 @@
     def forward(step, carry):
         @pl.when(step + 1 < steps)
         def _():
-            for which in range(2):
-                load_weights(step + 1, which).start()
+            fetch(step + 1)
 
         @pl.when(step >= 2)
         def _():
             store(act_hbm, 0, step - 2).wait()
 
-        for which in range(2):
-            load_weights(step, which).wait()
+        load_weights(step, 1).wait()
+
+        @pl.when(step < gate_steps)
+        def _():
+            load_weights(step, 0).wait()
+
+        @pl.when(step >= gate_steps)
+        def _():
+            load_weights(step, 0, wg_rest).wait()
+
         here = pl.ds(pl.multiple_of(step * cols, cols), cols)
         for top in range(0, rows, 256):
             band = pl.ds(top, 256)
@@ -882,9 +922,9 @@
             up_slope[band, here] = silu
         store(act_hbm, 0, step).start()
 
-        turn = step // 2
-
-        @pl.when((step % 2 == 0) & (turn >= 1) & (turn <= count - 2))
+        turn = (step + 1) // 2
+
+        @pl.when((step % 2 == 1) & (turn <= count - 2))
         def _():
             pump(turn)
 
@@ -893,7 +933,7 @@
     lax.fori_loop(0, steps, forward, 0)
     for step in range(max(steps - 2, 0), steps):
         store(act_hbm, 0, step).wait()
-    pumped = min((steps - 1) // 2, count - 2)
+    pumped = min(steps // 2, count - 2)
     load_gb.wait()
 
     def load_half(step, side):
@@ -971,7 +1011,7 @@
     lax.fori_loop(0, count - 1, drain, 0)
 
 
-def mlp_ring(rows_mlp, gate_all, up_all, w_down, grad_branch, count, collective_id):
+def mlp_ring(rows_mlp, gates, up_all, w_down, grad_branch, count, collective_id):
     rows, width = rows_mlp.shape
     hidden, block = w_down.shape
     cols, parts = 256, 2
@@ -979,7 +1019,7 @@
     return pl.pallas_call(
         functools.partial(mlp_kernel, count),
         out_shape=[wide] * 3 + [jax.ShapeDtypeStruct((hidden, width), BF16)],
-        in_specs=[pl.BlockSpec(memory_space=pl.ANY)] * 5,
+        in_specs=[ANY] * 6,
         out_specs=[pl.BlockSpec(memory_space=pl.ANY)] * 4,
         scratch_shapes=[
             pltpu.VMEM((rows, width), BF16),
@@ -1008,7 +1048,293 @@
             transcendentals=rows * hidden,
         ),
         name="mlp_ring",
-    )(rows_mlp, gate_all, up_all, w_down, grad_branch)
+    )(rows_mlp, *gates, up_all, w_down, grad_branch)
+
+
+class HeadWork:
+    def __init__(self, count, given, made, spare, rights):
+        self.length, self.sources = given[0], given[1:]
+        self.grads_out, self.token_out = made
+        num = len(self.sources)
+        self.bufs = spare[:num]
+        self.heads, self.grads, self.acc_k, self.acc_v, self.stage = spare[num : num + 5]
+        self.in_sems, self.out_sems = spare[num + 5 :]
+
+    def load(self, which):
+        return pltpu.make_async_copy(
+            self.sources[which], self.bufs[which], self.in_sems.at[which]
+        )
+
+    def begin(self):
+        for which in range(len(self.sources)):
+            self.load(which).start()
+
+    def store(self, band):
+        rows = self.stage.shape[1]
+        return pltpu.make_async_copy(
+            self.stage.at[band % 2],
+            self.token_out.at[pl.ds(band * rows, rows), :],
+            self.out_sems.at[band % 2],
+        )
+
+    def store_grads(self):
+        return pltpu.make_async_copy(self.grads, self.grads_out, self.out_sems.at[2])
+
+    def tokens(self, bands):
+        w_query, w_key, w_value = self.bufs[7:]
+        rows = self.stage.shape[1]
+        inner = w_query.shape[1]
+        for band in bands:
+            if band >= 2:
+                self.store(band - 2).wait()
+            lines = slice(band * rows, (band + 1) * rows)
+            for left in range(0, w_query.shape[0], 512):
+                cols = slice(left, left + 512)
+                value = nt_dot(self.grads[lines, :inner], w_query[cols, :])
+                value += nt_dot(self.grads[lines, inner : inner + 128], w_key[cols, :])
+                value += nt_dot(self.grads[lines, inner + 128 :], w_value[cols, :])
+                self.stage[band % 2, :, cols] = value.astype(BF16)
+            self.store(band).start()
+
+    def compute(self, step):
+        grad_attn, w_output, queries, keys, values, cosine, sine = self.bufs[:7]
+        inner = queries.shape[1]
+        pairs = inner // 128
+        if isinstance(step, int):
+            if step == 0:
+                for which in range(len(self.sources)):
+                    self.load(which).wait()
+                for top in range(0, LEN, 256):
+                    rows = slice(top, top + 256)
+                    self.heads[rows, :] = nt_dot(grad_attn[rows, :], w_output[...]).astype(BF16)
+                self.acc_k[...] = jnp.zeros_like(self.acc_k)
+                self.acc_v[...] = jnp.zeros_like(self.acc_v)
+            return
+
+        @pl.when(step <= pairs)
+        def _():
+            here = pl.ds(pl.multiple_of((step - 1) * 128, 128), 128)
+            attend_back_pair(
+                self.length[0], (step - 1) // 2, queries.at[:, here], keys, values,
+                self.heads.at[:, here], cosine, sine, self.grads.at[:, here],
+                self.acc_k, self.acc_v,
+            )
+
+        @pl.when(step == pairs)
+        def _():
+            self.grads[:, inner : inner + 128] = rope_back(
+                self.acc_k[...], cosine[...], sine[...]
+            )
+            self.grads[:, inner + 128 :] = self.acc_v[...].astype(BF16)
+            self.store_grads().start()
+
+        @pl.when(step == pairs + 1)
+        def _():
+            self.tokens((0, 1))
+
+        @pl.when(step == pairs + 2)
+        def _():
+            self.tokens((2, 3))
+
+    def finish(self):
+        self.store_grads().wait()
+        for band in (2, 3):
+            self.store(band).wait()
+
+
+def heads_ring(job, lengths, grad_attn, w_output, qkv, tables, weights, count, collective_id):
+    given = [grad_attn, w_output, *qkv, *tables, *weights]
+    rows, width = grad_attn.shape
+    inner = qkv[0].shape[1]
+    made = [
+        jax.ShapeDtypeStruct((rows, inner + 256), BF16),
+        jax.ShapeDtypeStruct((rows, width), BF16),
+    ]
+    spare = [pltpu.VMEM(g.shape, g.dtype) for g in given] + [
+        pltpu.VMEM((rows, inner), BF16),
+        pltpu.VMEM((rows, inner + 256), BF16),
+        pltpu.VMEM((rows, 128), F32),
+        pltpu.VMEM((rows, 128), F32),
+        pltpu.VMEM((2, rows // 4, width), BF16),
+        pltpu.SemaphoreType.DMA((len(given),)),
+        pltpu.SemaphoreType.DMA((3,)),
+    ]
+    specs = [pl.BlockSpec(memory_space=pltpu.SMEM)] + [ANY] * len(given)
+    return ring_scatter_dots(
+        [job], 2, count, collective_id, (HeadWork, [lengths] + given, specs, made, spare)
+    )
+
+
+def attend_ring_kernel(count, *refs):
+    length_ref, shard, sources = refs[0], refs[1], refs[2:9]
+    gathered, q_out, k_out, v_out, head_out, part_out = refs[9:15]
+    bufs = refs[15:22]
+    q_buf, k_buf, v_buf, head_buf, stage, own = refs[22:28]
+    send_sems, recv_sems, in_sems, out_sems, local_sem = refs[28:]
+    rows_buf, w_query, w_key, w_value, w_output, cosine, sine = bufs
+    shape = shard.shape
+    me = lax.axis_index("dp")
+    loads = [
+        pltpu.make_async_copy(source, buf, in_sems.at[k])
+        for k, (source, buf) in enumerate(zip(sources, bufs))
+    ]
+    for load in loads:
+        load.start()
+    load_own = pltpu.make_async_copy(shard, own, local_sem)
+    load_own.start()
+    place, neighbours = ring_setup(count)
+
+    def hop(step, side):
+        ref = piece(gathered, shape, 0, member_at(place, side, step, count), side, 0, 1)
+        return pltpu.make_async_remote_copy(
+            src_ref=ref,
+            dst_ref=ref,
+            send_sem=send_sems.at[side, step],
+            recv_sem=recv_sems.at[side, step],
+            device_id={"dp": neighbours[side]},
+            device_id_type=MESH_ID,
+        )
+
+    for side in range(2):
+        pltpu.make_async_remote_copy(
+            src_ref=piece(shard, shape, None, 0, side, 0, 1),
+            dst_ref=piece(gathered, shape, 0, me, side, 0, 1),
+            send_sem=send_sems.at[side, 0],
+            recv_sem=recv_sems.at[side, 0],
+            device_id={"dp": neighbours[side]},
+            device_id_type=MESH_ID,
+        ).start()
+
+    def pump(step, carry=0):
+        for side in range(2):
+            hop(step - 1, side).wait_recv()
+            hop(step, side).start()
+        return carry
+
+    load_own.wait()
+    store_own = pltpu.make_async_copy(
+        own, gathered.at[pl.ds(pl.multiple_of(me * shape[0], shape[0]), shape[0]), :], local_sem
+    )
+    store_own.start()
+    for load in loads:
+        load.wait()
+
+    def projection(band, carry):
+        lines = pl.ds(pl.multiple_of(band * 256, 256), 256)
+        project_rows(
+            rows_buf[lines, :], w_query, w_key, w_value, cosine[lines, :], sine[lines, :],
+            q_buf.at[lines, :], k_buf.at[lines, :], v_buf.at[lines, :],
+        )
+        return carry
+
+    lax.fori_loop(0, LEN // 256, projection, 0)
+    stores = [
+        pltpu.make_async_copy(buf, out, out_sems.at[k])
+        for k, (buf, out) in enumerate(
+            ((q_buf, q_out), (k_buf, k_out), (v_buf, v_out), (head_buf, head_out))
+        )
+    ]
+    for store in stores[:3]:
+        store.start()
+    pump(1)
+    pairs = q_buf.shape[1] // 128
+
+    def attention(pair, carry):
+        here = pl.ds(pl.multiple_of(pair * 128, 128), 128)
+        attend_pair(
+            length_ref[0], pair // 2, q_buf.at[:, here], k_buf, v_buf, head_buf.at[:, here]
+        )
+
+        @pl.when(pair + 2 <= count - 2)
+        def _():
+            pump(pair + 2)
+
+        return carry
+
+    lax.fori_loop(0, pairs, attention, 0)
+    stores[3].start()
+
+    def store_part(band):
+        return pltpu.make_async_copy(
+            stage.at[band % 2],
+            part_out.at[pl.ds(pl.multiple_of(band * 256, 256), 256), :],
+            out_sems.at[4 + band % 2],
+        )
+
+    def output(band, carry):
+        @pl.when(band >= 2)
+        def _():
+            store_part(band - 2).wait()
+
+        lines = pl.ds(pl.multiple_of(band * 256, 256), 256)
+        for left in range(0, w_output.shape[1], 512):
+            cols = slice(left, left + 512)
+            stage[band % 2, :, cols] = jnp.dot(
+                head_buf[lines, :], w_output[:, cols], preferred_element_type=F32
+            ).astype(BF16)
+        store_part(band).start()
+        return carry
+
+    lax.fori_loop(0, LEN // 256, output, 0)
+    lax.fori_loop(min(pairs + 2, count - 1), count - 1, pump, 0)
+    for band in (LEN // 256 - 2, LEN // 256 - 1):
+        store_part(band).wait()
+    for store in stores:
+        store.wait()
+    store_own.wait()
+    for side in range(2):
+        hop(count - 2, side).wait_recv()
+
+    def drain(step, carry):
+        for side in range(2):
+            hop(step, side).wait_send()
+        return carry
+
+    lax.fori_loop(0, count - 1, drain, 0)
+
+
+def attend_ring(shard, lengths, rows_attn, weights, tables, count, collective_id):
+    sources = [rows_attn, *weights, *tables]
+    rows, width = rows_attn.shape
+    inner = weights[0].shape[1]
+
+    def low(*shape):
+        return jax.ShapeDtypeStruct(shape, BF16)
+
+    return pl.pallas_call(
+        functools.partial(attend_ring_kernel, count),
+        out_shape=[
+            low(shard.shape[0] * count, shard.shape[1]),
+            low(rows, inner),
+            low(rows, 128),
+            low(rows, 128),
+            low(rows, inner),
+            low(rows, width),
+        ],
+        in_specs=[pl.BlockSpec(memory_space=pltpu.SMEM)] + [ANY] * (1 + len(sources)),
+        out_specs=[ANY] * 6,
+        scratch_shapes=[pltpu.VMEM(source.shape, source.dtype) for source in sources]
+        + [
+            pltpu.VMEM((rows, inner), BF16),
+            pltpu.VMEM((rows, 128), BF16),
+            pltpu.VMEM((rows, 128), BF16),
+            pltpu.VMEM((rows, inner), BF16),
+            pltpu.VMEM((2, 256, width), BF16),
+            pltpu.VMEM(shard.shape, BF16),
+            pltpu.SemaphoreType.DMA((2, count - 1)),
+            pltpu.SemaphoreType.DMA((2, count - 1)),
+            pltpu.SemaphoreType.DMA((len(sources),)),
+            pltpu.SemaphoreType.DMA((6,)),
+            pltpu.SemaphoreType.DMA,
+        ],
+        compiler_params=pltpu.CompilerParams(
+            collective_id=collective_id, has_side_effects=True, vmem_limit_bytes=56 << 20
+        ),
+        cost_estimate=pl.CostEstimate(
+            flops=24 << 30, bytes_accessed=60 << 20, transcendentals=8 << 20
+        ),
+        name="attend_ring",
+    )(lengths, shard, *sources)
 
 
 def ring_weight_grads(jobs, parts, count, collective_id):
@@ -1149,23 +1475,40 @@
         (0, 0, 0, 1), (1, 1, 1, 1), count, 0,
     )
     grad_branch = gather_rows(after(cot_masked.astype(BF16), rows_attn))
-    queries, keys, values = project(rows_attn, query_all, key_all, value_all, cosine, sine)
-    head_out = attend(queries, keys, values, lengths)
-    attn_part = dot(head_out, output_all).astype(BF16)
+    fused = count == 8
+    edge = 3 * w_gate.shape[1] // 8
+    gates = []
+    if fused:
+        first_gate, queries, keys, values, head_out, attn_part = attend_ring(
+            w_gate[:, :edge],
+            lengths,
+            rows_attn,
+            (query_all, key_all, value_all, output_all),
+            (cosine, sine),
+            count,
+            9,
+        )
+        gates.append(first_gate)
+    else:
+        queries, keys, values = project(rows_attn, query_all, key_all, value_all, cosine, sine)
+        head_out = attend(queries, keys, values, lengths)
+        attn_part = dot(head_out, output_all).astype(BF16)
     attn_branch = scatter_rows(attn_part)
-    (gate_all,) = ring_gather([after(w_gate, attn_part)], (0,), (2,), count, 1)
+    rest = w_gate[:, edge:] if fused else w_gate
+    (gate_all,) = ring_gather([after(rest, attn_part)], (0,), (2,), count, 1)
+    gates.append(gate_all)
     hidden = token_full + attn_branch
     inv_second = lax.rsqrt(jnp.mean(hidden * hidden, axis=1, keepdims=True) + epsilon)
     normed_mlp = (hidden * inv_second * gain_mlp).astype(BF16)
     normed_mlp = after(normed_mlp, gate_all)
     rows_mlp = gather_rows(normed_mlp)
     (up_all,) = ring_gather([after(w_up, normed_mlp)], (0,), (2,), count, 2)
-    if w_down.shape[1] % 128 == 0:
+    if fused:
         activated, grad_gate_pre, grad_up_pre, down_all = mlp_ring(
-            rows_mlp, gate_all, after(up_all, rows_mlp), w_down, grad_branch, count, 3
+            rows_mlp, gates, after(up_all, rows_mlp), w_down, grad_branch, count, 3
         )
         grad_down, norm_part, mlp_part = down_ring(
-            grad_branch, activated, grad_gate_pre, grad_up_pre, gate_all, up_all, down_all,
+            grad_branch, activated, grad_gate_pre, grad_up_pre, gates, up_all, down_all,
             count, 4,
         )
     else:
@@ -1186,8 +1529,6 @@
     (grad_gate,) = ring_weight_grads(
         [(after(rows_mlp, norm_part), grad_gate_pre)], 2, count, 5
     )
-    mlp_branch = scatter_rows(after(mlp_part, grad_norm_two, grad_gate))
-    layer_out = (hidden + mlp_branch).astype(BF16)
     scaled_two = grad_norm_two * gain_mlp
     gain_two_part = jnp.sum(grad_norm_two * hidden * inv_second, axis=0)
     grad_hidden = (
@@ -1197,18 +1538,43 @@
     )
     grad_hidden = after(grad_hidden, grad_gate)
     grad_attn = gather_rows(grad_hidden.astype(BF16))
-    (grad_up,) = ring_weight_grads(
-        [(after(rows_mlp, grad_hidden), grad_up_pre)], 2, count, 6
+    mlp_branch = scatter_rows(after(mlp_part, grad_hidden))
+    if fused:
+        middle = grad_up_pre.shape[1] // 2
+        (up_left,) = ring_weight_grads(
+            [(after(rows_mlp, grad_hidden), grad_up_pre[:, :middle])], 2, count, 6
+        )
+        up_right, grad_qkv, token_part = heads_ring(
+            (rows_mlp, grad_up_pre[:, middle:]),
+            lengths,
+            after(grad_attn, up_left),
+            output_all,
+            (queries, keys, values),
+            (cosine, sine),
+            (query_all, key_all, value_all),
+            count,
+            10,
+        )
+        grad_up = jnp.concatenate([up_left, up_right], axis=1)
+    else:
+        (grad_up,) = ring_weight_grads(
+            [(after(rows_mlp, grad_hidden), grad_up_pre)], 2, count, 6
+        )
+        grad_heads = nt_dot(after(grad_attn, grad_up), output_all).astype(BF16)
+        grad_qpre, grad_kpre, grad_vpre = attend_back(
+            queries, keys, values, grad_heads, lengths, cosine, sine
+        )
+        token_part = (
+            nt_dot(grad_qpre, query_all)
+            + nt_dot(grad_kpre, key_all)
+            + nt_dot(grad_vpre, value_all)
+        ).astype(BF16)
+        grad_qkv = jnp.concatenate([grad_qpre, grad_kpre, grad_vpre], axis=1)
+    layer_out = (hidden + after(mlp_branch, token_part)).astype(BF16)
+    grad_norm_one = scatter_rows(token_part)
+    attn_grads, grad_output = ring_weight_grads(
+        [(after(rows_attn, token_part), grad_qkv), (grad_attn, head_out)], 1, count, 7
     )
-    grad_heads = nt_dot(after(grad_attn, grad_up), output_all).astype(BF16)
-    grad_qpre, grad_kpre, grad_vpre = attend_back(
-        queries, keys, values, grad_heads, lengths, cosine, sine
-    )
-    token_part = (
-        nt_dot(grad_qpre, query_all) + nt_dot(grad_kpre, key_all) + nt_dot(grad_vpre, value_all)
-    ).astype(BF16)
-    grad_norm_one = scatter_rows(token_part)
-    grad_qkv = jnp.concatenate([grad_qpre, grad_kpre, grad_vpre], axis=1)
     scaled_one = grad_norm_one * gain_attn
     gain_one_part = jnp.sum(grad_norm_one * token_full * inv_first, axis=0)
     grad_tokens = (
@@ -1216,13 +1582,10 @@
         + inv_first * scaled_one
         - token_full * inv_first**3 * jnp.mean(scaled_one * token_full, axis=1, keepdims=True)
     )
-    attn_grads, grad_output = ring_weight_grads(
-        [(after(rows_attn, token_part), grad_qkv), (grad_attn, head_out)], 1, count, 7
-    )
     grad_attn_gain, grad_mlp_gain = sum_shares(
         after(gain_one_part, attn_grads), gain_two_part, count, group, 8
     )
-    query_cols, key_cols = grad_qpre.shape[1], grad_kpre.shape[1]
+    query_cols, key_cols = queries.shape[1], keys.shape[1]
     grad_query = attn_grads[:, :query_cols]
     grad_key = attn_grads[:, query_cols : query_cols + key_cols]
     grad_value = attn_grads[:, query_cols + key_cols :]

time: 818 us -> 715 us (0.87)
  Pallas kernels: 685 us -> 642 us
  waiting for transfers between devices: 42.3 us -> 0.92 us
  matrix products: 16.6 us -> 0 us
    reduce_scatter x4, waiting for transfers between devices: 42 us -> 0.05 us  [scatter_rows(): lax.psum_scatter(value.astype(BF16), 'tensor', scatter_dimension=0, tiled...]
    pallas_call x3, Pallas kernels: 218 us -> 182 us  [ring_gather(): pl.pallas_call(functools.partial(gather_kernel, count, items), out_shape=...]
    dot_general x5 -> x0, matrix products: 16.6 us -> none  [the longest x4 12.2 us: nt_dot(): lax.dot_general(left, right, (((1,), (1,)), ((), ())), preferred_element_...]
    pallas_call x3 -> x1, Pallas kernels: 50.3 us -> 47 us  [attend_ring(): pl.pallas_call(functools.partial(attend_ring_kernel, count), out_shape=[l...]
    pallas_call x4 -> x5, Pallas kernels: 307 us -> 306 us  [ring_scatter_dots(): pl.pallas_call(functools.partial(scatter_dot_kernel, count, items, parts,...]
  transfers between devices with their start and end apart: 8 -> 8, of which waited for: 1 -> 0; matrix products, arithmetic and copies ran while one was open for 2% -> 3% of each run, Pallas kernels for 54% -> 57%
where the time goes in v3:
time: 715 us; the launch traced here: 707 us
  Pallas kernels  642 us (90%)
  other arithmetic  28.3 us (4%)
  local copies, waits for them, and re-layouts  20.2 us (3%)
  between operations  15.5 us (2%)
    pallas_call x5, Pallas kernels, ring_scatter_dots(): pl.pallas_call(functools.partial(scatter_dot_kernel, count, items, parts,...  306 us
    pallas_call x3, Pallas kernels, ring_gather(): pl.pallas_call(functools.partial(gather_kernel, count, items), out_shape=...  182 us
    pallas_call x1, Pallas kernels, mlp_ring(): pl.pallas_call(functools.partial(mlp_kernel, count), out_shape=[wide] * 3...  96.6 us
    pallas_call x1, Pallas kernels, attend_ring(): pl.pallas_call(functools.partial(attend_ring_kernel, count), out_shape=[l...  47 us
  transfers between devices with their start and end apart: 8, of which 0 were waited for; matrix products, arithmetic and copies ran while one was open for 3% of the time, Pallas kernels for 57%

profile of v3, /device:TPU:0, one launch (start us, length us, event | category | flops | bytes accessed | tf_op | source)
XLA Modules:
  0.0 707.0 jit_solution(8593334034636193786)
XLA Ops:
  7.2 0.0 all-gather.5.cloned.1.call-start
  7.2 1.6 fusion.10
  8.8 0.7 convert_element_type.49
  9.5 2.5 fusion.12
  12.0 0.0 all-gather.5.cloned.1.call-update
  12.1 0.0 reduce-scatter.5.cloned.1.call-start
  12.8 0.8 slice.27.refs_1_
  13.5 55.6 %ring_gather_0.1 = (bf16[2048,512]{1,0:T(8,128)(2,1)}, bf16[2048,128]{1,0:T(8,128)(2,1)}, bf16[2048,128]{1,0:T(8,128)(2,1)}, bf16[512,2048]{1,0:T(8,128)(2,1)}) custom-call(bf16[256,512]{1,0:T(8,128)(2,1)} %refs_0_.1, bf16[256,128]{1,0:T(8,128)(2,1)} %refs_1_.1, bf16[256,128]{1,0:T(8,128)(2,1)} %refs_2_.2, bf16[512,256]{1,0:T(8,128)(2,1)} %refs_3_.1), custom_call_target="tpu_custom_call" | custom-call | bytes 91750400 | tf_op jit(solution)/shard_map/ring_gather_0/pallas_call | solution.py:364
  69.2 2.0 fusion.20
  71.2 1.8 pad_maximum_fusion.1
  73.0 47.0 %attend_ring.1 = (bf16[2048,768]{1,0:T(8,128)(2,1)}, bf16[1024,512]{1,0:T(8,128)(2,1)}, bf16[1024,128]{1,0:T(8,128)(2,1)}, bf16[1024,128]{1,0:T(8,128)(2,1)}, bf...) custom-call(s32[1]{0:T(128)} %copy.29.refs_0_.refs_2_, bf16[256,768]{1,0:T(8,128)(2,1)} %slice.27.refs_1_, ...), custom_call_target="tpu_custom_call" | custom-call | flops 25769803776 | bytes 62914560 | tf_op jit(solution)/shard_map/attend_ring/pallas_call | solution.py:1304
  120.1 0.0 copy-start.10
  120.1 0.0 reduce-scatter.5.cloned.1.call-update
  120.1 0.0 all-gather.9.cloned.1.call-start
  120.2 0.9 slice.28.refs_0_
  121.1 48.8 %ring_gather_1.1.refs_2_.refs_5_ = bf16[2048,1280]{1,0:T(8,128)(2,1)} custom-call(bf16[256,1280]{1,0:T(8,128)(2,1)} %slice.28.refs_0_), custom_call_target="tpu_custom_call" | custom-call | bytes 91750400 | tf_op jit(solution)/shard_map/ring_gather_1/pallas_call | solution.py:364
  169.9 0.0 reduce-scatter.5.cloned.1.call-done
  169.9 1.7 multiply_reduce_fusion
  171.7 0.0 copy-start.3
  171.7 1.5 multiply_convert_fusion
  173.2 0.0 all-gather.9.cloned.1.call-update
  173.2 0.0 all-gather.7.cloned.1.call-start
  173.3 1.2 fusion.17
  174.5 0.0 all-gather.7.cloned.1.call-update
  174.5 0.3 reduce-scatter.7.cloned.1.call-start
  174.8 78.0 %ring_gather_2.1.refs_3_.refs_6_ = bf16[2048,2048]{1,0:T(8,128)(2,1)} custom-call(bf16[256,2048]{1,0:T(8,128)(2,1)} %refs_0_.2), custom_call_target="tpu_custom_call" | custom-call | bytes 146800640 | tf_op jit(solution)/shard_map/ring_gather_2/pallas_call | solution.py:364
  252.8 0.0 all-gather.9.cloned.1.call-done.refs_0_
  252.8 0.0 all-gather.7.cloned.1.call-done.refs_5_.refs_0_
  252.8 96.6 %mlp_ring.1 = (bf16[1024,2048]{1,0:T(8,128)(2,1)}, bf16[1024,2048]{1,0:T(8,128)(2,1)}, bf16[1024,2048]{1,0:T(8,128)(2,1)}, bf16[2048,2048]{1,0:T(8,128)(2,1)}) custom-call(bf16[1024,2048]{1,0:T(8,128)(2,1)} %all-gather.9.cloned.1.call-done.refs_0_, bf16[2048,768]{1,0:T(8,128)(2,1)} %get-tuple-element.56.refs_1_.refs_4_, ...), custom_call_target="tpu_custom_call" | custom-call | flops 25769803776 | bytes 167772160 | tf_op jit(solution)/shard_map/mlp_ring/pallas_call | solution.py:1019
  349.4 84.5 %ring_scatter_4.1 = (f32[256,2048]{1,0:T(8,128)}, bf16[1024,2048]{1,0:T(8,128)(2,1)}, bf16[1024,2048]{1,0:T(8,128)(2,1)}) custom-call(bf16[1024,2048]{1,0:T(8,128)(2,1)} %all-gather.7.cloned.1.call-done.refs_5_.refs_0_, bf16[1024,2048]{1,0:T(8,128)(2,1)} %get-tuple-element.59.refs_1_, bf16[1024,2048]{1,0:T(8,128)(2,1)} %get-tuple-element.60.refs_2_.refs_1_, ...), custom_call_target="tpu_custom_call" | custom-call | flops 8589934592 | bytes 167772160 | tf_op jit(solution)/shard_map/ring_scatter_4/pallas_call | solution.py:655
  433.9 0.0 reduce-scatter.7.cloned.1.call-update
  434.0 0.0 all-gather.11.cloned.1.call-start
  434.0 74.2 %ring_scatter_5.1 = f32[256,2048]{1,0:T(8,128)} custom-call(bf16[1024,2048]{1,0:T(8,128)(2,1)} %all-gather.9.cloned.1.call-done.refs_0_, bf16[1024,2048]{1,0:T(8,128)(2,1)} %get-tuple-element.60.refs_2_.refs_1_), custom_call_target="tpu_custom_call" | custom-call | flops 8589934592 | bytes 167772160 | tf_op jit(solution)/shard_map/ring_scatter_5/pallas_call | solution.py:655
  508.2 0.0 reduce-scatter.7.cloned.1.call-done
  508.3 2.0 fusion.9
  510.3 0.9 fusion.6
  511.2 0.0 copy-start.2
  511.2 1.3 copy-done.2
  512.5 1.1 convert_element_type.59
  513.6 0.0 all-gather.11.cloned.1.call-update
  513.7 0.0 reduce-scatter.9.cloned.1.call-start
  513.7 0.7 reduce-scatter.9.cloned.1.call-update
  514.4 0.0 reduce-scatter.11.cloned.1.call-start
  514.5 4.7 fusion.21
  519.1 40.9 %ring_scatter_6.1 = f32[256,1024]{1,0:T(8,128)} custom-call(bf16[1024,2048]{1,0:T(8,128)(2,1)} %all-gather.9.cloned.1.call-done.refs_0_, bf16[1024,1024]{1,0:T(8,128)(2,1)} %get-tuple-element.109.refs_1_), custom_call_target="tpu_custom_call" | custom-call | flops 4294967296 | bytes 83886080 | tf_op jit(solution)/shard_map/ring_scatter_6/pallas_call | solution.py:655
  560.0 0.0 all-gather.11.cloned.1.call-done.refs_3_.refs_1_
  560.1 59.0 %ring_scatter_10.1 = (f32[256,1024]{1,0:T(8,128)}, bf16[1024,768]{1,0:T(8,128)(2,1)}, bf16[1024,2048]{1,0:T(8,128)(2,1)}) custom-call(bf16[1024,2048]{1,0:T(8,128)(2,1)} %all-gather.9.cloned.1.call-done.refs_0_, bf16[1024,1024]{1,0:T(8,128)(2,1)} %get-tuple-element.110.refs_1_, s32[1]{0:T(128)} %copy.29.refs_0_.refs_2_, ...), custom_call_target="tpu_custom_call" | custom-call | flops 4294967296 | bytes 83886080 | tf_op jit(solution)/shard_map/ring_scatter_10/pallas_call | solution.py:655
  619.0 0.0 reduce-scatter.11.cloned.1.call-update
  619.1 3.1 copy.27
  622.2 0.1 stack.10
  622.3 47.0 %ring_scatter_7.1 = (f32[256,768]{1,0:T(8,128)}, f32[256,512]{1,0:T(8,128)}) custom-call(bf16[1024,2048]{1,0:T(8,128)(2,1)} %all-gather.5.cloned.1.call-done.refs_2_.refs_0_, bf16[1024,2048]{1,0:T(8,128)(2,1)} %all-gather.11.cloned.1.call-done.refs_3_.refs_1_, bf16[1024,768]{1,0:T(8,128)(2,1)} %get-tuple-element.76.refs_2_, ...), custom_call_target="tpu_custom_call" | custom-call | flops 5368709120 | bytes 104857600 | tf_op jit(solution)/shard_map/ring_scatter_7/pallas_call | solution.py:655
  669.3 2.1 copy.26
  671.4 2.0 slice.31
  673.4 1.7 fusion.22
  675.1 1.5 pad_maximum_fusion
  676.5 2.8 convert_element_type.58
  679.3 2.0 fusion.16
  681.3 0.1 stack.9
  681.4 0.1 reshape.97
  681.5 0.7 pad.4.parts_ref
  682.2 9.9 %sum_shares.1 = f32[8,128]{1,0:T(8,128)} custom-call(f32[4,8,8,128]{3,2,1,0:T(8,128)} %pad.4.parts_ref), custom_call_target="tpu_custom_call" | custom-call | tf_op jit(solution)/shard_map/sum_shares/pallas_call | solution.py:1424
  692.1 1.3 slice_bitcast_fusion
  693.5 4.9 fusion.4
  698.4 1.3 copy.30
  (30 shorter events, 0.1 us)
Async XLA Ops:
  7.2 5.6 copy-start.7
  7.2 65.9 %all-gather.5.cloned.1.call-start = ((), (), s32[]{:S(2)}) async-start(), calls=%async_computation.4 | async-start | bytes 5242880 | tf_op jit(solution)/shard_map/all_gather | solution.py:1353
  12.1 157.8 %reduce-scatter.5.cloned.1.call-start = ((), (), s32[]{:S(2)}) async-start(), calls=%async_computation.5 | async-start | bytes 5242880 | tf_op jit(solution)/shard_map/reduce_scatter | solution.py:1357
  120.1 1.0 copy-start.10
  120.1 132.7 %all-gather.9.cloned.1.call-start = ((), (), s32[]{:S(2)}) async-start(), calls=%async_computation.7 | async-start | bytes 5242880 | tf_op jit(solution)/shard_map/all_gather | solution.py:1353
  121.1 48.8 %copy-start = (bf16[256,2048]{1,0:T(8,128)(2,1)S(1)}, bf16[256,2048]{1,0:T(8,128)(2,1)}, u32[]{:S(2)}) copy-start(bf16[256,2048]{1,0:T(8,128)(2,1)} %param.12) | copy-start | bytes 3145732
  169.9 1.8 copy-start.1
  171.7 1.6 copy-start.3
  173.2 79.6 %all-gather.7.cloned.1.call-start = ((), (), s32[]{:S(2)}) async-start(), calls=%async_computation.6 | async-start | bytes 5242880 | tf_op jit(solution)/shard_map/all_gather | solution.py:1353
  174.5 333.8 %reduce-scatter.7.cloned.1.call-start = ((), (), s32[]{:S(2)}) async-start(), calls=%async_computation.8 | async-start | bytes 5242880 | tf_op jit(solution)/shard_map/reduce_scatter | solution.py:1357
  434.0 126.1 %all-gather.11.cloned.1.call-start = ((), (), s32[]{:S(2)}) async-start(), calls=%async_computation.10 | async-start | bytes 5242880 | tf_op jit(solution)/shard_map/all_gather | solution.py:1353
  508.3 2.1 copy-start.4
  511.2 1.3 copy-start.2
  513.7 162.9 %reduce-scatter.9.cloned.1.call-start = ((), (), s32[]{:S(2)}) async-start(), calls=%async_computation.9 | async-start | bytes 5242880 | tf_op jit(solution)/shard_map/reduce_scatter | solution.py:1357
  514.4 164.9 %reduce-scatter.11.cloned.1.call-start = ((), (), s32[]{:S(2)}) async-start(), calls=%async_computation.11 | async-start | bytes 5242880 | tf_op jit(solution)/shard_map/reduce_scatter | solution.py:1357
  669.3 5.8 copy-start.8
  671.4 3.6 copy-start.9
  679.3 14.1 %copy-start.5 = (bf16[256,2048]{1,0:T(8,128)(2,1)S(1)}, bf16[256,2048]{1,0:T(8,128)(2,1)}, u32[]{:S(2)}) copy-start(bf16[256,2048]{1,0:T(8,128)(2,1)} %reduce-scatter.11.cloned.1.call-done) | copy-start | bytes 3145732
  693.5 4.9 copy-start.6
Sparse Core Ops, SparseCore 0:
  12.2 37.1 all-gather.4
  120.2 43.5 reduce-scatter.4
  173.3 32.8 all-gather.8
  208.2 34.4 all-gather.6
  434.1 43.8 reduce-scatter.6
  513.8 32.6 all-gather.10
  549.0 44.6 reduce-scatter.8
  619.2 42.9 reduce-scatter.10

commit v4 on v3

--- a/solution.py
+++ b/solution.py
@@ -1,4 +1,5 @@
 import functools
+from typing import Any, NamedTuple
 
 import jax
 import jax.numpy as jnp
@@ -31,12 +32,15 @@
 
 
 def rope_tables():
-    angles = jnp.arange(LEN, dtype=jnp.float32)[:, None] * rope_frequencies()[None, :]
-    cosine, sine = jnp.cos(angles), jnp.sin(angles)
-    return (
-        jnp.concatenate([cosine] * 4, axis=1),
-        jnp.concatenate([-sine, sine, -sine, sine], axis=1),
-    )
+    steps = jnp.arange(32, dtype=jnp.float32)[:, None]
+    frequency = jnp.concatenate([rope_frequencies()] * 4)[None, :]
+    low, high = steps * frequency, (32.0 * steps) * frequency
+    cos_low, sin_low = jnp.cos(low)[None, :, :], jnp.sin(low)[None, :, :]
+    cos_high, sin_high = jnp.cos(high)[:, None, :], jnp.sin(high)[:, None, :]
+    sign = jnp.where(jnp.arange(128) % HD < HD // 2, -1.0, 1.0)
+    cosine = cos_high * cos_low - sin_high * sin_low
+    sine = (sin_high * cos_low + cos_high * sin_low) * sign
+    return cosine.reshape(LEN, 128), sine.reshape(LEN, 128)
 
 
 def lane_index(shape):
@@ -121,21 +125,38 @@
 
 
 def attend_pair(length, kv, q_ref, k_ref, v_ref, o_ref):
+    square = (QB, QB)
+    causal = lax.broadcasted_iota(jnp.int32, square, 1) <= lax.broadcasted_iota(
+        jnp.int32, square, 0
+    )
+    bias = jnp.where(lane_index((1, LEN)) < length, 0.0, -1e30)
     for block in range(LEN // QB):
-        rows = slice(block * QB, (block + 1) * QB)
-        keys = (block + 1) * QB
-        pair = q_ref[rows, :].astype(F32) * HD**-0.5
-        query_pos = block * QB + lax.broadcasted_iota(jnp.int32, (QB, keys), 0)
-        key_pos = lax.broadcasted_iota(jnp.int32, (QB, keys), 1)
-        allowed = (key_pos <= query_pos) & (key_pos < length)
+        start = block * QB
+        here = slice(start, start + QB)
+        pair = q_ref[here, :].astype(F32) * HD**-0.5
         outs = []
         for which in range(2):
             query = pick_head(pair, which, kv).astype(BF16)
-            scores = jnp.where(allowed, nt_dot(query, k_ref[:keys, :]), -1e30)
-            exps = jnp.exp(scores - jnp.max(scores, axis=1, keepdims=True))
-            probs = (exps / jnp.sum(exps, axis=1, keepdims=True)).astype(BF16)
-            outs.append(jnp.dot(probs, v_ref[:keys, :], preferred_element_type=F32))
-        o_ref[rows, :] = join_heads(outs[0], outs[1], kv).astype(BF16)
+            near = jnp.where(causal, nt_dot(query, k_ref[here, :]), -1e30) + bias[:, here]
+            top = jnp.max(near, axis=1, keepdims=True)
+            if start:
+                far = nt_dot(query, k_ref[:start, :]) + bias[:, :start]
+                top = jnp.maximum(top, jnp.max(far, axis=1, keepdims=True))
+                far = jnp.exp(far - top)
+            near = jnp.exp(near - top)
+            total = jnp.sum(near, axis=1, keepdims=True)
+            if start:
+                total = total + jnp.sum(far, axis=1, keepdims=True)
+            inverse = 1.0 / total
+            out = jnp.dot(
+                (near * inverse).astype(BF16), v_ref[here, :], preferred_element_type=F32
+            )
+            if start:
+                out = out + jnp.dot(
+                    (far * inverse).astype(BF16), v_ref[:start, :], preferred_element_type=F32
+                )
+            outs.append(out)
+        o_ref[here, :] = join_heads(outs[0], outs[1], kv).astype(BF16)
 
 
 def attend_kernel(length_ref, q_ref, k_ref, v_ref, o_ref):
@@ -178,7 +199,7 @@
             grad = pick_head(grad_pair, which, kv).astype(BF16)
             scores = jnp.where(allowed, nt_dot(key_vecs, query), -1e30)
             exps = jnp.exp(scores - jnp.max(scores, axis=0, keepdims=True))
-            probs = exps / jnp.sum(exps, axis=0, keepdims=True)
+            probs = exps * (1.0 / jnp.sum(exps, axis=0, keepdims=True))
             grad_probs = nt_dot(v_ref[:keys, :], grad)
             inner = jnp.sum(probs * grad_probs, axis=0, keepdims=True)
             grad_scores = (probs * (grad_probs - inner)).astype(BF16)
@@ -241,14 +262,15 @@
     return (1 - high) * (2 * place) + high * (2 * (count - 1 - place) + 1)
 
 
-def ring_setup(count):
+def ring_setup(count, peers=None):
     place = ring_place(lax.axis_index("dp"), count)
     ahead = ring_member((place + 1) % count, count)
     behind = ring_member((place + count - 1) % count, count)
     barrier = pltpu.get_barrier_semaphore()
-    for other in (ahead, behind):
-        pl.semaphore_signal(barrier, inc=1, device_id={"dp": other}, device_id_type=MESH_ID)
-    pl.semaphore_wait(barrier, 2)
+    peers = peers or [{"dp": ahead}, {"dp": behind}]
+    for other in peers:
+        pl.semaphore_signal(barrier, inc=1, device_id=other, device_id_type=MESH_ID)
+    pl.semaphore_wait(barrier, len(peers))
     return place, (ahead, behind)
 
 
@@ -258,12 +280,12 @@
     return ring_member((place + steps) % count, count)
 
 
-def piece(ref, shape, axis, member, side, part, parts):
+def piece(ref, shape, axis, member, side, part, parts, first=0):
     rows, cols = shape
     sub = rows // (2 * parts)
     start = (side * parts + part) * sub
     if axis is None:
-        return ref.at[pl.ds(start, sub), :]
+        return ref.at[pl.ds(start, sub), first : first + cols]
     if axis == 0:
         return ref.at[pl.ds(pl.multiple_of(member * rows + start, sub), sub), :]
     return ref.at[pl.ds(start, sub), pl.ds(pl.multiple_of(member * cols, cols), cols)]
@@ -280,7 +302,7 @@
 
     def copy(step, side, slot):
         item, part = slots[slot]
-        shape, axis, parts = items[item]
+        shape, axis, parts, _ = items[item]
         origin = member_at(place, side, step, count)
         target = piece(outs[item], shape, axis, origin, side, part, parts)
         return target, pltpu.make_async_remote_copy(
@@ -293,10 +315,10 @@
         )
 
     for slot, (item, part) in enumerate(slots):
-        shape, axis, parts = items[item]
+        shape, axis, parts, first = items[item]
         for side in range(2):
             pltpu.make_async_remote_copy(
-                src_ref=piece(shards[item], shape, None, 0, side, part, parts),
+                src_ref=piece(shards[item], shape, None, 0, side, part, parts, first),
                 dst_ref=piece(outs[item], shape, axis, me, side, part, parts),
                 send_sem=send_sems.at[side, 0, slot],
                 recv_sem=recv_sems.at[side, 0, slot],
@@ -304,14 +326,19 @@
                 device_id_type=MESH_ID,
             ).start()
     loads = [
-        pltpu.make_async_copy(shards[k], stage[k], local_sem.at[k]) for k in range(num)
+        pltpu.make_async_copy(
+            shards[k].at[:, items[k][3] : items[k][3] + items[k][0][1]],
+            stage[k],
+            local_sem.at[k],
+        )
+        for k in range(num)
     ]
     for load in loads:
         load.start()
     stores = []
     for k in range(num):
         loads[k].wait()
-        shape, axis, parts = items[k]
+        shape, axis, parts, _ = items[k]
         rows, cols = shape
         if axis == 0:
             own = outs[k].at[pl.ds(pl.multiple_of(me * rows, rows), rows), :]
@@ -343,21 +370,19 @@
     lax.fori_loop(0, count - 1, drain, 0)
 
 
-def ring_gather(shards, axes, parts, count, collective_id):
+def ring_gather(shards, axes, parts, count, collective_id, first=0):
     turned = [a == 1 and s.shape[1] % 128 != 0 for s, a in zip(shards, axes)]
     if any(turned):
         shards = [s.T if t else s for s, t in zip(shards, turned)]
         axes = [0 if t else a for a, t in zip(axes, turned)]
         outs = ring_gather(shards, axes, parts, count, collective_id)
         return [o.T if t else o for o, t in zip(outs, turned)]
-    items = tuple((s.shape, a, q) for s, a, q in zip(shards, axes, parts))
+    shapes = [(s.shape[0], s.shape[1] - first) for s in shards]
+    items = tuple((s, a, q, first) for s, a, q in zip(shapes, axes, parts))
     slots = sum(parts)
     outs = [
-        jax.ShapeDtypeStruct(
-            (s.shape[0] * count, s.shape[1]) if a == 0 else (s.shape[0], s.shape[1] * count),
-            s.dtype,
-        )
-        for s, a in zip(shards, axes)
+        jax.ShapeDtypeStruct((s[0] * count, s[1]) if a == 0 else (s[0], s[1] * count), BF16)
+        for s, a in zip(shapes, axes)
     ]
     num = len(shards)
     nbytes = sum(s.size * 2 * (count - 1) for s in shards)
@@ -366,7 +391,7 @@
         out_shape=outs,
         in_specs=[pl.BlockSpec(memory_space=pl.ANY)] * num,
         out_specs=[pl.BlockSpec(memory_space=pl.ANY)] * num,
-        scratch_shapes=[pltpu.VMEM(s.shape, s.dtype) for s in shards]
+        scratch_shapes=[pltpu.VMEM(s, BF16) for s in shapes]
         + [
             pltpu.SemaphoreType.DMA((2, count - 1, slots)),
             pltpu.SemaphoreType.DMA((2, count - 1, slots)),
@@ -513,27 +538,52 @@
     )(*partials)
 
 
-def scatter_dot_kernel(count, items, parts, extra, *refs):
+class Job(NamedTuple):
+    left: Any
+    right: Any
+    start: int
+    cols: int
+    into: Any = None
+    target: int = 0
+    split: bool = False
+
+
+class Extra(NamedTuple):
+    builder: Any
+    given: list
+    given_specs: list
+    made: list
+    made_specs: list
+    spare: list
+
+
+def scatter_dot_kernel(count, items, num_outs, num_bases, parts, extra, *refs):
     num = len(items)
-    base = 6 * num + 5
-    beside = None
-    if extra is not None:
-        builder, takes, gives = extra
-        given, refs = refs[2 * num : 2 * num + takes], refs[: 2 * num] + refs[2 * num + takes :]
-        made, refs = refs[3 * num : 3 * num + gives], refs[: 3 * num] + refs[3 * num + gives :]
-        spare, refs = refs[3 * num + base :], refs[: 3 * num + base]
-    lefts, rights, outs = refs[:num], refs[num : 2 * num], refs[2 * num : 3 * num]
-    refs = refs[3 * num :]
-    left_bufs, right_bufs = refs[:num], refs[num : 2 * num]
-    firsts, owns, helds, totals = (refs[(2 + i) * num : (3 + i) * num] for i in range(4))
-    send_sems, recv_sems, left_sems, right_sems, store_sems = refs[6 * num :]
+    taken = 0
+
+    def take(amount):
+        nonlocal taken
+        taken += amount
+        return refs[taken - amount : taken]
+
+    lefts, rights, _ = take(num), take(num), take(num_bases)
+    given = take(len(extra.given) if extra else 0)
+    outs = take(num_outs)
+    made = take(len(extra.made) if extra else 0)
+    left_bufs, right_bufs, firsts, owns, helds, totals = (take(num) for _ in range(6))
+    send_sems, recv_sems, left_sems, right_sems, store_sems = take(5)
+    beside = extra.builder(count, given, made, refs[taken:], right_bufs) if extra else None
     entry_place = ring_place(lax.axis_index("dp"), count)
+    last = count - 1
 
     def load_right(item):
-        return pltpu.make_async_copy(rights[item], right_bufs[item], right_sems.at[item])
+        _, half, start, _ = items[item]
+        return pltpu.make_async_copy(
+            rights[item].at[:, start : start + 2 * half], right_bufs[item], right_sems.at[item]
+        )
 
     def load_left(step, side, item, place):
-        block, _ = items[item]
+        block = items[item][0]
         member = member_at(place, side, step + 1, count)
         slot = step % 2
         return pltpu.make_async_copy(
@@ -546,17 +596,10 @@
         load_right(item).start()
         for side in range(2):
             load_left(0, side, item, entry_place).start()
-    if extra is not None:
-        beside = builder(count, given, made, spare, right_bufs)
+    if beside:
         beside.begin()
-    place, neighbours = ring_setup(count)
+    place, neighbours = ring_setup(count, beside.peers() if beside else None)
     pairs = [(item, side) for item in range(num) for side in range(2)]
-
-    def own_sum(step, side, item):
-        _, half = items[item]
-        return tn_dot(
-            left_bufs[item][side, step % 2], right_bufs[item][:, side * half : (side + 1) * half]
-        )
 
     def send(step, side, item, part, source):
         return pltpu.make_async_remote_copy(
@@ -568,67 +611,74 @@
             device_id_type=MESH_ID,
         )
 
-    def prefetch(step):
-        for item, side in pairs:
-            load_left(step, side, item, place).start()
-
-    prefetch(1)
+    def store(item, side, part):
+        block, half, _, places = items[item]
+        out, column = places[side]
+        rows = block // parts
+        return pltpu.make_async_copy(
+            totals[item].at[side, part],
+            outs[out].at[part * rows : (part + 1) * rows, column : column + half],
+            store_sems.at[side, item * parts + part],
+        )
+
     for item in range(num):
         load_right(item).wait()
-    for item, side in pairs:
-        load_left(0, side, item, place).wait()
-        firsts[item][side] = own_sum(0, side, item).astype(BF16).reshape(firsts[item].shape[1:])
-        for part in range(parts):
-            send(0, side, item, part, firsts[item].at[side]).start()
-    if beside:
-        beside.compute(0)
-
-    def hop(step, carry):
-        prefetch(step + 1)
-        for item, side in pairs:
-            load_left(step, side, item, place).wait()
-            owns[item][side] = own_sum(step, side, item).reshape(owns[item].shape[1:])
+
+    def turn(step, carry):
+        @pl.when(step < last)
+        def _():
+            for item, side in pairs:
+                load_left(step + 1, side, item, place).start()
+
+        for item in range(num):
+            half = items[item][1]
+            for side in range(2):
+                load_left(step, side, item, place).wait()
+
+            def own_sum(side, inner):
+                cols = pl.ds(pl.multiple_of(side * half, half), half)
+                owns[item][side] = tn_dot(
+                    left_bufs[item][side, step % 2], right_bufs[item][:, cols]
+                ).reshape(owns[item].shape[1:])
+                return inner
+
+            lax.fori_loop(0, 2, own_sum, 0)
+
+        @pl.when(step == 0)
+        def _():
+            for part in range(parts):
+                for item, side in pairs:
+                    firsts[item][side, part] = owns[item][side, part].astype(BF16)
+                    send(0, side, item, part, firsts[item].at[side]).start()
+
         if beside:
             beside.compute(step)
-        for part in range(parts):
-            for item, side in pairs:
-                arrived = helds[item].at[side, step - 1]
-                send(step - 1, side, item, part, arrived).wait_recv()
-                arrived[part] = (
-                    arrived[part].astype(F32) + owns[item][side, part]
-                ).astype(BF16)
-                send(step, side, item, part, arrived).start()
+
+        @pl.when((step > 0) & (step < last))
+        def _():
+            for part in range(parts):
+                for item, side in pairs:
+                    arrived = helds[item].at[side, step - 1]
+                    send(step - 1, side, item, part, arrived).wait_recv()
+                    arrived[part] = (
+                        arrived[part].astype(F32) + owns[item][side, part]
+                    ).astype(BF16)
+                    send(step, side, item, part, arrived).start()
+
         return carry
 
-    lax.fori_loop(1, count - 1, hop, 0)
-    last = count - 1
-    for item, side in pairs:
-        load_left(last, side, item, place).wait()
-        owns[item][side] = own_sum(last, side, item).reshape(owns[item].shape[1:])
-    if beside:
-        beside.compute(last)
-    stores = []
+    lax.fori_loop(0, count, turn, 0)
     for part in range(parts):
         for item, side in pairs:
-            block, half = items[item]
             arrived = helds[item].at[side, last - 1]
             send(last - 1, side, item, part, arrived).wait_recv()
             totals[item][side, part] = arrived[part].astype(F32) + owns[item][side, part]
-            stores.append(
-                pltpu.make_async_copy(
-                    totals[item].at[side, part],
-                    outs[item].at[
-                        pl.ds(part * (block // parts), block // parts),
-                        pl.ds(side * half, half),
-                    ],
-                    store_sems.at[side, item * parts + part],
-                )
-            )
-            stores[-1].start()
-    for store in stores:
-        store.wait()
+            store(item, side, part).start()
     if beside:
         beside.finish()
+    for part in range(parts):
+        for item, side in pairs:
+            store(item, side, part).wait()
 
     def drain(step, carry):
         for part in range(parts):
@@ -636,35 +686,47 @@
                 send(step, side, item, part, helds[item].at[side, 0]).wait_send()
         return carry
 
-    lax.fori_loop(0, count - 1, drain, 0)
+    lax.fori_loop(0, last, drain, 0)
 
 
 def ring_scatter_dots(jobs, parts, count, collective_id, extra=None):
-    builder, given, given_specs, made, spare = extra or (None, [], [], [], [])
-    lefts, rights = [j[0] for j in jobs], [j[1] for j in jobs]
-    rows = lefts[0].shape[0]
-    items = tuple((l.shape[1] // count, r.shape[1] // 2) for l, r in jobs)
+    rows = jobs[0].left.shape[0]
+    items, shapes, bases, aliases = [], [], [], {}
+    for job in jobs:
+        block, half = job.left.shape[1] // count, job.cols // 2
+        if job.split:
+            places = ((len(shapes), 0), (len(shapes) + 1, 0))
+            shapes += [(block, half)] * 2
+        else:
+            places = ((len(shapes), job.target), (len(shapes), job.target + half))
+            if job.into is None:
+                shapes.append((block, job.cols))
+            elif isinstance(job.into, int):
+                shapes.append((block, job.into))
+            else:
+                aliases[2 * len(jobs) + len(bases)] = len(shapes)
+                bases.append(job.into)
+                shapes.append(job.into.shape)
+        items.append((block, half, job.start, places))
     num = len(jobs)
 
     def buffers(depth, dtype):
-        return [pltpu.VMEM(depth + (parts, b // parts, h), dtype) for b, h in items]
+        return [pltpu.VMEM(depth + (parts, b // parts, h), dtype) for b, h, _, _ in items]
 
     slots = num * parts
-    flops = sum(2 * rows * l.shape[1] * r.shape[1] for l, r in jobs)
-    nbytes = sum(2 * l.shape[1] * r.shape[1] for l, r in jobs)
+    flops = sum(2 * rows * j.left.shape[1] * j.cols for j in jobs)
+    nbytes = sum(2 * j.left.shape[1] * j.cols for j in jobs)
+    given, given_specs, made, made_specs, spare = extra[1:] if extra else ([], [], [], [], [])
     return pl.pallas_call(
         functools.partial(
-            scatter_dot_kernel,
-            count,
-            items,
-            parts,
-            (builder, len(given), len(made)) if extra else None,
+            scatter_dot_kernel, count, items, len(shapes), len(bases), parts, extra
         ),
-        out_shape=[jax.ShapeDtypeStruct((b, 2 * h), F32) for b, h in items] + made,
-        in_specs=[pl.BlockSpec(memory_space=pl.ANY)] * (2 * num) + given_specs,
-        out_specs=[pl.BlockSpec(memory_space=pl.ANY)] * (num + len(made)),
-        scratch_shapes=[pltpu.VMEM((2, 2, rows, b), BF16) for b, _ in items]
-        + [pltpu.VMEM(r.shape, BF16) for r in rights]
+        out_shape=[jax.ShapeDtypeStruct(s, F32) for s in shapes] + made,
+        in_specs=[ANY] * (2 * num + len(bases)) + given_specs,
+        out_specs=[ANY] * len(shapes) + made_specs,
+        input_output_aliases=aliases,
+        scratch_shapes=[pltpu.VMEM((2, 2, rows, i[0]), BF16) for i in items]
+        + [pltpu.VMEM((rows, 2 * i[1]), BF16) for i in items]
         + buffers((2,), BF16)
         + buffers((2,), F32)
         + buffers((2, count - 1), BF16)
@@ -684,7 +746,97 @@
             flops=flops, bytes_accessed=20 * nbytes, transcendentals=0
         ),
         name=f"ring_scatter_{collective_id}",
-    )(*lefts, *rights, *given)
+    )(*[j.left for j in jobs], *[j.right for j in jobs], *bases, *given)
+
+
+class ShareWork:
+    def __init__(self, count, given, made, spare, rights):
+        self.given, self.out = given, made[0]
+        self.pair, self.first, self.sums, self.second, self.sems = spare
+        self.count, self.group = count, self.second.shape[0] + 1
+        self.row, self.col = lax.axis_index("dp"), lax.axis_index("tensor")
+
+    def in_column(self, shift):
+        return {"dp": (self.row + shift) % self.count}
+
+    def in_group(self, shift):
+        return {"tensor": (self.col + shift) % self.group}
+
+    def peers(self):
+        return [self.in_column(s) for s in range(1, self.count)] + [
+            self.in_group(s) for s in range(1, self.group)
+        ]
+
+    def begin(self):
+        pass
+
+    def part(self, row):
+        width = self.sums.shape[1]
+        return pl.ds(pl.multiple_of(row * width, width), width)
+
+    def move(self, stage, shift):
+        if stage == 0:
+            source = self.pair.at[:, self.part((self.row + shift) % self.count)]
+            target, device, slot = self.first.at[shift - 1], self.in_column(shift), shift - 1
+        else:
+            source, target = self.sums, self.second.at[shift - 1]
+            device, slot = self.in_group(shift), self.count + shift - 2
+        return pltpu.make_async_remote_copy(
+            src_ref=source,
+            dst_ref=target,
+            send_sem=self.sems.at[0, slot],
+            recv_sem=self.sems.at[1, slot],
+            device_id=device,
+            device_id_type=MESH_ID,
+        )
+
+    def compute(self, step):
+        @pl.when(step == 0)
+        def _():
+            self.pair[...] = self.given[0][...]
+            self.pair[1:2, :] = self.given[1][...]
+            for shift in range(1, self.count):
+                self.move(0, shift).start()
+
+        @pl.when(step == 2)
+        def _():
+            total = self.pair[:, self.part(self.row)]
+            for shift in range(1, self.count):
+                self.move(0, shift).wait()
+                total = total + self.first[shift - 1]
+            self.sums[...] = total
+            for shift in range(1, self.group):
+                self.move(1, shift).start()
+
+    def finish(self):
+        total = self.sums[...]
+        for shift in range(1, self.group):
+            self.move(1, shift).wait()
+            total = total + self.second[shift - 1]
+        share = total.shape[1] // self.group
+        picked = jnp.zeros((8, share), F32)
+        for col in range(self.group):
+            picked = jnp.where(self.col == col, total[:, col * share : (col + 1) * share], picked)
+        self.out[:, :share] = picked
+
+
+def share_work(first, second, count, group):
+    width = first.shape[1] // count
+    vmem = pl.BlockSpec(memory_space=pltpu.VMEM)
+    return Extra(
+        ShareWork,
+        [first, second],
+        [vmem] * 2,
+        [jax.ShapeDtypeStruct((8, 128), F32)],
+        [vmem],
+        [
+            pltpu.VMEM(first.shape, F32),
+            pltpu.VMEM((count - 1, 8, width), F32),
+            pltpu.VMEM((8, width), F32),
+            pltpu.VMEM((group - 1, 8, width), F32),
+            pltpu.SemaphoreType.DMA((2, count + group - 2)),
+        ],
+    )
 
 
 class NormWork:
@@ -736,32 +888,31 @@
         for copy in self.loads(0):
             copy.start()
 
+    def peers(self):
+        return None
+
     def compute(self, step):
-        last = self.count - 1
-        if isinstance(step, int):
-            if step < last:
-                for copy in self.loads(step + 1):
-                    copy.start()
-            if step == 0:
-                for which in range(2):
-                    self.load_grad(which).wait()
-            if step >= 2:
-                for which in range(2):
-                    self.store(which, step - 2).wait()
-        else:
+        @pl.when(step < self.count - 1)
+        def _():
             for copy in self.loads(step + 1):
                 copy.start()
 
-            @pl.when(step >= 2)
-            def _():
-                for which in range(2):
-                    self.store(which, step - 2).wait()
+        @pl.when(step == 0)
+        def _():
+            for which in range(2):
+                self.load_grad(which).wait()
+
+        @pl.when(step >= 2)
+        def _():
+            for which in range(2):
+                self.store(which, step - 2).wait()
 
         for copy in self.loads(step):
             copy.wait()
         slot = step % 2
-        for top in range(0, self.act.shape[0], 256):
-            band = pl.ds(top, 256)
+
+        def lines(index, carry):
+            band = pl.ds(pl.multiple_of(index * 256, 256), 256)
             norm = nt_dot(self.grad_bufs[0, band, :], self.row_bufs[0, slot])
             norm += nt_dot(self.grad_bufs[1, band, :], self.row_bufs[1, slot])
             self.stage[0, slot, band, :] = norm.astype(BF16)
@@ -769,6 +920,9 @@
                 self.act[band, :], self.down_bufs[slot], preferred_element_type=F32
             )
             self.stage[1, slot, band, :] = value.astype(BF16)
+            return carry
+
+        lax.fori_loop(0, self.act.shape[0] // 256, lines, 0)
         for which in range(2):
             self.store(which, step).start()
 
@@ -795,7 +949,11 @@
     ]
     given = [grad_gate, grad_up, *gates, up_all, down_all]
     return ring_scatter_dots(
-        [(grad_branch, activated)], 2, count, cid, (NormWork, given, [ANY] * 6, [wide, wide], spare)
+        [Job(grad_branch, activated, 0, hidden)],
+        2,
+        count,
+        cid,
+        Extra(NormWork, given, [ANY] * 6, [wide, wide], [ANY] * 2, spare),
     )
 
 
@@ -920,6 +1078,7 @@
             stage[0, step % 2, band, :] = (silu * up).astype(BF16)
             gate_slope[band, here] = up * sig * (1.0 + gate * (1.0 - sig))
             up_slope[band, here] = silu
+            acc[band, here] = jnp.zeros((256, cols), F32)
         store(act_hbm, 0, step).start()
 
         turn = (step + 1) // 2
@@ -962,19 +1121,15 @@
         for side in range(2):
             member = member_at(place, side, step, count)
             load_half(step, side).wait()
-            for top in range(0, rows, 256):
-                band = pl.ds(top, 256)
-                lines = gb_buf[band, pl.ds(pl.multiple_of(member * block, block), block)]
-                value = nt_dot(lines, half_bufs[side])
-                spot = (band, pl.ds(side * half, half))
-
-                @pl.when(step == 0)
-                def _():
-                    acc[spot] = value
-
-                @pl.when(step > 0)
-                def _():
-                    acc[spot] += value
+            here = pl.ds(pl.multiple_of(member * block, block), block)
+            spot = pl.ds(side * half, half)
+
+            def lines(index, carry):
+                band = pl.ds(pl.multiple_of(index * 256, 256), 256)
+                acc[band, spot] += nt_dot(gb_buf[band, here], half_bufs[side])
+                return carry
+
+            lax.fori_loop(0, rows // 256, lines, 0)
 
         return carry
 
@@ -988,11 +1143,15 @@
             store(gu_hbm, 2, step - 2).wait()
 
         here = pl.ds(pl.multiple_of(step * cols, cols), cols)
-        for top in range(0, rows, 256):
-            band = pl.ds(top, 256)
+
+        def lines(index, carry):
+            band = pl.ds(pl.multiple_of(index * 256, 256), 256)
             value = acc[band, here]
             stage[1, step % 2, band, :] = (value * gate_slope[band, here]).astype(BF16)
             stage[2, step % 2, band, :] = (value * up_slope[band, here]).astype(BF16)
+            return carry
+
+        lax.fori_loop(0, rows // 256, lines, 0)
         store(gg_hbm, 1, step).start()
         store(gu_hbm, 2, step).start()
         return carry
@@ -1053,13 +1212,16 @@
 
 class HeadWork:
     def __init__(self, count, given, made, spare, rights):
-        self.length, self.sources = given[0], given[1:]
-        self.grads_out, self.token_out = made
+        self.length, self.gain, self.sources = given[0], given[1], given[2:]
+        self.grads_out, self.token_out, self.gain_out = made
         num = len(self.sources)
         self.bufs = spare[:num]
         self.heads, self.grads, self.acc_k, self.acc_v, self.stage = spare[num : num + 5]
         self.in_sems, self.out_sems = spare[num + 5 :]
 
+    def peers(self):
+        return None
+
     def load(self, which):
         return pltpu.make_async_copy(
             self.sources[which], self.bufs[which], self.in_sems.at[which]
@@ -1068,50 +1230,63 @@
     def begin(self):
         for which in range(len(self.sources)):
             self.load(which).start()
+        self.gain_out[...] = jnp.zeros_like(self.gain_out)
+        self.acc_k[...] = jnp.zeros_like(self.acc_k)
+        self.acc_v[...] = jnp.zeros_like(self.acc_v)
 
     def store(self, band):
         rows = self.stage.shape[1]
         return pltpu.make_async_copy(
             self.stage.at[band % 2],
-            self.token_out.at[pl.ds(band * rows, rows), :],
+            self.token_out.at[pl.ds(pl.multiple_of(band * rows, rows), rows), :],
             self.out_sems.at[band % 2],
         )
 
     def store_grads(self):
         return pltpu.make_async_copy(self.grads, self.grads_out, self.out_sems.at[2])
 
-    def tokens(self, bands):
-        w_query, w_key, w_value = self.bufs[7:]
+    def tokens(self, band):
+        w_query, w_key, w_value, normed = self.bufs[7:]
         rows = self.stage.shape[1]
         inner = w_query.shape[1]
-        for band in bands:
-            if band >= 2:
-                self.store(band - 2).wait()
-            lines = slice(band * rows, (band + 1) * rows)
-            for left in range(0, w_query.shape[0], 512):
-                cols = slice(left, left + 512)
-                value = nt_dot(self.grads[lines, :inner], w_query[cols, :])
-                value += nt_dot(self.grads[lines, inner : inner + 128], w_key[cols, :])
-                value += nt_dot(self.grads[lines, inner + 128 :], w_value[cols, :])
-                self.stage[band % 2, :, cols] = value.astype(BF16)
-            self.store(band).start()
+
+        @pl.when(band >= 2)
+        def _():
+            self.store(band - 2).wait()
+
+        lines = pl.ds(pl.multiple_of(band * rows, rows), rows)
+
+        def columns(index, carry):
+            cols = pl.ds(pl.multiple_of(index * 512, 512), 512)
+            value = nt_dot(self.grads[lines, :inner], w_query[cols, :])
+            value += nt_dot(self.grads[lines, inner : inner + 128], w_key[cols, :])
+            value += nt_dot(self.grads[lines, inner + 128 :], w_value[cols, :])
+            self.stage[band % 2, :, cols] = value.astype(BF16)
+            scaled = value * normed[lines, cols].astype(F32)
+            self.gain_out[0:1, cols] += jnp.sum(scaled, axis=0, keepdims=True)
+            return carry
+
+        lax.fori_loop(0, w_query.shape[0] // 512, columns, 0)
+        self.store(band).start()
 
     def compute(self, step):
         grad_attn, w_output, queries, keys, values, cosine, sine = self.bufs[:7]
         inner = queries.shape[1]
         pairs = inner // 128
-        if isinstance(step, int):
-            if step == 0:
-                for which in range(len(self.sources)):
-                    self.load(which).wait()
-                for top in range(0, LEN, 256):
-                    rows = slice(top, top + 256)
-                    self.heads[rows, :] = nt_dot(grad_attn[rows, :], w_output[...]).astype(BF16)
-                self.acc_k[...] = jnp.zeros_like(self.acc_k)
-                self.acc_v[...] = jnp.zeros_like(self.acc_v)
-            return
-
-        @pl.when(step <= pairs)
+
+        @pl.when(step == 0)
+        def _():
+            for which in range(len(self.sources)):
+                self.load(which).wait()
+
+            def band(index, carry):
+                rows = pl.ds(pl.multiple_of(index * 256, 256), 256)
+                self.heads[rows, :] = nt_dot(grad_attn[rows, :], w_output[...]).astype(BF16)
+                return carry
+
+            lax.fori_loop(0, LEN // 256, band, 0)
+
+        @pl.when((step >= 1) & (step <= pairs))
         def _():
             here = pl.ds(pl.multiple_of((step - 1) * 128, 128), 128)
             attend_back_pair(
@@ -1128,40 +1303,49 @@
             self.grads[:, inner + 128 :] = self.acc_v[...].astype(BF16)
             self.store_grads().start()
 
-        @pl.when(step == pairs + 1)
-        def _():
-            self.tokens((0, 1))
-
-        @pl.when(step == pairs + 2)
-        def _():
-            self.tokens((2, 3))
+        @pl.when((step > pairs) & (step <= pairs + 2))
+        def _():
+            def band(index, carry):
+                self.tokens(2 * (step - pairs - 1) + index)
+                return carry
+
+            lax.fori_loop(0, 2, band, 0)
 
     def finish(self):
+        self.gain_out[0:1, :] = self.gain_out[0:1, :] / self.gain[...]
         self.store_grads().wait()
         for band in (2, 3):
             self.store(band).wait()
 
 
-def heads_ring(job, lengths, grad_attn, w_output, qkv, tables, weights, count, collective_id):
-    given = [grad_attn, w_output, *qkv, *tables, *weights]
+def heads_ring(
+    job, lengths, gain, grad_attn, w_output, qkv, tables, weights, rows_attn, count, cid
+):
+    sources = [grad_attn, w_output, *qkv, *tables, *weights, rows_attn]
     rows, width = grad_attn.shape
     inner = qkv[0].shape[1]
     made = [
         jax.ShapeDtypeStruct((rows, inner + 256), BF16),
         jax.ShapeDtypeStruct((rows, width), BF16),
+        jax.ShapeDtypeStruct((8, width), F32),
     ]
-    spare = [pltpu.VMEM(g.shape, g.dtype) for g in given] + [
+    spare = [pltpu.VMEM(g.shape, g.dtype) for g in sources] + [
         pltpu.VMEM((rows, inner), BF16),
         pltpu.VMEM((rows, inner + 256), BF16),
         pltpu.VMEM((rows, 128), F32),
         pltpu.VMEM((rows, 128), F32),
         pltpu.VMEM((2, rows // 4, width), BF16),
-        pltpu.SemaphoreType.DMA((len(given),)),
+        pltpu.SemaphoreType.DMA((len(sources),)),
         pltpu.SemaphoreType.DMA((3,)),
     ]
-    specs = [pl.BlockSpec(memory_space=pltpu.SMEM)] + [ANY] * len(given)
+    vmem = pl.BlockSpec(memory_space=pltpu.VMEM)
+    specs = [pl.BlockSpec(memory_space=pltpu.SMEM), vmem] + [ANY] * len(sources)
     return ring_scatter_dots(
-        [job], 2, count, collective_id, (HeadWork, [lengths] + given, specs, made, spare)
+        [job],
+        2,
+        count,
+        cid,
+        Extra(HeadWork, [lengths, gain] + sources, specs, made, [ANY, ANY, vmem], spare),
     )
 
 
@@ -1172,7 +1356,7 @@
     q_buf, k_buf, v_buf, head_buf, stage, own = refs[22:28]
     send_sems, recv_sems, in_sems, out_sems, local_sem = refs[28:]
     rows_buf, w_query, w_key, w_value, w_output, cosine, sine = bufs
-    shape = shard.shape
+    shape = own.shape
     me = lax.axis_index("dp")
     loads = [
         pltpu.make_async_copy(source, buf, in_sems.at[k])
@@ -1180,7 +1364,7 @@
     ]
     for load in loads:
         load.start()
-    load_own = pltpu.make_async_copy(shard, own, local_sem)
+    load_own = pltpu.make_async_copy(shard.at[:, : shape[1]], own, local_sem)
     load_own.start()
     place, neighbours = ring_setup(count)
 
@@ -1267,11 +1451,15 @@
             store_part(band - 2).wait()
 
         lines = pl.ds(pl.multiple_of(band * 256, 256), 256)
-        for left in range(0, w_output.shape[1], 512):
-            cols = slice(left, left + 512)
+
+        def columns(index, inner):
+            cols = pl.ds(pl.multiple_of(index * 512, 512), 512)
             stage[band % 2, :, cols] = jnp.dot(
                 head_buf[lines, :], w_output[:, cols], preferred_element_type=F32
             ).astype(BF16)
+            return inner
+
+        lax.fori_loop(0, w_output.shape[1] // 512, columns, 0)
         store_part(band).start()
         return carry
 
@@ -1293,7 +1481,7 @@
     lax.fori_loop(0, count - 1, drain, 0)
 
 
-def attend_ring(shard, lengths, rows_attn, weights, tables, count, collective_id):
+def attend_ring(shard, edge, lengths, rows_attn, weights, tables, count, collective_id):
     sources = [rows_attn, *weights, *tables]
     rows, width = rows_attn.shape
     inner = weights[0].shape[1]
@@ -1304,7 +1492,7 @@
     return pl.pallas_call(
         functools.partial(attend_ring_kernel, count),
         out_shape=[
-            low(shard.shape[0] * count, shard.shape[1]),
+            low(shard.shape[0] * count, edge),
             low(rows, inner),
             low(rows, 128),
             low(rows, 128),
@@ -1320,7 +1508,7 @@
             pltpu.VMEM((rows, 128), BF16),
             pltpu.VMEM((rows, inner), BF16),
             pltpu.VMEM((2, 256, width), BF16),
-            pltpu.VMEM(shard.shape, BF16),
+            pltpu.VMEM((shard.shape[0], edge), BF16),
             pltpu.SemaphoreType.DMA((2, count - 1)),
             pltpu.SemaphoreType.DMA((2, count - 1)),
             pltpu.SemaphoreType.DMA((len(sources),)),
@@ -1339,6 +1527,7 @@
 
 def ring_weight_grads(jobs, parts, count, collective_id):
     if all(left.shape[1] // count % 128 == 0 for left, _ in jobs):
+        jobs = [Job(left, right, 0, right.shape[1]) for left, right in jobs]
         return ring_scatter_dots(jobs, parts, count, collective_id)
     partials = [tn_dot(left, right).astype(BF16) for left, right in jobs]
     num = len(jobs)
@@ -1480,7 +1669,8 @@
     gates = []
     if fused:
         first_gate, queries, keys, values, head_out, attn_part = attend_ring(
-            w_gate[:, :edge],
+            w_gate,
+            edge,
             lengths,
             rows_attn,
             (query_all, key_all, value_all, output_all),
@@ -1494,8 +1684,9 @@
         head_out = attend(queries, keys, values, lengths)
         attn_part = dot(head_out, output_all).astype(BF16)
     attn_branch = scatter_rows(attn_part)
-    rest = w_gate[:, edge:] if fused else w_gate
-    (gate_all,) = ring_gather([after(rest, attn_part)], (0,), (2,), count, 1)
+    (gate_all,) = ring_gather(
+        [after(w_gate, attn_part)], (0,), (2,), count, 1, edge if fused else 0
+    )
     gates.append(gate_all)
     hidden = token_full + attn_branch
     inv_second = lax.rsqrt(jnp.mean(hidden * hidden, axis=1, keepdims=True) + epsilon)
@@ -1541,21 +1732,24 @@
     mlp_branch = scatter_rows(after(mlp_part, grad_hidden))
     if fused:
         middle = grad_up_pre.shape[1] // 2
-        (up_left,) = ring_weight_grads(
-            [(after(rows_mlp, grad_hidden), grad_up_pre[:, :middle])], 2, count, 6
-        )
-        up_right, grad_qkv, token_part = heads_ring(
-            (rows_mlp, grad_up_pre[:, middle:]),
+        hidden_cols = grad_up_pre.shape[1]
+        (grad_up,) = ring_scatter_dots(
+            [Job(after(rows_mlp, grad_hidden), grad_up_pre, 0, middle, hidden_cols)],
+            2, count, 6,
+        )
+        grad_up, grad_qkv, token_part, gain_one = heads_ring(
+            Job(rows_mlp, grad_up_pre, middle, hidden_cols - middle, grad_up, middle),
             lengths,
-            after(grad_attn, up_left),
+            gain_attn[None, :],
+            after(grad_attn, grad_up),
             output_all,
             (queries, keys, values),
             (cosine, sine),
             (query_all, key_all, value_all),
+            rows_attn,
             count,
             10,
         )
-        grad_up = jnp.concatenate([up_left, up_right], axis=1)
     else:
         (grad_up,) = ring_weight_grads(
             [(after(rows_mlp, grad_hidden), grad_up_pre)], 2, count, 6
@@ -1569,26 +1763,44 @@
             + nt_dot(grad_kpre, key_all)
             + nt_dot(grad_vpre, value_all)
         ).astype(BF16)
-        grad_qkv = jnp.concatenate([grad_qpre, grad_kpre, grad_vpre], axis=1)
     layer_out = (hidden + after(mlp_branch, token_part)).astype(BF16)
     grad_norm_one = scatter_rows(token_part)
-    attn_grads, grad_output = ring_weight_grads(
-        [(after(rows_attn, token_part), grad_qkv), (grad_attn, head_out)], 1, count, 7
-    )
     scaled_one = grad_norm_one * gain_attn
-    gain_one_part = jnp.sum(grad_norm_one * token_full * inv_first, axis=0)
     grad_tokens = (
         grad_hidden
         + inv_first * scaled_one
         - token_full * inv_first**3 * jnp.mean(scaled_one * token_full, axis=1, keepdims=True)
     )
-    grad_attn_gain, grad_mlp_gain = sum_shares(
-        after(gain_one_part, attn_grads), gain_two_part, count, group, 8
-    )
-    query_cols, key_cols = queries.shape[1], keys.shape[1]
-    grad_query = attn_grads[:, :query_cols]
-    grad_key = attn_grads[:, query_cols : query_cols + key_cols]
-    grad_value = attn_grads[:, query_cols + key_cols :]
+    if fused:
+        query_cols, key_cols = queries.shape[1], keys.shape[1]
+        rows_late = after(rows_attn, token_part)
+        grad_query, grad_key, grad_value, grad_output, shares = ring_scatter_dots(
+            [
+                Job(rows_late, grad_qkv, 0, query_cols),
+                Job(rows_late, grad_qkv, query_cols, 2 * key_cols, split=True),
+                Job(grad_attn, head_out, 0, query_cols),
+            ],
+            1,
+            count,
+            7,
+            share_work(gain_one, gain_two_part[None, :], count, group),
+        )
+        share = gain_two_part.shape[0] // (count * group)
+        grad_attn_gain, grad_mlp_gain = shares[0, :share], shares[1, :share]
+    else:
+        grad_query, grad_key, grad_value, grad_output = ring_weight_grads(
+            [
+                (after(rows_attn, token_part), grad_qpre),
+                (rows_attn, grad_kpre),
+                (rows_attn, grad_vpre),
+                (grad_attn, head_out),
+            ],
+            1, count, 7,
+        )
+        gain_one_part = jnp.sum(grad_norm_one * token_full * inv_first, axis=0)
+        grad_attn_gain, grad_mlp_gain = sum_shares(
+            after(gain_one_part, grad_query), gain_two_part, count, group, 8
+        )
     grad_output, grad_down = grad_output.T, grad_down.T
     return (
         layer_out,

time: 715 us -> 703 us (0.983); the launches traced: 707 us -> 703 us
    slice x5 -> x0, local copies, waits for them, and re-layouts: 9.99 us -> none  [the longest x1 4.67 us: body(): grad_up_pre[:, :middle]]
    pallas_call x6 -> x5, Pallas kernels: 316 us -> 324 us  [ring_scatter_dots(): pl.pallas_call(functools.partial(scatter_dot_kernel, count, items, len(sh...]
  transfers between devices with their start and end apart: 8 -> 8, of which waited for: 0 -> 0; matrix products, arithmetic and copies ran while one was open for 3% -> 2% of each run, Pallas kernels for 57% -> 60%
where the time goes in v4:
time: 703 us
  Pallas kernels  647 us (92%)
  other arithmetic  25.1 us (4%)
  between operations  15 us (2%)
  local copies, waits for them, and re-layouts  14 us (2%)
    pallas_call x5, Pallas kernels, ring_scatter_dots(): pl.pallas_call(functools.partial(scatter_dot_kernel, count, items, len(sh...  324 us
    pallas_call x3, Pallas kernels, ring_gather(): pl.pallas_call(functools.partial(gather_kernel, count, items), out_shape=...  182 us
    pallas_call x1, Pallas kernels, mlp_ring(): pl.pallas_call(functools.partial(mlp_kernel, count), out_shape=[wide] * 3...  93.3 us
    pallas_call x1, Pallas kernels, attend_ring(): pl.pallas_call(functools.partial(attend_ring_kernel, count), out_shape=[l...  47.8 us
  transfers between devices with their start and end apart: 8, of which 0 were waited for; matrix products, arithmetic and copies ran while one was open for 2% of the time, Pallas kernels for 60%

profile of v4, /device:TPU:0, one launch (start us, length us, event | category | flops | bytes accessed | tf_op | source)
XLA Modules:
  0.0 702.6 jit_solution(5877229973024279867)
XLA Ops:
  7.2 0.0 all-gather.5.cloned.1.call-start
  7.2 1.5 fusion.7
  8.7 0.7 convert_element_type.47
  9.4 2.5 fusion.9
  11.9 0.0 all-gather.5.cloned.1.call-update
  12.0 0.0 reduce-scatter.5.cloned.1.call-start
  12.7 55.7 %ring_gather_0.1 = (bf16[2048,512]{1,0:T(8,128)(2,1)}, bf16[2048,128]{1,0:T(8,128)(2,1)}, bf16[2048,128]{1,0:T(8,128)(2,1)}, bf16[512,2048]{1,0:T(8,128)(2,1)}) custom-call(bf16[256,512]{1,0:T(8,128)(2,1)} %refs_0_.1, bf16[256,128]{1,0:T(8,128)(2,1)} %refs_1_.2, bf16[256,128]{1,0:T(8,128)(2,1)} %refs_2_.1, bf16[512,256]{1,0:T(8,128)(2,1)} %refs_3_.2), custom_call_target="tpu_custom_call" | custom-call | bytes 91750400 | tf_op jit(solution)/shard_map/ring_gather_0/pallas_call | solution.py:389
  68.4 0.1 pad_maximum_fusion
  68.5 0.2 multiply_cosine_fusion
  68.7 0.9 multiply_add_fusion
  69.6 0.0 copy-done.9
  69.6 0.8 bitcast_multiply_fusion.refs_8_.refs_11_
  70.4 47.8 %attend_ring.1 = (bf16[2048,768]{1,0:T(8,128)(2,1)}, bf16[1024,512]{1,0:T(8,128)(2,1)}, bf16[1024,128]{1,0:T(8,128)(2,1)}, bf16[1024,128]{1,0:T(8,128)(2,1)}, bf...) custom-call(s32[1]{0:T(128)} %copy.32.refs_0_.refs_3_, bf16[256,2048]{1,0:T(8,128)(2,1)} %refs_0_.2, ...), custom_call_target="tpu_custom_call" | custom-call | flops 25769803776 | bytes 62914560 | tf_op jit(solution)/shard_map/attend_ring/pallas_call | solution.py:1492
  118.2 0.0 copy-start.13
  118.2 0.0 reduce-scatter.5.cloned.1.call-update
  118.2 0.0 all-gather.9.cloned.1.call-start
  118.3 0.6 copy-done.13
  118.9 48.8 %ring_gather_1.1.refs_2_.refs_5_ = bf16[2048,1280]{1,0:T(8,128)(2,1)} custom-call(bf16[256,2048]{1,0:T(8,128)(2,1)} %refs_0_.2), custom_call_target="tpu_custom_call" | custom-call | bytes 146800640 | tf_op jit(solution)/shard_map/ring_gather_1/pallas_call | solution.py:389
  167.7 0.0 reduce-scatter.5.cloned.1.call-done
  167.7 1.7 multiply_reduce_fusion
  169.5 0.0 copy-start.5
  169.5 1.5 multiply_convert_fusion
  171.0 0.0 all-gather.9.cloned.1.call-update
  171.0 0.0 all-gather.7.cloned.1.call-start
  171.1 1.2 fusion.13
  172.3 0.0 all-gather.7.cloned.1.call-update
  172.4 0.2 reduce-scatter.7.cloned.1.call-start
  172.6 77.6 %ring_gather_2.1.refs_3_.refs_6_ = bf16[2048,2048]{1,0:T(8,128)(2,1)} custom-call(bf16[256,2048]{1,0:T(8,128)(2,1)} %refs_0_.3), custom_call_target="tpu_custom_call" | custom-call | bytes 146800640 | tf_op jit(solution)/shard_map/ring_gather_2/pallas_call | solution.py:389
  250.2 0.0 all-gather.9.cloned.1.call-done.refs_0_
  250.2 0.0 all-gather.7.cloned.1.call-done.refs_5_.refs_0_
  250.2 93.3 %mlp_ring.1 = (bf16[1024,2048]{1,0:T(8,128)(2,1)}, bf16[1024,2048]{1,0:T(8,128)(2,1)}, bf16[1024,2048]{1,0:T(8,128)(2,1)}, bf16[2048,2048]{1,0:T(8,128)(2,1)}) custom-call(bf16[1024,2048]{1,0:T(8,128)(2,1)} %all-gather.9.cloned.1.call-done.refs_0_, bf16[2048,768]{1,0:T(8,128)(2,1)} %get-tuple-element.59.refs_1_.refs_4_, ...), custom_call_target="tpu_custom_call" | custom-call | flops 25769803776 | bytes 167772160 | tf_op jit(solution)/shard_map/mlp_ring/pallas_call | solution.py:1178
  343.5 81.9 %ring_scatter_4.1 = (f32[256,2048]{1,0:T(8,128)}, bf16[1024,2048]{1,0:T(8,128)(2,1)}, bf16[1024,2048]{1,0:T(8,128)(2,1)}) custom-call(bf16[1024,2048]{1,0:T(8,128)(2,1)} %all-gather.7.cloned.1.call-done.refs_5_.refs_0_, bf16[1024,2048]{1,0:T(8,128)(2,1)} %get-tuple-element.62.refs_1_, bf16[1024,2048]{1,0:T(8,128)(2,1)} %get-tuple-element.63.refs_2_.refs_1_, ...), custom_call_target="tpu_custom_call" | custom-call | flops 8589934592 | bytes 167772160 | tf_op jit(solution)/shard_map/ring_scatter_4/pallas_call | solution.py:720
  425.4 0.0 reduce-scatter.7.cloned.1.call-update
  425.5 0.0 all-gather.11.cloned.1.call-start
  425.5 78.0 %ring_scatter_5.1 = f32[256,2048]{1,0:T(8,128)} custom-call(bf16[1024,2048]{1,0:T(8,128)(2,1)} %all-gather.9.cloned.1.call-done.refs_0_, bf16[1024,2048]{1,0:T(8,128)(2,1)} %get-tuple-element.63.refs_2_.refs_1_), custom_call_target="tpu_custom_call" | custom-call | flops 8589934592 | bytes 167772160 | tf_op jit(solution)/shard_map/ring_scatter_5/pallas_call | solution.py:720
  503.5 0.0 reduce-scatter.7.cloned.1.call-done
  503.6 2.6 fusion.6
  506.2 0.9 fusion.3
  507.1 0.0 copy-start.2
  507.1 1.3 copy-done.2
  508.4 1.1 convert_element_type.57
  509.5 0.0 all-gather.11.cloned.1.call-update
  509.5 0.0 reduce-scatter.9.cloned.1.call-start
  509.6 0.7 reduce-scatter.9.cloned.1.call-update
  510.3 0.3 reduce-scatter.11.cloned.1.call-start
  510.6 41.3 %ring_scatter_6.1.refs_2_ = f32[256,2048]{1,0:T(8,128)} custom-call(bf16[1024,2048]{1,0:T(8,128)(2,1)} %all-gather.9.cloned.1.call-done.refs_0_, bf16[1024,2048]{1,0:T(8,128)(2,1)} %get-tuple-element.64.refs_3_.refs_1_), custom_call_target="tpu_custom_call" | custom-call | flops 4294967296 | bytes 83886080 | tf_op jit(solution)/shard_map/ring_scatter_6/pallas_call | solution.py:720
  551.8 0.0 all-gather.11.cloned.1.call-done.refs_5_.refs_2_
  551.9 63.7 %ring_scatter_10.1 = (f32[256,2048]{1,0:T(8,128)}, bf16[1024,768]{1,0:T(8,128)(2,1)}, bf16[1024,2048]{1,0:T(8,128)(2,1)}, f32[8,2048]{1,0:T(8,128)}) custom-call(bf16[1024,2048]{1,0:T(8,128)(2,1)} %all-gather.9.cloned.1.call-done.refs_0_, bf16[1024,2048]{1,0:T(8,128)(2,1)} %get-tuple-element.64.refs_3_.refs_1_, ...), custom_call_target="tpu_custom_call", output_to_operand_aliasing={{0}: (2, {})} | custom-call | flops 4294967296 | bytes 83886080 | tf_op jit(solution)/shard_map/ring_scatter_10/pallas_call | solution.py:720
  615.6 0.0 reduce-scatter.11.cloned.1.call-update
  615.6 2.9 copy.25
  618.5 58.8 %ring_scatter_7.1 = (f32[256,512]{1,0:T(8,128)}, f32[256,128]{1,0:T(8,128)}, f32[256,128]{1,0:T(8,128)}, f32[256,512]{1,0:T(8,128)}, f32[8,128]{1,0:T(8,128)}) custom-call(bf16[1024,2048]{1,0:T(8,128)(2,1)} %all-gather.5.cloned.1.call-done.refs_2_.refs_15_.refs_0_.refs_1_, bf16[1024,2048]{1,0:T(8,128)(2,1)} %all-gather.5.cloned.1.call-done.refs_2_.refs_15_.refs_0_.refs_1_, ...), custom_call_target="tpu_custom_call" | custom-call | flops 5368709120 | bytes 104857600 | tf_op jit(solution)/shard_map/ring_scatter_7/pallas_call | solution.py:720
  677.3 0.0 copy-start.10
  677.3 2.0 copy.24
  679.4 1.3 slice_bitcast_fusion
  680.7 2.8 convert_element_type.56
  683.5 1.8 fusion.12
  685.3 0.1 copy-done.3
  685.4 4.6 fusion.11
  690.0 0.8 copy.33
  690.8 0.7 copy.34
  691.5 0.7 copy.35
  692.1 1.3 copy.36
  693.4 1.0 copy-done.4
  694.5 1.3 copy.37
  (31 shorter events, 0.1 us)
Async XLA Ops:
  7.2 63.3 %all-gather.5.cloned.1.call-start = ((), (), s32[]{:S(2)}) async-start(), calls=%async_computation.4 | async-start | bytes 5242880 | tf_op jit(solution)/shard_map/all_gather | solution.py:1542
  9.4 60.2 %copy-start.9 = (f32[2048]{0:T(1024)}, f32[2048]{0:T(1024)S(1)}, u32[]{:S(2)}) copy-start(f32[2048]{0:T(1024)S(1)} %convert_element_type.47) | copy-start | bytes 24580
  12.0 155.7 %reduce-scatter.5.cloned.1.call-start = ((), (), s32[]{:S(2)}) async-start(), calls=%async_computation.5 | async-start | bytes 5242880 | tf_op jit(solution)/shard_map/reduce_scatter | solution.py:1546
  118.2 0.7 copy-start.13
  118.2 132.0 %all-gather.9.cloned.1.call-start = ((), (), s32[]{:S(2)}) async-start(), calls=%async_computation.7 | async-start | bytes 5242880 | tf_op jit(solution)/shard_map/all_gather | solution.py:1542
  118.9 48.8 %copy-start = (bf16[256,2048]{1,0:T(8,128)(2,1)S(1)}, bf16[256,2048]{1,0:T(8,128)(2,1)}, u32[]{:S(2)}) copy-start(bf16[256,2048]{1,0:T(8,128)(2,1)} %param.12) | copy-start | bytes 3145732
  167.7 1.8 copy-start.1
  169.5 1.6 copy-start.5
  171.0 79.2 %all-gather.7.cloned.1.call-start = ((), (), s32[]{:S(2)}) async-start(), calls=%async_computation.6 | async-start | bytes 5242880 | tf_op jit(solution)/shard_map/all_gather | solution.py:1542
  172.4 331.2 %reduce-scatter.7.cloned.1.call-start = ((), (), s32[]{:S(2)}) async-start(), calls=%async_computation.8 | async-start | bytes 5242880 | tf_op jit(solution)/shard_map/reduce_scatter | solution.py:1546
  425.5 126.4 %all-gather.11.cloned.1.call-start = ((), (), s32[]{:S(2)}) async-start(), calls=%async_computation.10 | async-start | bytes 5242880 | tf_op jit(solution)/shard_map/all_gather | solution.py:1542
  503.6 2.6 copy-start.6
  507.1 1.3 copy-start.2
  509.5 171.1 %reduce-scatter.9.cloned.1.call-start = ((), (), s32[]{:S(2)}) async-start(), calls=%async_computation.9 | async-start | bytes 5242880 | tf_op jit(solution)/shard_map/reduce_scatter | solution.py:1546
  510.3 173.2 %reduce-scatter.11.cloned.1.call-start = ((), (), s32[]{:S(2)}) async-start(), calls=%async_computation.11 | async-start | bytes 5242880 | tf_op jit(solution)/shard_map/reduce_scatter | solution.py:1546
  677.3 6.1 copy-start.10
  683.5 1.9 copy-start.3
  685.4 4.6 copy-start.8
  685.4 5.4 copy-start.12
  685.4 6.1 copy-start.11
  685.4 6.8 copy-start.7
  692.1 2.3 copy-start.4
Sparse Core Ops, SparseCore 0:
  12.1 37.1 all-gather.4
  118.4 43.5 reduce-scatter.4
  171.2 32.9 all-gather.8
  206.1 34.4 all-gather.6
  425.6 46.3 reduce-scatter.6
  509.7 32.6 all-gather.10
  544.9 44.6 reduce-scatter.8
  615.8 43.1 reduce-scatter.10

commit v5 on v4

--- a/solution.py
+++ b/solution.py
@@ -545,7 +545,7 @@
     cols: int
     into: Any = None
     target: int = 0
-    split: bool = False
+    pieces: tuple = ()
 
 
 class Extra(NamedTuple):
@@ -611,15 +611,17 @@
             device_id_type=MESH_ID,
         )
 
-    def store(item, side, part):
-        block, half, _, places = items[item]
-        out, column = places[side]
+    def stores(item, side, part):
+        block, _, _, places = items[item]
         rows = block // parts
-        return pltpu.make_async_copy(
-            totals[item].at[side, part],
-            outs[out].at[part * rows : (part + 1) * rows, column : column + half],
-            store_sems.at[side, item * parts + part],
-        )
+        return [
+            pltpu.make_async_copy(
+                totals[item].at[side, part, :, source : source + cols],
+                outs[out].at[part * rows : (part + 1) * rows, column : column + cols],
+                store_sems.at[side, item * parts + part, k],
+            )
+            for k, (source, cols, out, column) in enumerate(places[side])
+        ]
 
     for item in range(num):
         load_right(item).wait()
@@ -673,12 +675,14 @@
             arrived = helds[item].at[side, last - 1]
             send(last - 1, side, item, part, arrived).wait_recv()
             totals[item][side, part] = arrived[part].astype(F32) + owns[item][side, part]
-            store(item, side, part).start()
+            for copy in stores(item, side, part):
+                copy.start()
     if beside:
         beside.finish()
     for part in range(parts):
         for item, side in pairs:
-            store(item, side, part).wait()
+            for copy in stores(item, side, part):
+                copy.wait()
 
     def drain(step, carry):
         for part in range(parts):
@@ -694,11 +698,22 @@
     items, shapes, bases, aliases = [], [], [], {}
     for job in jobs:
         block, half = job.left.shape[1] // count, job.cols // 2
-        if job.split:
-            places = ((len(shapes), 0), (len(shapes) + 1, 0))
-            shapes += [(block, half)] * 2
+        if job.pieces:
+            places, column = ([], []), 0
+            for cols in job.pieces:
+                for side in range(2):
+                    low = max(column, side * half)
+                    high = min(column + cols, (side + 1) * half)
+                    if low < high:
+                        places[side].append(
+                            (low - side * half, high - low, len(shapes), low - column)
+                        )
+                column += cols
+                shapes.append((block, cols))
         else:
-            places = ((len(shapes), job.target), (len(shapes), job.target + half))
+            places = [
+                [(0, half, len(shapes), job.target + side * half)] for side in range(2)
+            ]
             if job.into is None:
                 shapes.append((block, job.cols))
             elif isinstance(job.into, int):
@@ -736,7 +751,7 @@
             pltpu.SemaphoreType.DMA((2, count - 1, slots)),
             pltpu.SemaphoreType.DMA((2, 2, num)),
             pltpu.SemaphoreType.DMA((num,)),
-            pltpu.SemaphoreType.DMA((2, slots)),
+            pltpu.SemaphoreType.DMA((2, slots, 3)),
         ]
         + spare,
         compiler_params=pltpu.CompilerParams(
@@ -1276,7 +1291,7 @@
 
         @pl.when(step == 0)
         def _():
-            for which in range(len(self.sources)):
+            for which in range(2):
                 self.load(which).wait()
 
             def band(index, carry):
@@ -1285,6 +1300,16 @@
                 return carry
 
             lax.fori_loop(0, LEN // 256, band, 0)
+
+        @pl.when(step == 1)
+        def _():
+            for which in range(2, 7):
+                self.load(which).wait()
+
+        @pl.when(step == pairs + 1)
+        def _():
+            for which in range(7, len(self.sources)):
+                self.load(which).wait()
 
         @pl.when((step >= 1) & (step <= pairs))
         def _():
@@ -1400,8 +1425,8 @@
         own, gathered.at[pl.ds(pl.multiple_of(me * shape[0], shape[0]), shape[0]), :], local_sem
     )
     store_own.start()
-    for load in loads:
-        load.wait()
+    for k in (0, 1, 2, 3, 5, 6):
+        loads[k].wait()
 
     def projection(band, carry):
         lines = pl.ds(pl.multiple_of(band * 256, 256), 256)
@@ -1436,6 +1461,7 @@
         return carry
 
     lax.fori_loop(0, pairs, attention, 0)
+    loads[4].wait()
     stores[3].start()
 
     def store_part(band):
@@ -1461,10 +1487,15 @@
 
         lax.fori_loop(0, w_output.shape[1] // 512, columns, 0)
         store_part(band).start()
+
+        @pl.when((band == 0) & (pairs + 2 <= count - 2))
+        def _():
+            pump(pairs + 2)
+
         return carry
 
     lax.fori_loop(0, LEN // 256, output, 0)
-    lax.fori_loop(min(pairs + 2, count - 1), count - 1, pump, 0)
+    lax.fori_loop(min(pairs + 3, count - 1), count - 1, pump, 0)
     for band in (LEN // 256 - 2, LEN // 256 - 1):
         store_part(band).wait()
     for store in stores:
@@ -1543,9 +1574,7 @@
 
 
 def scatter_rows(value):
-    return lax.psum_scatter(value.astype(BF16), "tensor", scatter_dimension=0, tiled=True).astype(
-        F32
-    )
+    return lax.psum_scatter(value.astype(BF16), "tensor", scatter_dimension=0, tiled=True)
 
 
 def share_kernel(count, group, parts_ref, out_ref, first, sums, second, sems):
@@ -1688,7 +1717,7 @@
         [after(w_gate, attn_part)], (0,), (2,), count, 1, edge if fused else 0
     )
     gates.append(gate_all)
-    hidden = token_full + attn_branch
+    hidden = token_full + attn_branch.astype(F32)
     inv_second = lax.rsqrt(jnp.mean(hidden * hidden, axis=1, keepdims=True) + epsilon)
     normed_mlp = (hidden * inv_second * gain_mlp).astype(BF16)
     normed_mlp = after(normed_mlp, gate_all)
@@ -1716,7 +1745,7 @@
         grad_up_pre = (grad_act * gate_proj * gate_sig).astype(BF16)
         norm_part = (nt_dot(grad_gate_pre, gate_all) + nt_dot(grad_up_pre, up_all)).astype(BF16)
         (grad_down,) = ring_weight_grads([(grad_branch, activated)], 2, count, 4)
-    grad_norm_two = scatter_rows(norm_part)
+    grad_norm_two = scatter_rows(norm_part).astype(F32)
     (grad_gate,) = ring_weight_grads(
         [(after(rows_mlp, norm_part), grad_gate_pre)], 2, count, 5
     )
@@ -1731,7 +1760,7 @@
     grad_attn = gather_rows(grad_hidden.astype(BF16))
     mlp_branch = scatter_rows(after(mlp_part, grad_hidden))
     if fused:
-        middle = grad_up_pre.shape[1] // 2
+        middle = 5 * grad_up_pre.shape[1] // 8
         hidden_cols = grad_up_pre.shape[1]
         (grad_up,) = ring_scatter_dots(
             [Job(after(rows_mlp, grad_hidden), grad_up_pre, 0, middle, hidden_cols)],
@@ -1763,8 +1792,8 @@
             + nt_dot(grad_kpre, key_all)
             + nt_dot(grad_vpre, value_all)
         ).astype(BF16)
-    layer_out = (hidden + after(mlp_branch, token_part)).astype(BF16)
-    grad_norm_one = scatter_rows(token_part)
+    layer_out = (hidden + after(mlp_branch, token_part).astype(F32)).astype(BF16)
+    grad_norm_one = scatter_rows(token_part).astype(F32)
     scaled_one = grad_norm_one * gain_attn
     grad_tokens = (
         grad_hidden
@@ -1776,8 +1805,13 @@
         rows_late = after(rows_attn, token_part)
         grad_query, grad_key, grad_value, grad_output, shares = ring_scatter_dots(
             [
-                Job(rows_late, grad_qkv, 0, query_cols),
-                Job(rows_late, grad_qkv, query_cols, 2 * key_cols, split=True),
+                Job(
+                    rows_late,
+                    grad_qkv,
+                    0,
+                    query_cols + 2 * key_cols,
+                    pieces=(query_cols, key_cols, key_cols),
+                ),
                 Job(grad_attn, head_out, 0, query_cols),
             ],
             1,

time: 703 us -> 705 us (level)
  transfers between devices with their start and end apart: 8 -> 8, of which waited for: 0 -> 0; matrix products, arithmetic and copies ran while one was open for 2% -> 1% of each run, Pallas kernels for 60% -> 61%
where the time goes in v5:
time: 705 us; the launch traced here: 704 us
  Pallas kernels  651 us (92%)
  other arithmetic  22 us (3%)
  between operations  15 us (2%)
  local copies, waits for them, and re-layouts  14 us (2%)
    pallas_call x5, Pallas kernels, ring_scatter_dots(): pl.pallas_call(functools.partial(scatter_dot_kernel, count, items, len(sh...  328 us
    pallas_call x3, Pallas kernels, ring_gather(): pl.pallas_call(functools.partial(gather_kernel, count, items), out_shape=...  182 us
    pallas_call x1, Pallas kernels, mlp_ring(): pl.pallas_call(functools.partial(mlp_kernel, count), out_shape=[wide] * 3...  93.4 us
    pallas_call x1, Pallas kernels, attend_ring(): pl.pallas_call(functools.partial(attend_ring_kernel, count), out_shape=[l...  47.7 us
  transfers between devices with their start and end apart: 8, of which 0 were waited for; matrix products, arithmetic and copies ran while one was open for 1% of the time, Pallas kernels for 61%

profile of v5, /device:TPU:0, one launch (start us, length us, event | category | flops | bytes accessed | tf_op | source)
XLA Modules:
  0.0 704.1 jit_solution(3490470843178475277)
XLA Ops:
  7.2 0.0 all-gather.5.cloned.1.call-start
  7.2 1.5 fusion.7
  8.7 0.7 convert_element_type.47
  9.4 2.5 fusion.9
  11.9 0.0 all-gather.5.cloned.1.call-update
  12.0 0.0 reduce-scatter.5.cloned.1.call-start
  12.7 55.7 %ring_gather_0.1 = (bf16[2048,512]{1,0:T(8,128)(2,1)}, bf16[2048,128]{1,0:T(8,128)(2,1)}, bf16[2048,128]{1,0:T(8,128)(2,1)}, bf16[512,2048]{1,0:T(8,128)(2,1)}) custom-call(bf16[256,512]{1,0:T(8,128)(2,1)} %refs_0_.1, bf16[256,128]{1,0:T(8,128)(2,1)} %refs_1_.2, bf16[256,128]{1,0:T(8,128)(2,1)} %refs_2_.1, bf16[512,256]{1,0:T(8,128)(2,1)} %refs_3_.2), custom_call_target="tpu_custom_call" | custom-call | bytes 91750400 | tf_op jit(solution)/shard_map/ring_gather_0/pallas_call | solution.py:389
  68.4 0.1 pad_maximum_fusion
  68.5 0.2 multiply_cosine_fusion
  68.7 0.9 multiply_add_fusion
  69.6 0.0 copy-done.9
  69.6 0.8 bitcast_multiply_fusion.refs_8_.refs_11_
  70.4 47.7 %attend_ring.1 = (bf16[2048,768]{1,0:T(8,128)(2,1)}, bf16[1024,512]{1,0:T(8,128)(2,1)}, bf16[1024,128]{1,0:T(8,128)(2,1)}, bf16[1024,128]{1,0:T(8,128)(2,1)}, bf...) custom-call(s32[1]{0:T(128)} %copy.32.refs_0_.refs_3_, bf16[256,2048]{1,0:T(8,128)(2,1)} %refs_0_.2, ...), custom_call_target="tpu_custom_call" | custom-call | flops 25769803776 | bytes 62914560 | tf_op jit(solution)/shard_map/attend_ring/pallas_call | solution.py:1523
  118.2 0.0 copy-start.13
  118.2 0.0 reduce-scatter.5.cloned.1.call-update
  118.2 0.0 all-gather.9.cloned.1.call-start
  118.2 0.6 copy-done.13
  118.8 48.8 %ring_gather_1.1.refs_2_.refs_5_ = bf16[2048,1280]{1,0:T(8,128)(2,1)} custom-call(bf16[256,2048]{1,0:T(8,128)(2,1)} %refs_0_.2), custom_call_target="tpu_custom_call" | custom-call | bytes 146800640 | tf_op jit(solution)/shard_map/ring_gather_1/pallas_call | solution.py:389
  167.7 0.0 reduce-scatter.5.cloned.1.call-done
  167.7 1.7 multiply_reduce_fusion
  169.5 0.0 copy-done.1
  169.5 0.0 copy-start.5
  169.5 1.5 multiply_convert_fusion
  171.0 0.0 all-gather.9.cloned.1.call-update
  171.0 0.0 all-gather.7.cloned.1.call-start
  171.1 1.2 fusion.13
  172.3 0.0 all-gather.7.cloned.1.call-update
  172.3 0.2 reduce-scatter.7.cloned.1.call-start
  172.6 77.5 %ring_gather_2.1.refs_3_.refs_6_ = bf16[2048,2048]{1,0:T(8,128)(2,1)} custom-call(bf16[256,2048]{1,0:T(8,128)(2,1)} %refs_0_.3), custom_call_target="tpu_custom_call" | custom-call | bytes 146800640 | tf_op jit(solution)/shard_map/ring_gather_2/pallas_call | solution.py:389
  250.1 0.0 all-gather.9.cloned.1.call-done.refs_0_
  250.1 0.0 all-gather.7.cloned.1.call-done.refs_5_.refs_0_
  250.2 93.4 %mlp_ring.1 = (bf16[1024,2048]{1,0:T(8,128)(2,1)}, bf16[1024,2048]{1,0:T(8,128)(2,1)}, bf16[1024,2048]{1,0:T(8,128)(2,1)}, bf16[2048,2048]{1,0:T(8,128)(2,1)}) custom-call(bf16[1024,2048]{1,0:T(8,128)(2,1)} %all-gather.9.cloned.1.call-done.refs_0_, bf16[2048,768]{1,0:T(8,128)(2,1)} %get-tuple-element.59.refs_1_.refs_4_, ...), custom_call_target="tpu_custom_call" | custom-call | flops 25769803776 | bytes 167772160 | tf_op jit(solution)/shard_map/mlp_ring/pallas_call | solution.py:1193
  343.6 82.1 %ring_scatter_4.1 = (f32[256,2048]{1,0:T(8,128)}, bf16[1024,2048]{1,0:T(8,128)(2,1)}, bf16[1024,2048]{1,0:T(8,128)(2,1)}) custom-call(bf16[1024,2048]{1,0:T(8,128)(2,1)} %all-gather.7.cloned.1.call-done.refs_5_.refs_0_, bf16[1024,2048]{1,0:T(8,128)(2,1)} %get-tuple-element.62.refs_1_, bf16[1024,2048]{1,0:T(8,128)(2,1)} %get-tuple-element.63.refs_2_.refs_1_, ...), custom_call_target="tpu_custom_call" | custom-call | flops 8589934592 | bytes 167772160 | tf_op jit(solution)/shard_map/ring_scatter_4/pallas_call | solution.py:735
  425.7 0.0 reduce-scatter.7.cloned.1.call-update
  425.7 0.0 all-gather.11.cloned.1.call-start
  425.7 78.7 %ring_scatter_5.1 = f32[256,2048]{1,0:T(8,128)} custom-call(bf16[1024,2048]{1,0:T(8,128)(2,1)} %all-gather.9.cloned.1.call-done.refs_0_, bf16[1024,2048]{1,0:T(8,128)(2,1)} %get-tuple-element.63.refs_2_.refs_1_), custom_call_target="tpu_custom_call" | custom-call | flops 8589934592 | bytes 167772160 | tf_op jit(solution)/shard_map/ring_scatter_5/pallas_call | solution.py:735
  504.5 0.0 reduce-scatter.7.cloned.1.call-done
  504.5 2.6 fusion.6
  507.2 0.9 fusion.3
  508.0 0.0 copy-start.2
  508.0 1.3 copy-done.2
  509.4 1.1 convert_element_type.56
  510.5 0.0 all-gather.11.cloned.1.call-update
  510.5 0.0 reduce-scatter.9.cloned.1.call-start
  510.5 0.7 reduce-scatter.9.cloned.1.call-update
  511.3 0.3 reduce-scatter.11.cloned.1.call-start
  511.5 48.9 %ring_scatter_6.1.refs_2_ = f32[256,2048]{1,0:T(8,128)} custom-call(bf16[1024,2048]{1,0:T(8,128)(2,1)} %all-gather.9.cloned.1.call-done.refs_0_, bf16[1024,2048]{1,0:T(8,128)(2,1)} %get-tuple-element.64.refs_3_.refs_1_), custom_call_target="tpu_custom_call" | custom-call | flops 5368709120 | bytes 104857600 | tf_op jit(solution)/shard_map/ring_scatter_6/pallas_call | solution.py:735
  560.5 0.0 all-gather.11.cloned.1.call-done.refs_5_.refs_1_
  560.5 60.9 %ring_scatter_10.1 = (f32[256,2048]{1,0:T(8,128)}, bf16[1024,768]{1,0:T(8,128)(2,1)}, bf16[1024,2048]{1,0:T(8,128)(2,1)}, f32[8,2048]{1,0:T(8,128)}) custom-call(bf16[1024,2048]{1,0:T(8,128)(2,1)} %all-gather.9.cloned.1.call-done.refs_0_, bf16[1024,2048]{1,0:T(8,128)(2,1)} %get-tuple-element.64.refs_3_.refs_1_, ...), custom_call_target="tpu_custom_call", output_to_operand_aliasing={{0}: (2, {})} | custom-call | flops 3221225472 | bytes 62914560 | tf_op jit(solution)/shard_map/ring_scatter_10/pallas_call | solution.py:735
  621.4 0.0 reduce-scatter.11.cloned.1.call-update
  621.4 2.9 copy.25
  624.3 57.6 %ring_scatter_7.1 = (f32[256,512]{1,0:T(8,128)}, f32[256,128]{1,0:T(8,128)}, f32[256,128]{1,0:T(8,128)}, f32[256,512]{1,0:T(8,128)}, f32[8,128]{1,0:T(8,128)}) custom-call(bf16[1024,2048]{1,0:T(8,128)(2,1)} %all-gather.5.cloned.1.call-done.refs_2_.refs_15_.refs_0_, bf16[1024,2048]{1,0:T(8,128)(2,1)} %all-gather.11.cloned.1.call-done.refs_5_.refs_1_, ...), custom_call_target="tpu_custom_call" | custom-call | flops 5368709120 | bytes 104857600 | tf_op jit(solution)/shard_map/ring_scatter_7/pallas_call | solution.py:735
  681.9 2.0 copy.24
  683.9 1.3 slice_bitcast_fusion
  685.2 0.0 copy-start.3
  685.2 1.8 fusion.12
  687.0 0.1 copy-done.3
  687.1 4.3 fusion.11
  691.5 0.8 copy.33
  692.3 0.7 copy.34
  692.9 0.7 copy.35
  693.6 1.3 copy.36
  694.9 1.0 copy-done.4
  695.9 1.3 copy.37
  (30 shorter events, 0.1 us)
Async XLA Ops:
  7.2 63.3 %all-gather.5.cloned.1.call-start = ((), (), s32[]{:S(2)}) async-start(), calls=%async_computation.4 | async-start | bytes 5242880 | tf_op jit(solution)/shard_map/all_gather | solution.py:1573
  9.4 60.2 %copy-start.9 = (f32[2048]{0:T(1024)}, f32[2048]{0:T(1024)S(1)}, u32[]{:S(2)}) copy-start(f32[2048]{0:T(1024)S(1)} %convert_element_type.47) | copy-start | bytes 24580
  12.0 155.7 %reduce-scatter.5.cloned.1.call-start = ((), (), s32[]{:S(2)}) async-start(), calls=%async_computation.5 | async-start | bytes 5242880 | tf_op jit(solution)/shard_map/reduce_scatter | solution.py:1577
  118.2 0.7 copy-start.13
  118.2 131.9 %all-gather.9.cloned.1.call-start = ((), (), s32[]{:S(2)}) async-start(), calls=%async_computation.7 | async-start | bytes 5242880 | tf_op jit(solution)/shard_map/all_gather | solution.py:1573
  118.8 48.9 %copy-start = (bf16[256,2048]{1,0:T(8,128)(2,1)S(1)}, bf16[256,2048]{1,0:T(8,128)(2,1)}, u32[]{:S(2)}) copy-start(bf16[256,2048]{1,0:T(8,128)(2,1)} %param.12) | copy-start | bytes 3145732
  167.7 1.8 copy-start.1
  169.5 1.6 copy-start.5
  171.0 79.1 %all-gather.7.cloned.1.call-start = ((), (), s32[]{:S(2)}) async-start(), calls=%async_computation.6 | async-start | bytes 5242880 | tf_op jit(solution)/shard_map/all_gather | solution.py:1573
  172.3 332.2 %reduce-scatter.7.cloned.1.call-start = ((), (), s32[]{:S(2)}) async-start(), calls=%async_computation.8 | async-start | bytes 5242880 | tf_op jit(solution)/shard_map/reduce_scatter | solution.py:1577
  425.7 134.8 %all-gather.11.cloned.1.call-start = ((), (), s32[]{:S(2)}) async-start(), calls=%async_computation.10 | async-start | bytes 5242880 | tf_op jit(solution)/shard_map/all_gather | solution.py:1573
  504.5 2.6 copy-start.6
  508.0 1.3 copy-start.2
  510.5 174.7 %reduce-scatter.9.cloned.1.call-start = ((), (), s32[]{:S(2)}) async-start(), calls=%async_computation.9 | async-start | bytes 5242880 | tf_op jit(solution)/shard_map/reduce_scatter | solution.py:1577
  511.3 173.9 %reduce-scatter.11.cloned.1.call-start = ((), (), s32[]{:S(2)}) async-start(), calls=%async_computation.11 | async-start | bytes 5242880 | tf_op jit(solution)/shard_map/reduce_scatter | solution.py:1577
  624.3 60.9 %copy-start.10 = (f32[2048]{0:T(1024)S(1)}, f32[2048]{0:T(1024)}, u32[]{:S(2)}) copy-start(f32[2048]{0:T(1024)} %copy-done.9) | copy-start | bytes 24580
  685.2 1.9 copy-start.3
  687.1 4.3 copy-start.8
  687.1 5.1 copy-start.12
  687.1 5.8 copy-start.11
  687.1 6.5 copy-start.7
  693.6 2.3 copy-start.4
Sparse Core Ops, SparseCore 0:
  12.1 37.1 all-gather.4
  118.3 43.6 reduce-scatter.4
  171.1 33.0 all-gather.8
  206.2 34.4 all-gather.6
  425.8 46.2 reduce-scatter.6
  510.6 32.6 all-gather.10
  545.9 44.5 reduce-scatter.8
  621.5 42.8 reduce-scatter.10

commit v6 on v5

--- a/solution.py
+++ b/solution.py
@@ -124,7 +124,8 @@
     return jnp.where(lane_index(first.shape) < HD, first, second)
 
 
-def attend_pair(length, kv, q_ref, k_ref, v_ref, o_ref):
+def attend_pair(length, pair_index, q_ref, k_ref, v_ref, o_ref, stats_ref=None):
+    kv = pair_index // 2
     square = (QB, QB)
     causal = lax.broadcasted_iota(jnp.int32, square, 1) <= lax.broadcasted_iota(
         jnp.int32, square, 0
@@ -148,6 +149,10 @@
             if start:
                 total = total + jnp.sum(far, axis=1, keepdims=True)
             inverse = 1.0 / total
+            if stats_ref is not None:
+                kept = stats_ref[here, :]
+                mine = lane_index(kept.shape) == 2 * pair_index + which
+                stats_ref[here, :] = jnp.where(mine, top + jnp.log(total), kept)
             out = jnp.dot(
                 (near * inverse).astype(BF16), v_ref[here, :], preferred_element_type=F32
             )
@@ -160,7 +165,7 @@
 
 
 def attend_kernel(length_ref, q_ref, k_ref, v_ref, o_ref):
-    attend_pair(length_ref[0], pl.program_id(0) // 2, q_ref, k_ref, v_ref, o_ref)
+    attend_pair(length_ref[0], pl.program_id(0), q_ref, k_ref, v_ref, o_ref)
 
 
 def attend(queries, keys, values, lengths):
@@ -210,6 +215,61 @@
         gq_ref[rows, :] = rope_back(joined, cos_ref[rows, :], sin_ref[rows, :])
 
 
+def row_products(grads, outs, pair_index, kept):
+    product = grads.astype(F32) * outs.astype(F32)
+    lanes = lane_index(product.shape)
+    low = jnp.sum(jnp.where(lanes < HD, product, 0.0), axis=1, keepdims=True)
+    high = jnp.sum(jnp.where(lanes < HD, 0.0, product), axis=1, keepdims=True)
+    kept = jnp.where(lanes == 2 * pair_index, low, kept)
+    return jnp.where(lanes == 2 * pair_index + 1, high, kept)
+
+
+def attend_back_tiles(
+    pair_index, q_ref, k_ref, v_ref, g_ref, cos_ref, sin_ref, stats_ref, inner_ref, bias_ref,
+    gq_ref, acc_k, acc_v,
+):
+    kv = pair_index // 2
+    square = (QB, QB)
+    causal = lax.broadcasted_iota(jnp.int32, square, 0) <= lax.broadcasted_iota(
+        jnp.int32, square, 1
+    )
+    for block in range(LEN // QB):
+        rows = slice(block * QB, (block + 1) * QB)
+        pair = q_ref[rows, :].astype(F32) * HD**-0.5
+        grad_pair = g_ref[rows, :].astype(F32)
+        queries, grads, tops, inners = [], [], [], []
+        for which in range(2):
+            queries.append(pick_head(pair, which, kv).astype(BF16))
+            grads.append(pick_head(grad_pair, which, kv).astype(BF16))
+            head = pl.ds(2 * pair_index + which, 1)
+            tops.append(stats_ref[head, rows])
+            inners.append(inner_ref[head, rows])
+        grad_queries = [None, None]
+        for tile in range(block + 1):
+            here = slice(tile * QB, (tile + 1) * QB)
+            key_vecs, value_vecs = k_ref[here, :], v_ref[here, :]
+            bias = bias_ref[here, :]
+            bias = jnp.concatenate([bias] * (QB // 128), axis=1)
+            grad_key = grad_value = None
+            for which in range(2):
+                scores = nt_dot(key_vecs, queries[which]) + bias
+                if tile == block:
+                    scores = jnp.where(causal, scores, -1e30)
+                probs = jnp.exp(scores - tops[which])
+                grad_probs = nt_dot(value_vecs, grads[which])
+                grad_scores = (probs * (grad_probs - inners[which])).astype(BF16)
+                value = jnp.dot(probs.astype(BF16), grads[which], preferred_element_type=F32)
+                key = jnp.dot(grad_scores, queries[which], preferred_element_type=F32)
+                query = tn_dot(grad_scores, key_vecs)
+                grad_value = value if which == 0 else grad_value + value
+                grad_key = key if which == 0 else grad_key + key
+                grad_queries[which] = query if tile == 0 else grad_queries[which] + query
+            acc_v[here, :] += grad_value
+            acc_k[here, :] += grad_key
+        joined = join_heads(grad_queries[0], grad_queries[1], kv) * HD**-0.5
+        gq_ref[rows, :] = rope_back(joined, cos_ref[rows, :], sin_ref[rows, :])
+
+
 def attend_back_kernel(
     length_ref, q_ref, k_ref, v_ref, g_ref, cos_ref, sin_ref, gq_ref, gk_ref, gv_ref, acc_k, acc_v
 ):
@@ -262,12 +322,12 @@
     return (1 - high) * (2 * place) + high * (2 * (count - 1 - place) + 1)
 
 
-def ring_setup(count, peers=None):
+def ring_setup(count, peers=None, more=()):
     place = ring_place(lax.axis_index("dp"), count)
     ahead = ring_member((place + 1) % count, count)
     behind = ring_member((place + count - 1) % count, count)
     barrier = pltpu.get_barrier_semaphore()
-    peers = peers or [{"dp": ahead}, {"dp": behind}]
+    peers = (peers or [{"dp": ahead}, {"dp": behind}]) + list(more)
     for other in peers:
         pl.semaphore_signal(barrier, inc=1, device_id=other, device_id_type=MESH_ID)
     pl.semaphore_wait(barrier, len(peers))
@@ -598,7 +658,7 @@
             load_left(0, side, item, entry_place).start()
     if beside:
         beside.begin()
-    place, neighbours = ring_setup(count, beside.peers() if beside else None)
+    place, neighbours = ring_setup(count, *(beside.peers() if beside else ()))
     pairs = [(item, side) for item in range(num) for side in range(2)]
 
     def send(step, side, item, part, source):
@@ -778,9 +838,8 @@
         return {"tensor": (self.col + shift) % self.group}
 
     def peers(self):
-        return [self.in_column(s) for s in range(1, self.count)] + [
-            self.in_group(s) for s in range(1, self.group)
-        ]
+        column = [self.in_column(s) for s in range(1, self.count)]
+        return column, [self.in_group(s) for s in range(1, self.group)]
 
     def begin(self):
         pass
@@ -813,7 +872,7 @@
             for shift in range(1, self.count):
                 self.move(0, shift).start()
 
-        @pl.when(step == 2)
+        @pl.when(step == 5)
         def _():
             total = self.pair[:, self.part(self.row)]
             for shift in range(1, self.count):
@@ -833,6 +892,88 @@
         for col in range(self.group):
             picked = jnp.where(self.col == col, total[:, col * share : (col + 1) * share], picked)
         self.out[:, :share] = picked
+
+
+class GatherWork:
+    def __init__(self, count, given, made, spare, rights):
+        self.own, self.out = given[0], made[0]
+        self.stage, self.sems, self.local = spare
+        self.col = lax.axis_index("tensor")
+        self.rows = self.own.shape[0]
+        self.parts = self.sems.shape[2]
+
+    def core(self):
+        return {"tensor": self.col + 1 - 2 * (self.col % 2)}
+
+    def across(self):
+        return {"tensor": (self.col + 2) % 4}
+
+    def peers(self):
+        return None, [self.core(), self.across()]
+
+    def begin(self):
+        pltpu.make_async_copy(self.own, self.stage, self.local).start()
+
+    def spot(self, member, part):
+        size = self.rows // self.parts
+        return pl.ds(pl.multiple_of(member * self.rows + part * size, size), size)
+
+    def move(self, kind, part):
+        size = self.rows // self.parts
+        member = (self.col + 2) % 4 if kind == 2 else self.col
+        target = self.out.at[self.spot(member, part), :]
+        source = target if kind == 2 else self.own.at[part * size : (part + 1) * size, :]
+        return pltpu.make_async_remote_copy(
+            src_ref=source,
+            dst_ref=target,
+            send_sem=self.sems.at[0, kind, part],
+            recv_sem=self.sems.at[1, kind, part],
+            device_id=self.across() if kind == 0 else self.core(),
+            device_id_type=MESH_ID,
+        )
+
+    def keep(self):
+        here = pl.ds(pl.multiple_of(self.col * self.rows, self.rows), self.rows)
+        return pltpu.make_async_copy(self.stage, self.out.at[here, :], self.local)
+
+    def compute(self, step):
+        @pl.when(step == 0)
+        def _():
+            for part in range(self.parts):
+                self.move(0, part).start()
+                self.move(1, part).start()
+            pltpu.make_async_copy(self.own, self.stage, self.local).wait()
+            self.keep().start()
+
+        for part, turn in enumerate((2, 4, 5, 6)):
+
+            @pl.when(step == turn)
+            def _():
+                self.move(0, part).wait_recv()
+                self.move(2, part).start()
+
+    def finish(self):
+        for part in range(self.parts):
+            self.move(0, part).wait_send()
+            self.move(1, part).wait()
+            self.move(2, part).wait()
+        self.keep().wait()
+
+
+def gather_work(own):
+    rows, width = own.shape
+    return Extra(
+        GatherWork,
+        [own],
+        [ANY],
+        [jax.ShapeDtypeStruct((4 * rows, width), BF16)],
+        [ANY],
+        [
+            pltpu.VMEM(own.shape, BF16),
+            pltpu.SemaphoreType.DMA((2, 3, 4)),
+            pltpu.SemaphoreType.DMA,
+        ],
+    )
 
 
 def share_work(first, second, count, group):
@@ -904,7 +1045,7 @@
             copy.start()
 
     def peers(self):
-        return None
+        return ()
 
     def compute(self, step):
         @pl.when(step < self.count - 1)
@@ -1232,10 +1373,11 @@
         num = len(self.sources)
         self.bufs = spare[:num]
         self.heads, self.grads, self.acc_k, self.acc_v, self.stage = spare[num : num + 5]
-        self.in_sems, self.out_sems = spare[num + 5 :]
+        self.stats, self.inner, self.bias = spare[num + 5 : num + 8]
+        self.in_sems, self.out_sems = spare[num + 8 :]
 
     def peers(self):
-        return None
+        return ()
 
     def load(self, which):
         return pltpu.make_async_copy(
@@ -1248,6 +1390,8 @@
         self.gain_out[...] = jnp.zeros_like(self.gain_out)
         self.acc_k[...] = jnp.zeros_like(self.acc_k)
         self.acc_v[...] = jnp.zeros_like(self.acc_v)
+        key_pos = lax.broadcasted_iota(jnp.int32, self.bias.shape, 0)
+        self.bias[...] = jnp.where(key_pos < self.length[0], 0.0, -1e30)
 
     def store(self, band):
         rows = self.stage.shape[1]
@@ -1261,7 +1405,7 @@
         return pltpu.make_async_copy(self.grads, self.grads_out, self.out_sems.at[2])
 
     def tokens(self, band):
-        w_query, w_key, w_value, normed = self.bufs[7:]
+        w_query, w_key, w_value, normed = self.bufs[9:]
         rows = self.stage.shape[1]
         inner = w_query.shape[1]
 
@@ -1285,7 +1429,7 @@
         self.store(band).start()
 
     def compute(self, step):
-        grad_attn, w_output, queries, keys, values, cosine, sine = self.bufs[:7]
+        grad_attn, w_output, queries, keys, values, cosine, sine, outs, stats = self.bufs[:9]
         inner = queries.shape[1]
         pairs = inner // 128
 
@@ -1303,20 +1447,34 @@
 
         @pl.when(step == 1)
         def _():
-            for which in range(2, 7):
+            for which in range(2, 9):
                 self.load(which).wait()
 
+            self.stats[...] = jnp.transpose(stats[...])
+
+            def products(index, carry):
+                rows = pl.ds(pl.multiple_of(index * 256, 256), 256)
+                kept = jnp.zeros((256, 128), F32)
+                for pair in range(pairs):
+                    cols = slice(pair * 128, (pair + 1) * 128)
+                    kept = row_products(self.heads[rows, cols], outs[rows, cols], pair, kept)
+                stats[rows, :] = kept
+                return carry
+
+            lax.fori_loop(0, LEN // 256, products, 0)
+            self.inner[...] = jnp.transpose(stats[...])
+
         @pl.when(step == pairs + 1)
         def _():
-            for which in range(7, len(self.sources)):
+            for which in range(9, len(self.sources)):
                 self.load(which).wait()
 
         @pl.when((step >= 1) & (step <= pairs))
         def _():
             here = pl.ds(pl.multiple_of((step - 1) * 128, 128), 128)
-            attend_back_pair(
-                self.length[0], (step - 1) // 2, queries.at[:, here], keys, values,
-                self.heads.at[:, here], cosine, sine, self.grads.at[:, here],
+            attend_back_tiles(
+                step - 1, queries.at[:, here], keys, values, self.heads.at[:, here], cosine,
+                sine, self.stats, self.inner, self.bias, self.grads.at[:, here],
                 self.acc_k, self.acc_v,
             )
 
@@ -1344,9 +1502,9 @@
 
 
 def heads_ring(
-    job, lengths, gain, grad_attn, w_output, qkv, tables, weights, rows_attn, count, cid
+    job, lengths, gain, grad_attn, w_output, qkv, tables, saved, weights, rows_attn, count, cid
 ):
-    sources = [grad_attn, w_output, *qkv, *tables, *weights, rows_attn]
+    sources = [grad_attn, w_output, *qkv, *tables, *saved, *weights, rows_attn]
     rows, width = grad_attn.shape
     inner = qkv[0].shape[1]
     made = [
@@ -1360,6 +1518,9 @@
         pltpu.VMEM((rows, 128), F32),
         pltpu.VMEM((rows, 128), F32),
         pltpu.VMEM((2, rows // 4, width), BF16),
+        pltpu.VMEM((128, rows), F32),
+        pltpu.VMEM((128, rows), F32),
+        pltpu.VMEM((rows, 128), F32),
         pltpu.SemaphoreType.DMA((len(sources),)),
         pltpu.SemaphoreType.DMA((3,)),
     ]
@@ -1376,10 +1537,10 @@
 
 def attend_ring_kernel(count, *refs):
     length_ref, shard, sources = refs[0], refs[1], refs[2:9]
-    gathered, q_out, k_out, v_out, head_out, part_out = refs[9:15]
-    bufs = refs[15:22]
-    q_buf, k_buf, v_buf, head_buf, stage, own = refs[22:28]
-    send_sems, recv_sems, in_sems, out_sems, local_sem = refs[28:]
+    gathered, q_out, k_out, v_out, head_out, part_out, stats_out = refs[9:16]
+    bufs = refs[16:23]
+    q_buf, k_buf, v_buf, head_buf, stage, own, stats = refs[23:30]
+    send_sems, recv_sems, in_sems, out_sems, local_sem = refs[30:]
     rows_buf, w_query, w_key, w_value, w_output, cosine, sine = bufs
     shape = own.shape
     me = lax.axis_index("dp")
@@ -1428,6 +1589,8 @@
     for k in (0, 1, 2, 3, 5, 6):
         loads[k].wait()
 
+    stats[...] = jnp.zeros_like(stats)
+
     def projection(band, carry):
         lines = pl.ds(pl.multiple_of(band * 256, 256), 256)
         project_rows(
@@ -1451,7 +1614,7 @@
     def attention(pair, carry):
         here = pl.ds(pl.multiple_of(pair * 128, 128), 128)
         attend_pair(
-            length_ref[0], pair // 2, q_buf.at[:, here], k_buf, v_buf, head_buf.at[:, here]
+            length_ref[0], pair, q_buf.at[:, here], k_buf, v_buf, head_buf.at[:, here], stats
         )
 
         @pl.when(pair + 2 <= count - 2)
@@ -1463,6 +1626,8 @@
     lax.fori_loop(0, pairs, attention, 0)
     loads[4].wait()
     stores[3].start()
+    store_stats = pltpu.make_async_copy(stats, stats_out, out_sems.at[6])
+    store_stats.start()
 
     def store_part(band):
         return pltpu.make_async_copy(
@@ -1500,6 +1665,7 @@
         store_part(band).wait()
     for store in stores:
         store.wait()
+    store_stats.wait()
     store_own.wait()
     for side in range(2):
         hop(count - 2, side).wait_recv()
@@ -1529,9 +1695,10 @@
             low(rows, 128),
             low(rows, inner),
             low(rows, width),
+            jax.ShapeDtypeStruct((rows, 128), F32),
         ],
         in_specs=[pl.BlockSpec(memory_space=pltpu.SMEM)] + [ANY] * (1 + len(sources)),
-        out_specs=[ANY] * 6,
+        out_specs=[ANY] * 7,
         scratch_shapes=[pltpu.VMEM(source.shape, source.dtype) for source in sources]
         + [
             pltpu.VMEM((rows, inner), BF16),
@@ -1540,10 +1707,11 @@
             pltpu.VMEM((rows, inner), BF16),
             pltpu.VMEM((2, 256, width), BF16),
             pltpu.VMEM((shard.shape[0], edge), BF16),
+            pltpu.VMEM((rows, 128), F32),
             pltpu.SemaphoreType.DMA((2, count - 1)),
             pltpu.SemaphoreType.DMA((2, count - 1)),
             pltpu.SemaphoreType.DMA((len(sources),)),
-            pltpu.SemaphoreType.DMA((6,)),
+            pltpu.SemaphoreType.DMA((7,)),
             pltpu.SemaphoreType.DMA,
         ],
         compiler_params=pltpu.CompilerParams(
@@ -1693,11 +1861,11 @@
         (0, 0, 0, 1), (1, 1, 1, 1), count, 0,
     )
     grad_branch = gather_rows(after(cot_masked.astype(BF16), rows_attn))
-    fused = count == 8
+    fused = count == 8 and group == 4
     edge = 3 * w_gate.shape[1] // 8
     gates = []
     if fused:
-        first_gate, queries, keys, values, head_out, attn_part = attend_ring(
+        first_gate, queries, keys, values, head_out, attn_part, stats = attend_ring(
             w_gate,
             edge,
             lengths,
@@ -1757,29 +1925,31 @@
         - hidden * inv_second**3 * jnp.mean(scaled_two * hidden, axis=1, keepdims=True)
     )
     grad_hidden = after(grad_hidden, grad_gate)
-    grad_attn = gather_rows(grad_hidden.astype(BF16))
-    mlp_branch = scatter_rows(after(mlp_part, grad_hidden))
     if fused:
-        middle = 5 * grad_up_pre.shape[1] // 8
+        middle = 3 * grad_up_pre.shape[1] // 8
         hidden_cols = grad_up_pre.shape[1]
-        (grad_up,) = ring_scatter_dots(
-            [Job(after(rows_mlp, grad_hidden), grad_up_pre, 0, middle, hidden_cols)],
-            2, count, 6,
-        )
+        grad_up, grad_attn = ring_scatter_dots(
+            [Job(rows_mlp, grad_up_pre, 0, middle, hidden_cols)],
+            2, count, 6, gather_work(grad_hidden.astype(BF16)),
+        )
+        mlp_branch = scatter_rows(after(mlp_part, grad_attn))
         grad_up, grad_qkv, token_part, gain_one = heads_ring(
             Job(rows_mlp, grad_up_pre, middle, hidden_cols - middle, grad_up, middle),
             lengths,
             gain_attn[None, :],
-            after(grad_attn, grad_up),
+            grad_attn,
             output_all,
             (queries, keys, values),
             (cosine, sine),
+            (head_out, stats),
             (query_all, key_all, value_all),
             rows_attn,
             count,
             10,
         )
     else:
+        grad_attn = gather_rows(grad_hidden.astype(BF16))
+        mlp_branch = scatter_rows(after(mlp_part, grad_hidden))
         (grad_up,) = ring_weight_grads(
             [(after(rows_mlp, grad_hidden), grad_up_pre)], 2, count, 6
         )

time: 705 us -> 702 us (level)
  transfers between devices with their start and end apart: 8 -> 7, of which waited for: 0 -> 0; matrix products, arithmetic and copies ran while one was open for 1% -> 1% of each run, Pallas kernels for 61% -> 56%
where the time goes in v6:
time: 702 us; the launch traced here: 701 us
  Pallas kernels  649 us (92%)
  other arithmetic  22 us (3%)
  between operations  15 us (2%)
  local copies, waits for them, and re-layouts  14 us (2%)
    pallas_call x5, Pallas kernels, ring_scatter_dots(): pl.pallas_call(functools.partial(scatter_dot_kernel, count, items, len(sh...  326 us
    pallas_call x3, Pallas kernels, ring_gather(): pl.pallas_call(functools.partial(gather_kernel, count, items), out_shape=...  182 us
    pallas_call x1, Pallas kernels, mlp_ring(): pl.pallas_call(functools.partial(mlp_kernel, count), out_shape=[wide] * 3...  93.4 us
    pallas_call x1, Pallas kernels, attend_ring(): pl.pallas_call(functools.partial(attend_ring_kernel, count), out_shape=[l...  47.8 us
  transfers between devices with their start and end apart: 7, of which 0 were waited for; matrix products, arithmetic and copies ran while one was open for 1% of the time, Pallas kernels for 56%

profile of v6, /device:TPU:0, one launch (start us, length us, event | category | flops | bytes accessed | tf_op | source)
XLA Modules:
  0.0 701.0 jit_solution(1533467706415965876)
XLA Ops:
  7.2 0.0 all-gather.4.cloned.1.call-start
  7.2 1.5 fusion.7
  8.7 0.7 convert_element_type.47
  9.4 2.5 fusion.9
  11.9 0.0 all-gather.4.cloned.1.call-update
  12.0 0.0 reduce-scatter.5.cloned.1.call-start
  12.7 55.7 %ring_gather_0.1 = (bf16[2048,512]{1,0:T(8,128)(2,1)}, bf16[2048,128]{1,0:T(8,128)(2,1)}, bf16[2048,128]{1,0:T(8,128)(2,1)}, bf16[512,2048]{1,0:T(8,128)(2,1)}) custom-call(bf16[256,512]{1,0:T(8,128)(2,1)} %refs_0_.1, bf16[256,128]{1,0:T(8,128)(2,1)} %refs_1_.2, bf16[256,128]{1,0:T(8,128)(2,1)} %refs_2_.1, bf16[512,256]{1,0:T(8,128)(2,1)} %refs_3_.2), custom_call_target="tpu_custom_call" | custom-call | bytes 91750400 | tf_op jit(solution)/shard_map/ring_gather_0/pallas_call | solution.py:449
  68.4 0.1 pad_maximum_fusion
  68.5 0.2 multiply_cosine_fusion
  68.7 0.9 multiply_add_fusion
  69.6 0.0 copy-done.9
  69.6 0.8 bitcast_multiply_fusion.refs_8_.refs_11_
  70.4 47.8 %attend_ring.1 = (bf16[2048,768]{1,0:T(8,128)(2,1)}, bf16[1024,512]{1,0:T(8,128)(2,1)}, bf16[1024,128]{1,0:T(8,128)(2,1)}, bf16[1024,128]{1,0:T(8,128)(2,1)}, bf...) custom-call(s32[1]{0:T(128)} %copy.32.refs_0_.refs_3_, bf16[256,2048]{1,0:T(8,128)(2,1)} %refs_0_.2, ...), custom_call_target="tpu_custom_call" | custom-call | flops 25769803776 | bytes 62914560 | tf_op jit(solution)/shard_map/attend_ring/pallas_call | solution.py:1689
  118.2 0.0 copy-start.13
  118.3 0.0 reduce-scatter.5.cloned.1.call-update
  118.3 0.0 all-gather.8.cloned.1.call-start
  118.3 0.6 copy-done.13
  118.9 48.7 %ring_gather_1.1.refs_2_.refs_5_ = bf16[2048,1280]{1,0:T(8,128)(2,1)} custom-call(bf16[256,2048]{1,0:T(8,128)(2,1)} %refs_0_.2), custom_call_target="tpu_custom_call" | custom-call | bytes 146800640 | tf_op jit(solution)/shard_map/ring_gather_1/pallas_call | solution.py:449
  167.7 0.0 reduce-scatter.5.cloned.1.call-done
  167.7 0.0 copy-done
  167.7 0.0 copy-start.1
  167.7 1.7 multiply_reduce_fusion
  169.5 0.0 copy-done.1
  169.5 0.0 copy-start.5
  169.5 1.5 multiply_convert_fusion
  171.0 0.0 all-gather.8.cloned.1.call-update
  171.0 0.0 all-gather.6.cloned.1.call-start
  171.1 0.0 copy-done.5
  171.1 1.2 fusion.13
  172.3 0.0 all-gather.6.cloned.1.call-update
  172.4 0.2 reduce-scatter.7.cloned.1.call-start
  172.6 77.6 %ring_gather_2.1.refs_3_.refs_6_ = bf16[2048,2048]{1,0:T(8,128)(2,1)} custom-call(bf16[256,2048]{1,0:T(8,128)(2,1)} %refs_0_.3), custom_call_target="tpu_custom_call" | custom-call | bytes 146800640 | tf_op jit(solution)/shard_map/ring_gather_2/pallas_call | solution.py:449
  250.2 0.0 all-gather.8.cloned.1.call-done.refs_0_
  250.2 0.0 all-gather.6.cloned.1.call-done.refs_5_.refs_0_
  250.2 93.4 %mlp_ring.1 = (bf16[1024,2048]{1,0:T(8,128)(2,1)}, bf16[1024,2048]{1,0:T(8,128)(2,1)}, bf16[1024,2048]{1,0:T(8,128)(2,1)}, bf16[2048,2048]{1,0:T(8,128)(2,1)}) custom-call(bf16[1024,2048]{1,0:T(8,128)(2,1)} %all-gather.8.cloned.1.call-done.refs_0_, bf16[2048,768]{1,0:T(8,128)(2,1)} %get-tuple-element.60.refs_1_.refs_4_, ...), custom_call_target="tpu_custom_call" | custom-call | flops 25769803776 | bytes 167772160 | tf_op jit(solution)/shard_map/mlp_ring/pallas_call | solution.py:1334
  343.6 82.4 %ring_scatter_4.1 = (f32[256,2048]{1,0:T(8,128)}, bf16[1024,2048]{1,0:T(8,128)(2,1)}, bf16[1024,2048]{1,0:T(8,128)(2,1)}) custom-call(bf16[1024,2048]{1,0:T(8,128)(2,1)} %all-gather.6.cloned.1.call-done.refs_5_.refs_0_, bf16[1024,2048]{1,0:T(8,128)(2,1)} %get-tuple-element.63.refs_1_, bf16[1024,2048]{1,0:T(8,128)(2,1)} %get-tuple-element.64.refs_2_.refs_1_, ...), custom_call_target="tpu_custom_call" | custom-call | flops 8589934592 | bytes 167772160 | tf_op jit(solution)/shard_map/ring_scatter_4/pallas_call | solution.py:795
  426.0 0.0 reduce-scatter.7.cloned.1.call-update
  426.0 0.0 reduce-scatter.9.cloned.1.call-start
  426.1 79.0 %ring_scatter_5.1 = f32[256,2048]{1,0:T(8,128)} custom-call(bf16[1024,2048]{1,0:T(8,128)(2,1)} %all-gather.8.cloned.1.call-done.refs_0_, bf16[1024,2048]{1,0:T(8,128)(2,1)} %get-tuple-element.64.refs_2_.refs_1_), custom_call_target="tpu_custom_call" | custom-call | flops 8589934592 | bytes 167772160 | tf_op jit(solution)/shard_map/ring_scatter_5/pallas_call | solution.py:795
  505.0 0.0 reduce-scatter.7.cloned.1.call-done
  505.1 2.6 fusion.6
  507.7 0.9 fusion.3
  508.6 0.0 copy-start.2
  508.6 1.3 copy-done.2
  509.9 1.1 convert_element_type.56.refs_2_
  511.0 36.3 %ring_scatter_6.1 = (f32[256,2048]{1,0:T(8,128)}, bf16[1024,2048]{1,0:T(8,128)(2,1)}) custom-call(bf16[1024,2048]{1,0:T(8,128)(2,1)} %all-gather.8.cloned.1.call-done.refs_0_, bf16[1024,2048]{1,0:T(8,128)(2,1)} %get-tuple-element.65.refs_3_.refs_1_, bf16[256,2048]{1,0:T(8,128)(2,1)} %convert_element_type.56.refs_2_), custom_call_target="tpu_custom_call" | custom-call | flops 3221225472 | bytes 62914560 | tf_op jit(solution)/shard_map/ring_scatter_6/pallas_call | solution.py:795
  547.4 0.0 reduce-scatter.9.cloned.1.call-update
  547.4 0.3 reduce-scatter.11.cloned.1.call-start
  547.7 70.6 %ring_scatter_10.1 = (f32[256,2048]{1,0:T(8,128)}, bf16[1024,768]{1,0:T(8,128)(2,1)}, bf16[1024,2048]{1,0:T(8,128)(2,1)}, f32[8,2048]{1,0:T(8,128)}) custom-call(bf16[1024,2048]{1,0:T(8,128)(2,1)} %all-gather.8.cloned.1.call-done.refs_0_, bf16[1024,2048]{1,0:T(8,128)(2,1)} %get-tuple-element.65.refs_3_.refs_1_, ...), custom_call_target="tpu_custom_call", output_to_operand_aliasing={{0}: (2, {})} | custom-call | flops 5368709120 | bytes 104857600 | tf_op jit(solution)/shard_map/ring_scatter_10/pallas_call | solution.py:795
  618.3 0.0 reduce-scatter.11.cloned.1.call-update
  618.3 2.9 copy.25
  621.2 57.6 %ring_scatter_7.1 = (f32[256,512]{1,0:T(8,128)}, f32[256,128]{1,0:T(8,128)}, f32[256,128]{1,0:T(8,128)}, f32[256,512]{1,0:T(8,128)}, f32[8,128]{1,0:T(8,128)}) custom-call(bf16[1024,2048]{1,0:T(8,128)(2,1)} %all-gather.4.cloned.1.call-done.refs_2_.refs_17_.refs_0_, bf16[1024,2048]{1,0:T(8,128)(2,1)} %get-tuple-element.71.refs_5_.refs_1_, ...), custom_call_target="tpu_custom_call" | custom-call | flops 5368709120 | bytes 104857600 | tf_op jit(solution)/shard_map/ring_scatter_7/pallas_call | solution.py:795
  678.8 2.0 copy.24
  680.8 1.3 slice_bitcast_fusion
  682.1 0.0 copy-start.3
  682.1 1.8 fusion.12
  683.9 0.1 copy-done.3
  684.0 4.3 fusion.11
  688.3 0.8 copy.33
  689.1 0.7 copy.34
  689.8 0.7 copy.35
  690.4 1.3 copy.36
  691.8 1.0 copy-done.4
  692.8 1.3 copy.37
  (27 shorter events, 0.1 us)
Async XLA Ops:
  7.2 63.3 %all-gather.4.cloned.1.call-start = ((), (), s32[]{:S(2)}) async-start(), calls=%async_computation.4 | async-start | bytes 5242880 | tf_op jit(solution)/shard_map/all_gather | solution.py:1741
  9.4 60.2 %copy-start.9 = (f32[2048]{0:T(1024)}, f32[2048]{0:T(1024)S(1)}, u32[]{:S(2)}) copy-start(f32[2048]{0:T(1024)S(1)} %convert_element_type.47) | copy-start | bytes 24580
  12.0 155.7 %reduce-scatter.5.cloned.1.call-start = ((), (), s32[]{:S(2)}) async-start(), calls=%async_computation.5 | async-start | bytes 5242880 | tf_op jit(solution)/shard_map/reduce_scatter | solution.py:1745
  118.2 0.7 copy-start.13
  118.3 131.9 %all-gather.8.cloned.1.call-start = ((), (), s32[]{:S(2)}) async-start(), calls=%async_computation.7 | async-start | bytes 5242880 | tf_op jit(solution)/shard_map/all_gather | solution.py:1741
  118.9 48.8 %copy-start = (bf16[256,2048]{1,0:T(8,128)(2,1)S(1)}, bf16[256,2048]{1,0:T(8,128)(2,1)}, u32[]{:S(2)}) copy-start(bf16[256,2048]{1,0:T(8,128)(2,1)} %param.12) | copy-start | bytes 3145732
  167.7 1.8 copy-start.1
  169.5 1.6 copy-start.5
  171.0 79.2 %all-gather.6.cloned.1.call-start = ((), (), s32[]{:S(2)}) async-start(), calls=%async_computation.6 | async-start | bytes 5242880 | tf_op jit(solution)/shard_map/all_gather | solution.py:1741
  172.4 332.7 %reduce-scatter.7.cloned.1.call-start = ((), (), s32[]{:S(2)}) async-start(), calls=%async_computation.8 | async-start | bytes 5242880 | tf_op jit(solution)/shard_map/reduce_scatter | solution.py:1745
  426.0 256.1 %reduce-scatter.9.cloned.1.call-start = ((), (), s32[]{:S(2)}) async-start(), calls=%async_computation.9 | async-start | bytes 5242880 | tf_op jit(solution)/shard_map/reduce_scatter | solution.py:1745
  505.1 2.6 copy-start.6
  508.6 1.3 copy-start.2
  547.4 134.7 %reduce-scatter.11.cloned.1.call-start = ((), (), s32[]{:S(2)}) async-start(), calls=%async_computation.10 | async-start | bytes 5242880 | tf_op jit(solution)/shard_map/reduce_scatter | solution.py:1745
  621.2 60.9 %copy-start.10 = (f32[2048]{0:T(1024)S(1)}, f32[2048]{0:T(1024)}, u32[]{:S(2)}) copy-start(f32[2048]{0:T(1024)} %copy-done.9) | copy-start | bytes 24580
  682.1 1.9 copy-start.3
  684.0 4.3 copy-start.8
  684.0 5.1 copy-start.12
  684.0 5.8 copy-start.11
  684.0 6.5 copy-start.7
  690.4 2.3 copy-start.4
Sparse Core Ops, SparseCore 0:
  12.1 37.1 all-gather.3
  118.4 43.6 reduce-scatter.4
  171.2 33.2 all-gather.7
  206.4 34.4 all-gather.5
  426.1 45.8 reduce-scatter.6
  547.5 42.7 reduce-scatter.8
  618.4 42.7 reduce-scatter.10

commit v7 on v6

--- a/solution.py
+++ b/solution.py
@@ -632,9 +632,13 @@
     made = take(len(extra.made) if extra else 0)
     left_bufs, right_bufs, firsts, owns, helds, totals = (take(num) for _ in range(6))
     send_sems, recv_sems, left_sems, right_sems, store_sems = take(5)
-    beside = extra.builder(count, given, made, refs[taken:], right_bufs) if extra else None
+    beside = (
+        extra.builder(count, given, made, refs[taken:], (left_bufs, right_bufs)) if extra else None
+    )
     entry_place = ring_place(lax.axis_index("dp"), count)
     last = count - 1
+
+    ready = [buf.shape[0] == 8 for buf in right_bufs]
 
     def load_right(item):
         _, half, start, _ = items[item]
@@ -646,14 +650,19 @@
         block = items[item][0]
         member = member_at(place, side, step + 1, count)
         slot = step % 2
+        here = pl.ds(pl.multiple_of(member * block, block), block)
+        if ready[item]:
+            half = items[item][1]
+            source = lefts[item].at[here, side * half : (side + 1) * half]
+        else:
+            source = lefts[item].at[:, here]
         return pltpu.make_async_copy(
-            lefts[item].at[:, pl.ds(pl.multiple_of(member * block, block), block)],
-            left_bufs[item].at[side, slot],
-            left_sems.at[side, slot, item],
+            source, left_bufs[item].at[side, slot], left_sems.at[side, slot, item]
         )
 
     for item in range(num):
-        load_right(item).start()
+        if not ready[item]:
+            load_right(item).start()
         for side in range(2):
             load_left(0, side, item, entry_place).start()
     if beside:
@@ -684,7 +693,8 @@
         ]
 
     for item in range(num):
-        load_right(item).wait()
+        if not ready[item]:
+            load_right(item).wait()
 
     def turn(step, carry):
         @pl.when(step < last)
@@ -696,6 +706,13 @@
             half = items[item][1]
             for side in range(2):
                 load_left(step, side, item, place).wait()
+
+            if ready[item]:
+                for side in range(2):
+                    owns[item][side] = (
+                        left_bufs[item][side, step % 2].astype(F32).reshape(owns[item].shape[1:])
+                    )
+                continue
 
             def own_sum(side, inner):
                 cols = pl.ds(pl.multiple_of(side * half, half), half)
@@ -754,10 +771,11 @@
 
 
 def ring_scatter_dots(jobs, parts, count, collective_id, extra=None):
-    rows = jobs[0].left.shape[0]
+    rows = next((j.left.shape[0] for j in jobs if j.right is not None), 0)
     items, shapes, bases, aliases = [], [], [], {}
     for job in jobs:
-        block, half = job.left.shape[1] // count, job.cols // 2
+        width = job.left.shape[1] if job.right is not None else job.left.shape[0]
+        block, half = width // count, job.cols // 2
         if job.pieces:
             places, column = ([], []), 0
             for cols in job.pieces:
@@ -789,8 +807,9 @@
         return [pltpu.VMEM(depth + (parts, b // parts, h), dtype) for b, h, _, _ in items]
 
     slots = num * parts
-    flops = sum(2 * rows * j.left.shape[1] * j.cols for j in jobs)
-    nbytes = sum(2 * j.left.shape[1] * j.cols for j in jobs)
+    flops = sum(2 * rows * count * i[0] * 2 * i[1] for i in items)
+    nbytes = sum(2 * count * i[0] * 2 * i[1] for i in items)
+    dots = [j.right is not None for j in jobs]
     given, given_specs, made, made_specs, spare = extra[1:] if extra else ([], [], [], [], [])
     return pl.pallas_call(
         functools.partial(
@@ -800,8 +819,14 @@
         in_specs=[ANY] * (2 * num + len(bases)) + given_specs,
         out_specs=[ANY] * len(shapes) + made_specs,
         input_output_aliases=aliases,
-        scratch_shapes=[pltpu.VMEM((2, 2, rows, i[0]), BF16) for i in items]
-        + [pltpu.VMEM((rows, 2 * i[1]), BF16) for i in items]
+        scratch_shapes=[
+            pltpu.VMEM((2, 2) + ((rows, i[0]) if dot_job else (i[0], i[1])), BF16)
+            for i, dot_job in zip(items, dots)
+        ]
+        + [
+            pltpu.VMEM((rows, 2 * i[1]) if dot_job else (8, 128), BF16)
+            for i, dot_job in zip(items, dots)
+        ]
         + buffers((2,), BF16)
         + buffers((2,), F32)
         + buffers((2, count - 1), BF16)
@@ -821,11 +846,16 @@
             flops=flops, bytes_accessed=20 * nbytes, transcendentals=0
         ),
         name=f"ring_scatter_{collective_id}",
-    )(*[j.left for j in jobs], *[j.right for j in jobs], *bases, *given)
+    )(
+        *[j.left for j in jobs],
+        *[j.left if j.right is None else j.right for j in jobs],
+        *bases,
+        *given,
+    )
 
 
 class ShareWork:
-    def __init__(self, count, given, made, spare, rights):
+    def __init__(self, count, given, made, spare, bufs):
         self.given, self.out = given, made[0]
         self.pair, self.first, self.sums, self.second, self.sems = spare
         self.count, self.group = count, self.second.shape[0] + 1
@@ -894,8 +924,70 @@
         self.out[:, :share] = picked
 
 
+class ProductWork:
+    def __init__(self, count, given, made, spare, bufs):
+        self.right, self.out = given[0], made[0]
+        self.right_buf, self.stage, self.load_sem, self.sems = spare
+        self.left, self.count = bufs[0][0], count
+        self.place = ring_place(lax.axis_index("dp"), count)
+        self.start = self.right.shape[1] - self.right_buf.shape[1]
+
+    def peers(self):
+        return ()
+
+    def load(self):
+        return pltpu.make_async_copy(
+            self.right.at[:, self.start :], self.right_buf, self.load_sem
+        )
+
+    def begin(self):
+        self.load().start()
+
+    def store(self, step):
+        block = self.stage.shape[1]
+        member = member_at(self.place, 0, step + 1, self.count)
+        return pltpu.make_async_copy(
+            self.stage.at[step % 2],
+            self.out.at[pl.ds(pl.multiple_of(member * block, block), block), :],
+            self.sems.at[step % 2],
+        )
+
+    def compute(self, step):
+        @pl.when(step == 0)
+        def _():
+            self.load().wait()
+
+        @pl.when(step >= 2)
+        def _():
+            self.store(step - 2).wait()
+
+        self.stage[step % 2] = tn_dot(self.left[0, step % 2], self.right_buf[...]).astype(BF16)
+        self.store(step).start()
+
+    def finish(self):
+        for step in (self.count - 2, self.count - 1):
+            self.store(step).wait()
+
+
+def product_work(right, start, count, width):
+    rows, cols = right.shape[0], right.shape[1] - start
+    return Extra(
+        ProductWork,
+        [right],
+        [ANY],
+        [jax.ShapeDtypeStruct((width, cols), BF16)],
+        [ANY],
+        [
+            pltpu.VMEM((rows, cols), BF16),
+            pltpu.VMEM((2, width // count, cols), BF16),
+            pltpu.SemaphoreType.DMA,
+            pltpu.SemaphoreType.DMA((2,)),
+        ],
+    )
+
+
 class GatherWork:
-    def __init__(self, count, given, made, spare, rights):
+    def __init__(self, count, given, made, spare, bufs):
         self.own, self.out = given[0], made[0]
         self.stage, self.sems, self.local = spare
         self.col = lax.axis_index("tensor")
@@ -996,13 +1088,13 @@
 
 
 class NormWork:
-    def __init__(self, count, given, made, spare, rights):
+    def __init__(self, count, given, made, spare, bufs):
         self.grads, self.gates = given[:2], tuple(given[2:4])
         self.up, self.down = given[4:]
         self.outs = made
         self.grad_bufs, self.row_bufs, self.down_bufs, self.stage = spare[0], *spare[1:4]
         self.grad_sems, self.row_sems, self.down_sems, self.out_sems = spare[4:]
-        self.act = rights[0]
+        self.act = bufs[1][0]
         self.count = count
         self.block = self.row_bufs.shape[2]
 
@@ -1367,7 +1459,7 @@
 
 
 class HeadWork:
-    def __init__(self, count, given, made, spare, rights):
+    def __init__(self, count, given, made, spare, bufs):
         self.length, self.gain, self.sources = given[0], given[1], given[2:]
         self.grads_out, self.token_out, self.gain_out = made
         num = len(self.sources)
@@ -1528,7 +1620,7 @@
     specs = [pl.BlockSpec(memory_space=pltpu.SMEM), vmem] + [ANY] * len(sources)
     return ring_scatter_dots(
         [job],
-        2,
+        4,
         count,
         cid,
         Extra(HeadWork, [lengths, gain] + sources, specs, made, [ANY, ANY, vmem], spare),
@@ -1914,9 +2006,16 @@
         norm_part = (nt_dot(grad_gate_pre, gate_all) + nt_dot(grad_up_pre, up_all)).astype(BF16)
         (grad_down,) = ring_weight_grads([(grad_branch, activated)], 2, count, 4)
     grad_norm_two = scatter_rows(norm_part).astype(F32)
-    (grad_gate,) = ring_weight_grads(
-        [(after(rows_mlp, norm_part), grad_gate_pre)], 2, count, 5
-    )
+    middle = 3 * grad_up_pre.shape[1] // 8
+    if fused:
+        grad_gate, up_part = ring_scatter_dots(
+            [Job(after(rows_mlp, norm_part), grad_gate_pre, 0, grad_gate_pre.shape[1])],
+            2, count, 5, product_work(grad_up_pre, middle, count, rows_mlp.shape[1]),
+        )
+    else:
+        (grad_gate,) = ring_weight_grads(
+            [(after(rows_mlp, norm_part), grad_gate_pre)], 2, count, 5
+        )
     scaled_two = grad_norm_two * gain_mlp
     gain_two_part = jnp.sum(grad_norm_two * hidden * inv_second, axis=0)
     grad_hidden = (
@@ -1926,15 +2025,14 @@
     )
     grad_hidden = after(grad_hidden, grad_gate)
     if fused:
-        middle = 3 * grad_up_pre.shape[1] // 8
         hidden_cols = grad_up_pre.shape[1]
         grad_up, grad_attn = ring_scatter_dots(
             [Job(rows_mlp, grad_up_pre, 0, middle, hidden_cols)],
-            2, count, 6, gather_work(grad_hidden.astype(BF16)),
+            4, count, 6, gather_work(grad_hidden.astype(BF16)),
         )
         mlp_branch = scatter_rows(after(mlp_part, grad_attn))
         grad_up, grad_qkv, token_part, gain_one = heads_ring(
-            Job(rows_mlp, grad_up_pre, middle, hidden_cols - middle, grad_up, middle),
+            Job(up_part, None, 0, hidden_cols - middle, grad_up, middle),
             lengths,
             gain_attn[None, :],
             grad_attn,

time: 702 us -> 696 us (level)
  transfers between devices with their start and end apart: 7 -> 7, of which waited for: 0 -> 0; matrix products, arithmetic and copies ran while one was open for 1% -> 1% of each run, Pallas kernels for 56% -> 55%
where the time goes in v7:
time: 696 us
  Pallas kernels  644 us (93%)
  other arithmetic  22 us (3%)
  between operations  15 us (2%)
  local copies, waits for them, and re-layouts  14 us (2%)
    pallas_call x5, Pallas kernels, ring_scatter_dots(): pl.pallas_call(functools.partial(scatter_dot_kernel, count, items, len(sh...  320 us
    pallas_call x3, Pallas kernels, ring_gather(): pl.pallas_call(functools.partial(gather_kernel, count, items), out_shape=...  182 us
    pallas_call x1, Pallas kernels, mlp_ring(): pl.pallas_call(functools.partial(mlp_kernel, count), out_shape=[wide] * 3...  93.5 us
    pallas_call x1, Pallas kernels, attend_ring(): pl.pallas_call(functools.partial(attend_ring_kernel, count), out_shape=[l...  47.8 us
  transfers between devices with their start and end apart: 7, of which 0 were waited for; matrix products, arithmetic and copies ran while one was open for 1% of the time, Pallas kernels for 55%

profile of v7, /device:TPU:0, one launch (start us, length us, event | category | flops | bytes accessed | tf_op | source)
XLA Modules:
  0.0 695.6 jit_solution(16399909182331849133)
XLA Ops:
  7.2 0.0 all-gather.4.cloned.1.call-start
  7.2 1.5 fusion.7
  8.7 0.7 convert_element_type.47
  9.4 2.5 fusion.9
  11.9 0.0 all-gather.4.cloned.1.call-update
  12.0 0.0 reduce-scatter.5.cloned.1.call-start
  12.7 55.7 %ring_gather_0.1 = (bf16[2048,512]{1,0:T(8,128)(2,1)}, bf16[2048,128]{1,0:T(8,128)(2,1)}, bf16[2048,128]{1,0:T(8,128)(2,1)}, bf16[512,2048]{1,0:T(8,128)(2,1)}) custom-call(bf16[256,512]{1,0:T(8,128)(2,1)} %refs_0_.1, bf16[256,128]{1,0:T(8,128)(2,1)} %refs_1_.2, bf16[256,128]{1,0:T(8,128)(2,1)} %refs_2_.1, bf16[512,256]{1,0:T(8,128)(2,1)} %refs_3_.2), custom_call_target="tpu_custom_call" | custom-call | bytes 91750400 | tf_op jit(solution)/shard_map/ring_gather_0/pallas_call | solution.py:449
  68.4 0.1 pad_maximum_fusion
  68.5 0.2 multiply_cosine_fusion
  68.7 0.9 multiply_add_fusion
  69.6 0.0 copy-done.9
  69.6 0.8 bitcast_multiply_fusion.refs_8_.refs_11_
  70.4 47.8 %attend_ring.1 = (bf16[2048,768]{1,0:T(8,128)(2,1)}, bf16[1024,512]{1,0:T(8,128)(2,1)}, bf16[1024,128]{1,0:T(8,128)(2,1)}, bf16[1024,128]{1,0:T(8,128)(2,1)}, bf...) custom-call(s32[1]{0:T(128)} %copy.32.refs_0_.refs_3_, bf16[256,2048]{1,0:T(8,128)(2,1)} %refs_0_.2, ...), custom_call_target="tpu_custom_call" | custom-call | flops 25769803776 | bytes 62914560 | tf_op jit(solution)/shard_map/attend_ring/pallas_call | solution.py:1781
  118.3 0.0 copy-start.13
  118.3 0.0 reduce-scatter.5.cloned.1.call-update
  118.3 0.0 all-gather.8.cloned.1.call-start
  118.3 0.6 copy-done.13
  119.0 48.7 %ring_gather_1.1.refs_2_.refs_5_ = bf16[2048,1280]{1,0:T(8,128)(2,1)} custom-call(bf16[256,2048]{1,0:T(8,128)(2,1)} %refs_0_.2), custom_call_target="tpu_custom_call" | custom-call | bytes 146800640 | tf_op jit(solution)/shard_map/ring_gather_1/pallas_call | solution.py:449
  167.7 0.0 reduce-scatter.5.cloned.1.call-done
  167.7 1.7 multiply_reduce_fusion
  169.5 0.0 copy-done.1
  169.5 0.0 copy-start.5
  169.5 1.5 multiply_convert_fusion
  171.0 0.0 all-gather.8.cloned.1.call-update
  171.0 0.0 all-gather.6.cloned.1.call-start
  171.1 0.0 copy-done.5
  171.1 1.2 fusion.13
  172.3 0.0 all-gather.6.cloned.1.call-update
  172.3 0.2 reduce-scatter.7.cloned.1.call-start
  172.6 77.5 %ring_gather_2.1.refs_3_.refs_6_ = bf16[2048,2048]{1,0:T(8,128)(2,1)} custom-call(bf16[256,2048]{1,0:T(8,128)(2,1)} %refs_0_.3), custom_call_target="tpu_custom_call" | custom-call | bytes 146800640 | tf_op jit(solution)/shard_map/ring_gather_2/pallas_call | solution.py:449
  250.1 0.0 all-gather.8.cloned.1.call-done.refs_0_
  250.2 0.0 all-gather.6.cloned.1.call-done.refs_5_.refs_0_
  250.2 93.5 %mlp_ring.1 = (bf16[1024,2048]{1,0:T(8,128)(2,1)}, bf16[1024,2048]{1,0:T(8,128)(2,1)}, bf16[1024,2048]{1,0:T(8,128)(2,1)}, bf16[2048,2048]{1,0:T(8,128)(2,1)}) custom-call(bf16[1024,2048]{1,0:T(8,128)(2,1)} %all-gather.8.cloned.1.call-done.refs_0_, bf16[2048,768]{1,0:T(8,128)(2,1)} %get-tuple-element.62.refs_1_.refs_4_, ...), custom_call_target="tpu_custom_call" | custom-call | flops 25769803776 | bytes 167772160 | tf_op jit(solution)/shard_map/mlp_ring/pallas_call | solution.py:1426
  343.7 82.6 %ring_scatter_4.1 = (f32[256,2048]{1,0:T(8,128)}, bf16[1024,2048]{1,0:T(8,128)(2,1)}, bf16[1024,2048]{1,0:T(8,128)(2,1)}) custom-call(bf16[1024,2048]{1,0:T(8,128)(2,1)} %all-gather.6.cloned.1.call-done.refs_5_.refs_0_, bf16[1024,2048]{1,0:T(8,128)(2,1)} %get-tuple-element.65.refs_1_, bf16[1024,2048]{1,0:T(8,128)(2,1)} %get-tuple-element.66.refs_2_.refs_1_, ...), custom_call_target="tpu_custom_call" | custom-call | flops 8589934592 | bytes 167772160 | tf_op jit(solution)/shard_map/ring_scatter_4/pallas_call | solution.py:814
  426.3 0.0 reduce-scatter.7.cloned.1.call-update
  426.3 0.0 reduce-scatter.9.cloned.1.call-start
  426.3 80.0 %ring_scatter_5.1 = (f32[256,2048]{1,0:T(8,128)}, bf16[2048,1280]{1,0:T(8,128)(2,1)}) custom-call(bf16[1024,2048]{1,0:T(8,128)(2,1)} %all-gather.8.cloned.1.call-done.refs_0_, bf16[1024,2048]{1,0:T(8,128)(2,1)} %get-tuple-element.66.refs_2_.refs_1_, bf16[1024,2048]{1,0:T(8,128)(2,1)} %get-tuple-element.67.refs_3_.refs_2_.refs_1_), custom_call_target="tpu_custom_call" | custom-call | flops 8589934592 | bytes 167772160 | tf_op jit(solution)/shard_map/ring_scatter_5/pallas_call | solution.py:814
  506.4 0.0 reduce-scatter.7.cloned.1.call-done
  506.4 2.6 fusion.6
  509.0 0.9 fusion.3
  509.9 0.0 copy-start.2
  509.9 1.3 copy-done.2
  511.2 1.1 convert_element_type.56.refs_2_
  512.3 36.0 %ring_scatter_6.1 = (f32[256,2048]{1,0:T(8,128)}, bf16[1024,2048]{1,0:T(8,128)(2,1)}) custom-call(bf16[1024,2048]{1,0:T(8,128)(2,1)} %all-gather.8.cloned.1.call-done.refs_0_, bf16[1024,2048]{1,0:T(8,128)(2,1)} %get-tuple-element.67.refs_3_.refs_2_.refs_1_, bf16[256,2048]{1,0:T(8,128)(2,1)} %convert_element_type.56.refs_2_), custom_call_target="tpu_custom_call" | custom-call | flops 3221225472 | bytes 62914560 | tf_op jit(solution)/shard_map/ring_scatter_6/pallas_call | solution.py:814
  548.3 0.0 reduce-scatter.9.cloned.1.call-update
  548.3 0.3 reduce-scatter.11.cloned.1.call-start
  548.6 64.2 %ring_scatter_10.1 = (f32[256,2048]{1,0:T(8,128)}, bf16[1024,768]{1,0:T(8,128)(2,1)}, bf16[1024,2048]{1,0:T(8,128)(2,1)}, f32[8,2048]{1,0:T(8,128)}) custom-call(bf16[2048,1280]{1,0:T(8,128)(2,1)} %get-tuple-element.76.refs_0_.refs_1_, bf16[2048,1280]{1,0:T(8,128)(2,1)} %get-tuple-element.76.refs_0_.refs_1_, ...), custom_call_target="tpu_custom_call", output_to_operand_aliasing={{0}: (2, {})} | custom-call | bytes 104857600 | tf_op jit(solution)/shard_map/ring_scatter_10/pallas_call | solution.py:814
  612.8 0.0 reduce-scatter.11.cloned.1.call-update
  612.8 2.9 copy.25
  615.7 57.7 %ring_scatter_7.1 = (f32[256,512]{1,0:T(8,128)}, f32[256,128]{1,0:T(8,128)}, f32[256,128]{1,0:T(8,128)}, f32[256,512]{1,0:T(8,128)}, f32[8,128]{1,0:T(8,128)}) custom-call(bf16[1024,2048]{1,0:T(8,128)(2,1)} %all-gather.4.cloned.1.call-done.refs_2_.refs_17_.refs_0_, bf16[1024,2048]{1,0:T(8,128)(2,1)} %get-tuple-element.74.refs_5_.refs_1_, ...), custom_call_target="tpu_custom_call" | custom-call | flops 5368709120 | bytes 104857600 | tf_op jit(solution)/shard_map/ring_scatter_7/pallas_call | solution.py:814
  673.4 2.0 copy.24
  675.5 1.3 slice_bitcast_fusion
  676.7 0.0 copy-start.3
  676.8 1.8 fusion.12
  678.6 0.1 copy-done.3
  678.7 4.3 fusion.11
  683.0 0.8 copy.33
  683.8 0.7 copy.34
  684.5 0.0 copy-done.11
  684.5 0.7 copy.35
  685.1 0.0 copy-done.7
  685.1 1.3 copy.36
  686.4 1.0 copy-done.4
  687.5 1.3 copy.37
  (27 shorter events, 0.1 us)
Async XLA Ops:
  7.2 63.3 %all-gather.4.cloned.1.call-start = ((), (), s32[]{:S(2)}) async-start(), calls=%async_computation.4 | async-start | bytes 5242880 | tf_op jit(solution)/shard_map/all_gather | solution.py:1833
  9.4 60.2 %copy-start.9 = (f32[2048]{0:T(1024)}, f32[2048]{0:T(1024)S(1)}, u32[]{:S(2)}) copy-start(f32[2048]{0:T(1024)S(1)} %convert_element_type.47) | copy-start | bytes 24580
  12.0 155.7 %reduce-scatter.5.cloned.1.call-start = ((), (), s32[]{:S(2)}) async-start(), calls=%async_computation.5 | async-start | bytes 5242880 | tf_op jit(solution)/shard_map/reduce_scatter | solution.py:1837
  118.3 0.7 copy-start.13
  118.3 131.8 %all-gather.8.cloned.1.call-start = ((), (), s32[]{:S(2)}) async-start(), calls=%async_computation.7 | async-start | bytes 5242880 | tf_op jit(solution)/shard_map/all_gather | solution.py:1833
  119.0 48.8 %copy-start = (bf16[256,2048]{1,0:T(8,128)(2,1)S(1)}, bf16[256,2048]{1,0:T(8,128)(2,1)}, u32[]{:S(2)}) copy-start(bf16[256,2048]{1,0:T(8,128)(2,1)} %param.12) | copy-start | bytes 3145732
  167.7 1.8 copy-start.1
  169.5 1.6 copy-start.5
  171.0 79.1 %all-gather.6.cloned.1.call-start = ((), (), s32[]{:S(2)}) async-start(), calls=%async_computation.6 | async-start | bytes 5242880 | tf_op jit(solution)/shard_map/all_gather | solution.py:1833
  172.3 334.0 %reduce-scatter.7.cloned.1.call-start = ((), (), s32[]{:S(2)}) async-start(), calls=%async_computation.8 | async-start | bytes 5242880 | tf_op jit(solution)/shard_map/reduce_scatter | solution.py:1837
  426.3 250.4 %reduce-scatter.9.cloned.1.call-start = ((), (), s32[]{:S(2)}) async-start(), calls=%async_computation.9 | async-start | bytes 5242880 | tf_op jit(solution)/shard_map/reduce_scatter | solution.py:1837
  506.4 2.6 copy-start.6
  509.9 1.3 copy-start.2
  548.3 128.4 %reduce-scatter.11.cloned.1.call-start = ((), (), s32[]{:S(2)}) async-start(), calls=%async_computation.10 | async-start | bytes 5242880 | tf_op jit(solution)/shard_map/reduce_scatter | solution.py:1837
  615.7 61.0 %copy-start.10 = (f32[2048]{0:T(1024)S(1)}, f32[2048]{0:T(1024)}, u32[]{:S(2)}) copy-start(f32[2048]{0:T(1024)} %copy-done.9) | copy-start | bytes 24580
  676.7 1.9 copy-start.3
  678.7 4.3 copy-start.8
  678.7 5.1 copy-start.12
  678.7 5.8 copy-start.11
  678.7 6.5 copy-start.7
  685.1 2.3 copy-start.4
Sparse Core Ops, SparseCore 0:
  12.1 37.1 all-gather.3
  118.4 43.6 reduce-scatter.4
  171.2 33.2 all-gather.7
  206.5 34.4 all-gather.5
  426.4 44.7 reduce-scatter.6
  548.4 42.7 reduce-scatter.8
  612.9 42.5 reduce-scatter.10

commit v8 on v7

--- a/solution.py
+++ b/solution.py
@@ -226,14 +226,14 @@
 
 def attend_back_tiles(
     pair_index, q_ref, k_ref, v_ref, g_ref, cos_ref, sin_ref, stats_ref, inner_ref, bias_ref,
-    gq_ref, acc_k, acc_v,
+    gq_ref, acc_k, acc_v, blocks,
 ):
     kv = pair_index // 2
     square = (QB, QB)
     causal = lax.broadcasted_iota(jnp.int32, square, 0) <= lax.broadcasted_iota(
         jnp.int32, square, 1
     )
-    for block in range(LEN // QB):
+    for block in blocks:
         rows = slice(block * QB, (block + 1) * QB)
         pair = q_ref[rows, :].astype(F32) * HD**-0.5
         grad_pair = g_ref[rows, :].astype(F32)
@@ -1556,35 +1556,41 @@
             lax.fori_loop(0, LEN // 256, products, 0)
             self.inner[...] = jnp.transpose(stats[...])
 
-        @pl.when(step == pairs + 1)
-        def _():
-            for which in range(9, len(self.sources)):
-                self.load(which).wait()
+        def tiles(pair, blocks):
+            here = pl.ds(pl.multiple_of(pair * 128, 128), 128)
+            attend_back_tiles(
+                pair, queries.at[:, here], keys, values, self.heads.at[:, here], cosine, sine,
+                self.stats, self.inner, self.bias, self.grads.at[:, here], self.acc_k,
+                self.acc_v, blocks,
+            )
 
         @pl.when((step >= 1) & (step <= pairs))
         def _():
-            here = pl.ds(pl.multiple_of((step - 1) * 128, 128), 128)
-            attend_back_tiles(
-                step - 1, queries.at[:, here], keys, values, self.heads.at[:, here], cosine,
-                sine, self.stats, self.inner, self.bias, self.grads.at[:, here],
-                self.acc_k, self.acc_v,
-            )
-
-        @pl.when(step == pairs)
+            tiles(step - 1, (2, 3))
+
+        @pl.when((step > pairs) & (step <= pairs + 2))
+        def _():
+            def early(index, carry):
+                tiles(pairs // 2 * (step - pairs - 1) + index, (0, 1))
+                return carry
+
+            lax.fori_loop(0, pairs // 2, early, 0)
+
+        @pl.when(step == pairs + 3)
         def _():
             self.grads[:, inner : inner + 128] = rope_back(
                 self.acc_k[...], cosine[...], sine[...]
             )
             self.grads[:, inner + 128 :] = self.acc_v[...].astype(BF16)
             self.store_grads().start()
-
-        @pl.when((step > pairs) & (step <= pairs + 2))
-        def _():
+            for which in range(9, len(self.sources)):
+                self.load(which).wait()
+
             def band(index, carry):
-                self.tokens(2 * (step - pairs - 1) + index)
+                self.tokens(index)
                 return carry
 
-            lax.fori_loop(0, 2, band, 0)
+            lax.fori_loop(0, 4, band, 0)
 
     def finish(self):
         self.gain_out[0:1, :] = self.gain_out[0:1, :] / self.gain[...]

time: 696 us -> 699 us (level)
  no operation moved by 1% of the time
where the time goes in v8:
time: 699 us; the launch traced here: 698 us
  Pallas kernels  646 us (92%)
  other arithmetic  22 us (3%)
  between operations  15 us (2%)
  local copies, waits for them, and re-layouts  14 us (2%)
    pallas_call x5, Pallas kernels, ring_scatter_dots(): pl.pallas_call(functools.partial(scatter_dot_kernel, count, items, len(sh...  323 us
    pallas_call x3, Pallas kernels, ring_gather(): pl.pallas_call(functools.partial(gather_kernel, count, items), out_shape=...  182 us
    pallas_call x1, Pallas kernels, mlp_ring(): pl.pallas_call(functools.partial(mlp_kernel, count), out_shape=[wide] * 3...  93.5 us
    pallas_call x1, Pallas kernels, attend_ring(): pl.pallas_call(functools.partial(attend_ring_kernel, count), out_shape=[l...  47.8 us
  transfers between devices with their start and end apart: 7, of which 0 were waited for; matrix products, arithmetic and copies ran while one was open for 1% of the time, Pallas kernels for 55%

profile of v8, /device:TPU:0, one launch (start us, length us, event | category | flops | bytes accessed | tf_op | source)
XLA Modules:
  0.0 698.4 jit_solution(7544740771410255351)
XLA Ops:
  7.2 0.0 all-gather.4.cloned.1.call-start
  7.2 1.5 fusion.7
  8.7 0.7 convert_element_type.47
  9.4 2.5 fusion.9
  11.9 0.0 all-gather.4.cloned.1.call-update
  12.0 0.0 reduce-scatter.5.cloned.1.call-start
  12.7 55.7 %ring_gather_0.1 = (bf16[2048,512]{1,0:T(8,128)(2,1)}, bf16[2048,128]{1,0:T(8,128)(2,1)}, bf16[2048,128]{1,0:T(8,128)(2,1)}, bf16[512,2048]{1,0:T(8,128)(2,1)}) custom-call(bf16[256,512]{1,0:T(8,128)(2,1)} %refs_0_.1, bf16[256,128]{1,0:T(8,128)(2,1)} %refs_1_.2, bf16[256,128]{1,0:T(8,128)(2,1)} %refs_2_.1, bf16[512,256]{1,0:T(8,128)(2,1)} %refs_3_.2), custom_call_target="tpu_custom_call" | custom-call | bytes 91750400 | tf_op jit(solution)/shard_map/ring_gather_0/pallas_call | solution.py:449
  68.4 0.1 pad_maximum_fusion
  68.5 0.2 multiply_cosine_fusion
  68.7 0.9 multiply_add_fusion
  69.6 0.0 copy-done.9
  69.6 0.8 bitcast_multiply_fusion.refs_8_.refs_11_
  70.4 47.8 %attend_ring.1 = (bf16[2048,768]{1,0:T(8,128)(2,1)}, bf16[1024,512]{1,0:T(8,128)(2,1)}, bf16[1024,128]{1,0:T(8,128)(2,1)}, bf16[1024,128]{1,0:T(8,128)(2,1)}, bf...) custom-call(s32[1]{0:T(128)} %copy.32.refs_0_.refs_3_, bf16[256,2048]{1,0:T(8,128)(2,1)} %refs_0_.2, ...), custom_call_target="tpu_custom_call" | custom-call | flops 25769803776 | bytes 62914560 | tf_op jit(solution)/shard_map/attend_ring/pallas_call | solution.py:1787
  118.3 0.0 copy-start.13
  118.3 0.0 reduce-scatter.5.cloned.1.call-update
  118.3 0.0 all-gather.8.cloned.1.call-start
  118.3 0.6 copy-done.13
  119.0 48.7 %ring_gather_1.1.refs_2_.refs_5_ = bf16[2048,1280]{1,0:T(8,128)(2,1)} custom-call(bf16[256,2048]{1,0:T(8,128)(2,1)} %refs_0_.2), custom_call_target="tpu_custom_call" | custom-call | bytes 146800640 | tf_op jit(solution)/shard_map/ring_gather_1/pallas_call | solution.py:449
  167.7 0.0 reduce-scatter.5.cloned.1.call-done
  167.7 0.0 copy-done
  167.7 0.0 copy-start.1
  167.7 1.7 multiply_reduce_fusion
  169.5 0.0 copy-done.1
  169.5 0.0 copy-start.5
  169.5 1.5 multiply_convert_fusion
  171.0 0.0 all-gather.8.cloned.1.call-update
  171.0 0.0 all-gather.6.cloned.1.call-start
  171.1 0.0 copy-done.5
  171.1 1.2 fusion.13
  172.3 0.0 all-gather.6.cloned.1.call-update
  172.3 0.2 reduce-scatter.7.cloned.1.call-start
  172.6 77.5 %ring_gather_2.1.refs_3_.refs_6_ = bf16[2048,2048]{1,0:T(8,128)(2,1)} custom-call(bf16[256,2048]{1,0:T(8,128)(2,1)} %refs_0_.3), custom_call_target="tpu_custom_call" | custom-call | bytes 146800640 | tf_op jit(solution)/shard_map/ring_gather_2/pallas_call | solution.py:449
  250.1 0.0 all-gather.8.cloned.1.call-done.refs_0_
  250.2 0.0 all-gather.6.cloned.1.call-done.refs_5_.refs_0_
  250.2 93.5 %mlp_ring.1 = (bf16[1024,2048]{1,0:T(8,128)(2,1)}, bf16[1024,2048]{1,0:T(8,128)(2,1)}, bf16[1024,2048]{1,0:T(8,128)(2,1)}, bf16[2048,2048]{1,0:T(8,128)(2,1)}) custom-call(bf16[1024,2048]{1,0:T(8,128)(2,1)} %all-gather.8.cloned.1.call-done.refs_0_, bf16[2048,768]{1,0:T(8,128)(2,1)} %get-tuple-element.62.refs_1_.refs_4_, ...), custom_call_target="tpu_custom_call" | custom-call | flops 25769803776 | bytes 167772160 | tf_op jit(solution)/shard_map/mlp_ring/pallas_call | solution.py:1426
  343.7 82.6 %ring_scatter_4.1 = (f32[256,2048]{1,0:T(8,128)}, bf16[1024,2048]{1,0:T(8,128)(2,1)}, bf16[1024,2048]{1,0:T(8,128)(2,1)}) custom-call(bf16[1024,2048]{1,0:T(8,128)(2,1)} %all-gather.6.cloned.1.call-done.refs_5_.refs_0_, bf16[1024,2048]{1,0:T(8,128)(2,1)} %get-tuple-element.65.refs_1_, bf16[1024,2048]{1,0:T(8,128)(2,1)} %get-tuple-element.66.refs_2_.refs_1_, ...), custom_call_target="tpu_custom_call" | custom-call | flops 8589934592 | bytes 167772160 | tf_op jit(solution)/shard_map/ring_scatter_4/pallas_call | solution.py:814
  426.3 0.0 reduce-scatter.7.cloned.1.call-update
  426.3 0.0 reduce-scatter.9.cloned.1.call-start
  426.3 80.0 %ring_scatter_5.1 = (f32[256,2048]{1,0:T(8,128)}, bf16[2048,1280]{1,0:T(8,128)(2,1)}) custom-call(bf16[1024,2048]{1,0:T(8,128)(2,1)} %all-gather.8.cloned.1.call-done.refs_0_, bf16[1024,2048]{1,0:T(8,128)(2,1)} %get-tuple-element.66.refs_2_.refs_1_, bf16[1024,2048]{1,0:T(8,128)(2,1)} %get-tuple-element.67.refs_3_.refs_2_.refs_1_), custom_call_target="tpu_custom_call" | custom-call | flops 8589934592 | bytes 167772160 | tf_op jit(solution)/shard_map/ring_scatter_5/pallas_call | solution.py:814
  506.4 0.0 reduce-scatter.7.cloned.1.call-done
  506.4 2.6 fusion.6
  509.0 0.9 fusion.3
  509.9 0.0 copy-start.2
  509.9 1.3 copy-done.2
  511.2 1.1 convert_element_type.56.refs_2_
  512.3 36.0 %ring_scatter_6.1 = (f32[256,2048]{1,0:T(8,128)}, bf16[1024,2048]{1,0:T(8,128)(2,1)}) custom-call(bf16[1024,2048]{1,0:T(8,128)(2,1)} %all-gather.8.cloned.1.call-done.refs_0_, bf16[1024,2048]{1,0:T(8,128)(2,1)} %get-tuple-element.67.refs_3_.refs_2_.refs_1_, bf16[256,2048]{1,0:T(8,128)(2,1)} %convert_element_type.56.refs_2_), custom_call_target="tpu_custom_call" | custom-call | flops 3221225472 | bytes 62914560 | tf_op jit(solution)/shard_map/ring_scatter_6/pallas_call | solution.py:814
  548.3 0.0 reduce-scatter.9.cloned.1.call-update
  548.3 0.3 reduce-scatter.11.cloned.1.call-start
  548.6 66.9 %ring_scatter_10.1 = (f32[256,2048]{1,0:T(8,128)}, bf16[1024,768]{1,0:T(8,128)(2,1)}, bf16[1024,2048]{1,0:T(8,128)(2,1)}, f32[8,2048]{1,0:T(8,128)}) custom-call(bf16[2048,1280]{1,0:T(8,128)(2,1)} %get-tuple-element.76.refs_0_.refs_1_, bf16[2048,1280]{1,0:T(8,128)(2,1)} %get-tuple-element.76.refs_0_.refs_1_, ...), custom_call_target="tpu_custom_call", output_to_operand_aliasing={{0}: (2, {})} | custom-call | bytes 104857600 | tf_op jit(solution)/shard_map/ring_scatter_10/pallas_call | solution.py:814
  615.5 0.0 reduce-scatter.11.cloned.1.call-update
  615.6 2.9 copy.25
  618.4 57.8 %ring_scatter_7.1 = (f32[256,512]{1,0:T(8,128)}, f32[256,128]{1,0:T(8,128)}, f32[256,128]{1,0:T(8,128)}, f32[256,512]{1,0:T(8,128)}, f32[8,128]{1,0:T(8,128)}) custom-call(bf16[1024,2048]{1,0:T(8,128)(2,1)} %all-gather.4.cloned.1.call-done.refs_2_.refs_17_.refs_0_, bf16[1024,2048]{1,0:T(8,128)(2,1)} %get-tuple-element.74.refs_5_.refs_1_, ...), custom_call_target="tpu_custom_call" | custom-call | flops 5368709120 | bytes 104857600 | tf_op jit(solution)/shard_map/ring_scatter_7/pallas_call | solution.py:814
  676.2 2.0 copy.24
  678.3 1.3 slice_bitcast_fusion
  679.5 0.0 copy-start.3
  679.5 1.8 fusion.12
  681.4 0.1 copy-done.3
  681.5 4.3 fusion.11
  685.8 0.8 copy.33
  686.6 0.7 copy.34
  687.3 0.7 copy.35
  687.9 1.3 copy.36
  689.2 1.0 copy-done.4
  690.3 1.3 copy.37
  (27 shorter events, 0.1 us)
Async XLA Ops:
  7.2 63.3 %all-gather.4.cloned.1.call-start = ((), (), s32[]{:S(2)}) async-start(), calls=%async_computation.4 | async-start | bytes 5242880 | tf_op jit(solution)/shard_map/all_gather | solution.py:1839
  9.4 60.2 %copy-start.9 = (f32[2048]{0:T(1024)}, f32[2048]{0:T(1024)S(1)}, u32[]{:S(2)}) copy-start(f32[2048]{0:T(1024)S(1)} %convert_element_type.47) | copy-start | bytes 24580
  12.0 155.7 %reduce-scatter.5.cloned.1.call-start = ((), (), s32[]{:S(2)}) async-start(), calls=%async_computation.5 | async-start | bytes 5242880 | tf_op jit(solution)/shard_map/reduce_scatter | solution.py:1843
  118.3 0.7 copy-start.13
  118.3 131.8 %all-gather.8.cloned.1.call-start = ((), (), s32[]{:S(2)}) async-start(), calls=%async_computation.7 | async-start | bytes 5242880 | tf_op jit(solution)/shard_map/all_gather | solution.py:1839
  119.0 48.8 %copy-start = (bf16[256,2048]{1,0:T(8,128)(2,1)S(1)}, bf16[256,2048]{1,0:T(8,128)(2,1)}, u32[]{:S(2)}) copy-start(bf16[256,2048]{1,0:T(8,128)(2,1)} %param.12) | copy-start | bytes 3145732
  167.7 1.8 copy-start.1
  169.5 1.6 copy-start.5
  171.0 79.1 %all-gather.6.cloned.1.call-start = ((), (), s32[]{:S(2)}) async-start(), calls=%async_computation.6 | async-start | bytes 5242880 | tf_op jit(solution)/shard_map/all_gather | solution.py:1839
  172.3 334.0 %reduce-scatter.7.cloned.1.call-start = ((), (), s32[]{:S(2)}) async-start(), calls=%async_computation.8 | async-start | bytes 5242880 | tf_op jit(solution)/shard_map/reduce_scatter | solution.py:1843
  426.3 253.2 %reduce-scatter.9.cloned.1.call-start = ((), (), s32[]{:S(2)}) async-start(), calls=%async_computation.9 | async-start | bytes 5242880 | tf_op jit(solution)/shard_map/reduce_scatter | solution.py:1843
  506.4 2.6 copy-start.6
  509.9 1.3 copy-start.2
  548.3 131.2 %reduce-scatter.11.cloned.1.call-start = ((), (), s32[]{:S(2)}) async-start(), calls=%async_computation.10 | async-start | bytes 5242880 | tf_op jit(solution)/shard_map/reduce_scatter | solution.py:1843
  618.4 61.1 %copy-start.10 = (f32[2048]{0:T(1024)S(1)}, f32[2048]{0:T(1024)}, u32[]{:S(2)}) copy-start(f32[2048]{0:T(1024)} %copy-done.9) | copy-start | bytes 24580
  679.5 1.9 copy-start.3
  681.4 4.3 copy-start.8
  681.5 5.1 copy-start.12
  681.5 5.8 copy-start.11
  681.5 6.5 copy-start.7
  687.9 2.3 copy-start.4
Sparse Core Ops, SparseCore 0:
  12.1 37.1 all-gather.3
  118.4 43.6 reduce-scatter.4
  171.2 33.2 all-gather.7
  206.5 34.4 all-gather.5
  426.4 44.7 reduce-scatter.6
  548.4 42.7 reduce-scatter.8
  615.7 42.0 reduce-scatter.10

commit v9 on v7

--- a/solution.py
+++ b/solution.py
@@ -2006,7 +2006,7 @@
         norm_part = (nt_dot(grad_gate_pre, gate_all) + nt_dot(grad_up_pre, up_all)).astype(BF16)
         (grad_down,) = ring_weight_grads([(grad_branch, activated)], 2, count, 4)
     grad_norm_two = scatter_rows(norm_part).astype(F32)
-    middle = 3 * grad_up_pre.shape[1] // 8
+    middle = 2 * grad_up_pre.shape[1] // 8
     if fused:
         grad_gate, up_part = ring_scatter_dots(
             [Job(after(rows_mlp, norm_part), grad_gate_pre, 0, grad_gate_pre.shape[1])],

time: 696 us -> 700 us (level)
  transfers between devices with their start and end apart: 7 -> 7, of which waited for: 0 -> 0; matrix products, arithmetic and copies ran while one was open for 1% -> 1% of each run, Pallas kernels for 55% -> 56%
where the time goes in v9:
time: 700 us; the launch traced here: 699 us
  Pallas kernels  647 us (92%)
  other arithmetic  22 us (3%)
  between operations  15 us (2%)
  local copies, waits for them, and re-layouts  14 us (2%)
    pallas_call x5, Pallas kernels, ring_scatter_dots(): pl.pallas_call(functools.partial(scatter_dot_kernel, count, items, len(sh...  324 us
    pallas_call x3, Pallas kernels, ring_gather(): pl.pallas_call(functools.partial(gather_kernel, count, items), out_shape=...  182 us
    pallas_call x1, Pallas kernels, mlp_ring(): pl.pallas_call(functools.partial(mlp_kernel, count), out_shape=[wide] * 3...  93.5 us
    pallas_call x1, Pallas kernels, attend_ring(): pl.pallas_call(functools.partial(attend_ring_kernel, count), out_shape=[l...  47.8 us
  transfers between devices with their start and end apart: 7, of which 0 were waited for; matrix products, arithmetic and copies ran while one was open for 1% of the time, Pallas kernels for 56%

profile of v9, /device:TPU:0, one launch (start us, length us, event | category | flops | bytes accessed | tf_op | source)
XLA Modules:
  0.0 699.2 jit_solution(16763809015002730348)
XLA Ops:
  7.2 0.0 all-gather.4.cloned.1.call-start
  7.2 1.5 fusion.7
  8.7 0.7 convert_element_type.47
  9.4 2.5 fusion.9
  11.9 0.0 all-gather.4.cloned.1.call-update
  12.0 0.0 reduce-scatter.5.cloned.1.call-start
  12.7 55.7 %ring_gather_0.1 = (bf16[2048,512]{1,0:T(8,128)(2,1)}, bf16[2048,128]{1,0:T(8,128)(2,1)}, bf16[2048,128]{1,0:T(8,128)(2,1)}, bf16[512,2048]{1,0:T(8,128)(2,1)}) custom-call(bf16[256,512]{1,0:T(8,128)(2,1)} %refs_0_.1, bf16[256,128]{1,0:T(8,128)(2,1)} %refs_1_.2, bf16[256,128]{1,0:T(8,128)(2,1)} %refs_2_.1, bf16[512,256]{1,0:T(8,128)(2,1)} %refs_3_.2), custom_call_target="tpu_custom_call" | custom-call | bytes 91750400 | tf_op jit(solution)/shard_map/ring_gather_0/pallas_call | solution.py:449
  68.4 0.1 pad_maximum_fusion
  68.5 0.2 multiply_cosine_fusion
  68.7 0.9 multiply_add_fusion
  69.6 0.0 copy-done.9
  69.6 0.8 bitcast_multiply_fusion.refs_8_.refs_11_
  70.4 47.8 %attend_ring.1 = (bf16[2048,768]{1,0:T(8,128)(2,1)}, bf16[1024,512]{1,0:T(8,128)(2,1)}, bf16[1024,128]{1,0:T(8,128)(2,1)}, bf16[1024,128]{1,0:T(8,128)(2,1)}, bf...) custom-call(s32[1]{0:T(128)} %copy.32.refs_0_.refs_3_, bf16[256,2048]{1,0:T(8,128)(2,1)} %refs_0_.2, ...), custom_call_target="tpu_custom_call" | custom-call | flops 25769803776 | bytes 62914560 | tf_op jit(solution)/shard_map/attend_ring/pallas_call | solution.py:1781
  118.3 0.0 copy-start.13
  118.3 0.0 reduce-scatter.5.cloned.1.call-update
  118.3 0.0 all-gather.8.cloned.1.call-start
  118.3 0.6 copy-done.13
  119.0 48.7 %ring_gather_1.1.refs_2_.refs_5_ = bf16[2048,1280]{1,0:T(8,128)(2,1)} custom-call(bf16[256,2048]{1,0:T(8,128)(2,1)} %refs_0_.2), custom_call_target="tpu_custom_call" | custom-call | bytes 146800640 | tf_op jit(solution)/shard_map/ring_gather_1/pallas_call | solution.py:449
  167.7 0.0 reduce-scatter.5.cloned.1.call-done
  167.7 0.0 copy-done
  167.7 0.0 copy-start.1
  167.7 1.7 multiply_reduce_fusion
  169.5 0.0 copy-done.1
  169.5 0.0 copy-start.5
  169.5 1.5 multiply_convert_fusion
  171.0 0.0 all-gather.8.cloned.1.call-update
  171.0 0.0 all-gather.6.cloned.1.call-start
  171.1 1.2 fusion.13
  172.3 0.0 all-gather.6.cloned.1.call-update
  172.3 0.2 reduce-scatter.7.cloned.1.call-start
  172.6 77.5 %ring_gather_2.1.refs_3_.refs_6_ = bf16[2048,2048]{1,0:T(8,128)(2,1)} custom-call(bf16[256,2048]{1,0:T(8,128)(2,1)} %refs_0_.3), custom_call_target="tpu_custom_call" | custom-call | bytes 146800640 | tf_op jit(solution)/shard_map/ring_gather_2/pallas_call | solution.py:449
  250.1 0.0 all-gather.8.cloned.1.call-done.refs_0_
  250.2 0.0 all-gather.6.cloned.1.call-done.refs_5_.refs_0_
  250.2 93.5 %mlp_ring.1 = (bf16[1024,2048]{1,0:T(8,128)(2,1)}, bf16[1024,2048]{1,0:T(8,128)(2,1)}, bf16[1024,2048]{1,0:T(8,128)(2,1)}, bf16[2048,2048]{1,0:T(8,128)(2,1)}) custom-call(bf16[1024,2048]{1,0:T(8,128)(2,1)} %all-gather.8.cloned.1.call-done.refs_0_, bf16[2048,768]{1,0:T(8,128)(2,1)} %get-tuple-element.62.refs_1_.refs_4_, ...), custom_call_target="tpu_custom_call" | custom-call | flops 25769803776 | bytes 167772160 | tf_op jit(solution)/shard_map/mlp_ring/pallas_call | solution.py:1426
  343.7 82.6 %ring_scatter_4.1 = (f32[256,2048]{1,0:T(8,128)}, bf16[1024,2048]{1,0:T(8,128)(2,1)}, bf16[1024,2048]{1,0:T(8,128)(2,1)}) custom-call(bf16[1024,2048]{1,0:T(8,128)(2,1)} %all-gather.6.cloned.1.call-done.refs_5_.refs_0_, bf16[1024,2048]{1,0:T(8,128)(2,1)} %get-tuple-element.65.refs_1_, bf16[1024,2048]{1,0:T(8,128)(2,1)} %get-tuple-element.66.refs_2_.refs_1_, ...), custom_call_target="tpu_custom_call" | custom-call | flops 8589934592 | bytes 167772160 | tf_op jit(solution)/shard_map/ring_scatter_4/pallas_call | solution.py:814
  426.3 0.0 reduce-scatter.7.cloned.1.call-update
  426.3 0.0 reduce-scatter.9.cloned.1.call-start
  426.3 80.1 %ring_scatter_5.1 = (f32[256,2048]{1,0:T(8,128)}, bf16[2048,1536]{1,0:T(8,128)(2,1)}) custom-call(bf16[1024,2048]{1,0:T(8,128)(2,1)} %all-gather.8.cloned.1.call-done.refs_0_, bf16[1024,2048]{1,0:T(8,128)(2,1)} %get-tuple-element.66.refs_2_.refs_1_, bf16[1024,2048]{1,0:T(8,128)(2,1)} %get-tuple-element.67.refs_3_.refs_2_.refs_1_), custom_call_target="tpu_custom_call" | custom-call | flops 8589934592 | bytes 167772160 | tf_op jit(solution)/shard_map/ring_scatter_5/pallas_call | solution.py:814
  506.5 0.0 reduce-scatter.7.cloned.1.call-done
  506.5 0.0 copy-start.6
  506.5 2.6 fusion.6
  509.2 0.9 fusion.3
  510.0 0.0 copy-start.2
  510.0 1.3 copy-done.2
  511.4 1.1 convert_element_type.56.refs_2_
  512.5 29.9 %ring_scatter_6.1 = (f32[256,2048]{1,0:T(8,128)}, bf16[1024,2048]{1,0:T(8,128)(2,1)}) custom-call(bf16[1024,2048]{1,0:T(8,128)(2,1)} %all-gather.8.cloned.1.call-done.refs_0_, bf16[1024,2048]{1,0:T(8,128)(2,1)} %get-tuple-element.67.refs_3_.refs_2_.refs_1_, bf16[256,2048]{1,0:T(8,128)(2,1)} %convert_element_type.56.refs_2_), custom_call_target="tpu_custom_call" | custom-call | flops 2147483648 | bytes 41943040 | tf_op jit(solution)/shard_map/ring_scatter_6/pallas_call | solution.py:814
  542.4 0.0 reduce-scatter.9.cloned.1.call-update
  542.4 0.3 reduce-scatter.11.cloned.1.call-start
  542.7 70.6 %ring_scatter_10.1 = (f32[256,2048]{1,0:T(8,128)}, bf16[1024,768]{1,0:T(8,128)(2,1)}, bf16[1024,2048]{1,0:T(8,128)(2,1)}, f32[8,2048]{1,0:T(8,128)}) custom-call(bf16[2048,1536]{1,0:T(8,128)(2,1)} %get-tuple-element.76.refs_0_.refs_1_, bf16[2048,1536]{1,0:T(8,128)(2,1)} %get-tuple-element.76.refs_0_.refs_1_, ...), custom_call_target="tpu_custom_call", output_to_operand_aliasing={{0}: (2, {})} | custom-call | bytes 125829120 | tf_op jit(solution)/shard_map/ring_scatter_10/pallas_call | solution.py:814
  613.4 0.0 reduce-scatter.11.cloned.1.call-update
  613.4 2.9 copy.25
  616.3 60.7 %ring_scatter_7.1 = (f32[256,512]{1,0:T(8,128)}, f32[256,128]{1,0:T(8,128)}, f32[256,128]{1,0:T(8,128)}, f32[256,512]{1,0:T(8,128)}, f32[8,128]{1,0:T(8,128)}) custom-call(bf16[1024,2048]{1,0:T(8,128)(2,1)} %all-gather.4.cloned.1.call-done.refs_2_.refs_17_.refs_0_, bf16[1024,2048]{1,0:T(8,128)(2,1)} %get-tuple-element.74.refs_5_.refs_1_, ...), custom_call_target="tpu_custom_call" | custom-call | flops 5368709120 | bytes 104857600 | tf_op jit(solution)/shard_map/ring_scatter_7/pallas_call | solution.py:814
  677.0 2.0 copy.24
  679.0 1.3 slice_bitcast_fusion
  680.3 0.0 copy-start.3
  680.3 1.8 fusion.12
  682.1 0.1 copy-done.3
  682.2 4.3 fusion.11
  686.5 0.8 copy.33
  687.3 0.7 copy.34
  688.0 0.7 copy.35
  688.7 1.3 copy.36
  690.0 1.0 copy-done.4
  691.0 1.3 copy.37
  (27 shorter events, 0.1 us)
Async XLA Ops:
  7.2 63.3 %all-gather.4.cloned.1.call-start = ((), (), s32[]{:S(2)}) async-start(), calls=%async_computation.4 | async-start | bytes 5242880 | tf_op jit(solution)/shard_map/all_gather | solution.py:1833
  9.4 60.2 %copy-start.9 = (f32[2048]{0:T(1024)}, f32[2048]{0:T(1024)S(1)}, u32[]{:S(2)}) copy-start(f32[2048]{0:T(1024)S(1)} %convert_element_type.47) | copy-start | bytes 24580
  12.0 155.7 %reduce-scatter.5.cloned.1.call-start = ((), (), s32[]{:S(2)}) async-start(), calls=%async_computation.5 | async-start | bytes 5242880 | tf_op jit(solution)/shard_map/reduce_scatter | solution.py:1837
  118.3 0.7 copy-start.13
  118.3 131.8 %all-gather.8.cloned.1.call-start = ((), (), s32[]{:S(2)}) async-start(), calls=%async_computation.7 | async-start | bytes 5242880 | tf_op jit(solution)/shard_map/all_gather | solution.py:1833
  119.0 48.8 %copy-start = (bf16[256,2048]{1,0:T(8,128)(2,1)S(1)}, bf16[256,2048]{1,0:T(8,128)(2,1)}, u32[]{:S(2)}) copy-start(bf16[256,2048]{1,0:T(8,128)(2,1)} %param.12) | copy-start | bytes 3145732
  167.7 1.8 copy-start.1
  169.5 1.6 copy-start.5
  171.0 79.1 %all-gather.6.cloned.1.call-start = ((), (), s32[]{:S(2)}) async-start(), calls=%async_computation.6 | async-start | bytes 5242880 | tf_op jit(solution)/shard_map/all_gather | solution.py:1833
  172.3 334.2 %reduce-scatter.7.cloned.1.call-start = ((), (), s32[]{:S(2)}) async-start(), calls=%async_computation.8 | async-start | bytes 5242880 | tf_op jit(solution)/shard_map/reduce_scatter | solution.py:1837
  426.3 254.0 %reduce-scatter.9.cloned.1.call-start = ((), (), s32[]{:S(2)}) async-start(), calls=%async_computation.9 | async-start | bytes 5242880 | tf_op jit(solution)/shard_map/reduce_scatter | solution.py:1837
  506.5 2.6 copy-start.6
  510.0 1.3 copy-start.2
  542.4 137.8 %reduce-scatter.11.cloned.1.call-start = ((), (), s32[]{:S(2)}) async-start(), calls=%async_computation.10 | async-start | bytes 5242880 | tf_op jit(solution)/shard_map/reduce_scatter | solution.py:1837
  616.3 64.0 %copy-start.10 = (f32[2048]{0:T(1024)S(1)}, f32[2048]{0:T(1024)}, u32[]{:S(2)}) copy-start(f32[2048]{0:T(1024)} %copy-done.9) | copy-start | bytes 24580
  680.3 1.9 copy-start.3
  682.2 4.3 copy-start.8
  682.2 5.1 copy-start.12
  682.2 5.8 copy-start.11
  682.2 6.5 copy-start.7
  688.7 2.3 copy-start.4
Sparse Core Ops, SparseCore 0:
  12.1 37.1 all-gather.3
  118.4 43.6 reduce-scatter.4
  171.2 33.2 all-gather.7
  206.5 34.4 all-gather.5
  426.4 44.6 reduce-scatter.6
  542.6 45.2 reduce-scatter.8
  613.5 46.4 reduce-scatter.10
